TPU v7x, 32 devices: a whole 2x2x4 slice. The times are simulated.
32 devices in a mesh: section: 2 (over core), dp: 4 (over z), tensor: 4 (over y, x).
Axes of the slice: x: 2, y: 2, z: 4, core: 2. Of those that a mesh axis runs over, the one named last changes fastest.
Arguments:
- tokens: bfloat16 [2, 3072, 1152], P(None, ('dp', 'tensor')), may hold values from -6 to 6
- cotangent: bfloat16 [2, 3072, 1152], P(None, ('dp', 'tensor')), may hold values from -6 to 6
- cond: bfloat16 [24, 1152], P('dp'), may hold values from -6 to 6
- patch_item: int32 [2, 3072], P(None, 'dp'), may hold values from -1 to 23, as said below
- patch_pos: int32 [2, 2, 3072], P(None, None, 'dp'), may hold values from 0 to 19, as said below
- w_qkv: bfloat16 [2, 3, 1152, 1152], P('section', None, None, 'tensor'), may hold values from -0.1875 to 0.1875
- w_out: bfloat16 [2, 1152, 1152], P('section', 'tensor'), may hold values from -0.75 to 0.75
- w_gate_up: bfloat16 [2, 2, 1152, 3072], P('section', None, None, 'tensor'), may hold values from -0.1875 to 0.1875
- w_down: bfloat16 [2, 3072, 1152], P('section', 'tensor'), may hold values from -0.109375 to 0.109375
- qk_gain: bfloat16 [2, 2, 72], P('section'), may hold values from 0.5 to 1.5
- ada_weight: bfloat16 [2, 1152, 6912], P('section', None, 'tensor'), may hold values from -0.1875 to 0.1875
- ada_bias: bfloat16 [2, 6912], P('section', 'tensor'), may hold values from -3 to 3
Outputs:
- layer_out: bfloat16 [2, 2, 3072, 1152], P('section', None, ('dp', 'tensor'))
- input_grads: float32 [2, 2, 3072, 1152], P('section', None, ('dp', 'tensor'))
- cond_grad: float32 [24, 1152], P('dp')
- g_qkv: float32 [2, 3, 1152, 1152], P('section', None, 'dp', 'tensor')
- g_out: float32 [2, 1152, 1152], P('section', 'tensor', 'dp')
- g_gate_up: float32 [2, 2, 1152, 3072], P('section', None, 'dp', 'tensor')
- g_down: float32 [2, 3072, 1152], P('section', 'tensor', 'dp')
- g_qk_gain: float32 [2, 2, 72], P('section')
- g_ada_weight: float32 [2, 1152, 6912], P('section', 'dp', 'tensor')
- g_ada_bias: float32 [2, 6912], P('section', ('tensor', 'dp'))
Inputs may be any that keep to these rules, and one draw needn't show every extreme that they name: `patch_item`: each micro-batch sequence of 768 slots holds 3 whole items one after another, each of 240 or 256 slots, then padding slots marked -1. The items of data shard d and micro-batch m are numbered (d * 2 + m) * 3 + j in order. patch_pos[0] and patch_pos[1] are a patch's row and column in its item's grid, in row-major order within the item; padding slots have 0 and 0.
All inputs are finite; a program needn't handle non-finite values.
Results may differ from a plain program's by a relative error of at most 0.015.
Values may be sent and summed in bfloat16 or wider, within the bound.
A program may use at most 256 MiB of HBM per device.

v0:
```python
import functools

import jax
import jax.numpy as jnp
from jax import lax
from jax.experimental import pallas as pl
from jax.experimental.pallas import tpu as pltpu
from jax.sharding import PartitionSpec as P

EPS = 1e-06
PRECISE = lax.Precision.HIGHEST
F32 = jnp.float32
BF = jnp.bfloat16
S, DP, T = "section", "dp", "tensor"
PAD = 128
TILE = 256


def nn(a, b):
    return jnp.dot(a, b, preferred_element_type=F32)


def nt(a, b):
    return lax.dot_general(a, b, (((1,), (1,)), ((), ())), preferred_element_type=F32)


def tn(a, b):
    return lax.dot_general(a, b, (((0,), (0,)), ((), ())), preferred_element_type=F32)


def two(dot, a, b):
    high = a.astype(BF)
    low = (a - high.astype(F32)).astype(BF)
    return dot(high, b) + dot(low, b)


def sds(shape, dtype):
    return jax.ShapeDtypeStruct(shape, dtype)


def vmem():
    return pl.BlockSpec(memory_space=pltpu.VMEM)


def anywhere():
    return pl.BlockSpec(memory_space=pl.ANY)


def ring(square):
    me = lax.axis_index(T)
    near = me + 1 - 2 * (me % 2)
    if square:
        return me, near, me + 2 - 4 * (me // 2), 3 - me
    return me, near, 3 - me, (me + 2) % 4


def greet(place):
    sem = pltpu.get_barrier_semaphore()
    for peer in (place[1], place[2]):
        pl.semaphore_signal(
            sem, inc=1, device_id={T: peer}, device_id_type=pl.DeviceIdType.MESH
        )
    pl.semaphore_wait(sem, 2)


def remote(src, dst, sems, index, peer):
    return pltpu.make_async_remote_copy(
        src_ref=src,
        dst_ref=dst,
        send_sem=sems[0].at[index],
        recv_sem=sems[1].at[index],
        device_id={T: peer},
        device_id_type=pl.DeviceIdType.MESH,
    )


def chunk_rows(chunk, rows):
    return pl.ds(pl.multiple_of(chunk * rows, rows), rows)


def gather(place, mine, whole, sems, base, use):
    me, a, b, d = place
    rows = mine.shape[0]
    half = rows // 2
    lo, hi = pl.ds(0, half), pl.ds(half, half)

    def part(chunk, upper):
        return pl.ds(pl.multiple_of(chunk * rows + upper * half, half), half)

    a0 = remote(mine.at[lo], whole.at[part(me, 0)], sems, base, a)
    b0 = remote(mine.at[hi], whole.at[part(me, 1)], sems, base + 1, b)
    a1 = remote(mine.at[hi], whole.at[part(me, 1)], sems, base + 2, a)
    b1 = remote(mine.at[lo], whole.at[part(me, 0)], sems, base + 3, b)
    for copy in (a0, b0, a1, b1):
        copy.start()
    whole[chunk_rows(me, rows), :] = mine[...]
    use(me)
    a0.wait_recv()
    b2 = remote(whole.at[part(a, 0)], whole.at[part(a, 0)], sems, base + 4, b)
    b2.start()
    b0.wait_recv()
    a2 = remote(whole.at[part(b, 1)], whole.at[part(b, 1)], sems, base + 5, a)
    a2.start()
    a1.wait_recv()
    use(a)
    b1.wait_recv()
    use(b)
    b2.wait_recv()
    a2.wait_recv()
    use(d)
    for copy in (a0, b0, a1, b1, a2, b2):
        copy.wait_send()


def scatter(place, term, bufs, sems, base):
    me, a, b, d = place
    out, into, keep, own = bufs
    half = keep.shape[1]
    lo, hi = pl.ds(0, half), pl.ds(half, half)
    out[0] = term(d).astype(BF)
    d0 = remote(out.at[0, lo], into.at[0, lo], sems, base, a)
    d1 = remote(out.at[0, hi], into.at[0, hi], sems, base + 1, b)
    d0.start()
    d1.start()
    total = term(a)
    out[1, lo] = total[:half].astype(BF)
    a0 = remote(out.at[1, lo], into.at[1, lo], sems, base + 2, a)
    a0.start()
    keep[0] = total[half:]
    total = term(b)
    out[2, hi] = total[half:].astype(BF)
    b0 = remote(out.at[2, hi], into.at[2, hi], sems, base + 3, b)
    b0.start()
    keep[1] = total[:half]
    own[...] = term(me)
    d1.wait_recv()
    out[1, hi] = (keep[0] + into[0, hi].astype(F32)).astype(BF)
    a1 = remote(out.at[1, hi], into.at[1, hi], sems, base + 4, a)
    a1.start()
    d0.wait_recv()
    out[2, lo] = (keep[1] + into[0, lo].astype(F32)).astype(BF)
    b1 = remote(out.at[2, lo], into.at[2, lo], sems, base + 5, b)
    b1.start()
    for copy in (a0, b0, a1, b1):
        copy.wait_recv()
    for copy in (d0, d1, a0, b0, a1, b1):
        copy.wait_send()


def scattered(bufs, rows):
    return bufs[3][rows] + bufs[1][1, rows].astype(F32) + bufs[1][2, rows].astype(F32)


def scatter_scratch(rows, width):
    return [
        pltpu.VMEM((3, rows, width), BF),
        pltpu.VMEM((3, rows, width), BF),
        pltpu.VMEM((2, rows // 2, width), F32),
        pltpu.VMEM((rows, width), F32),
    ]


def dma_sems(count):
    return [pltpu.SemaphoreType.DMA((count,)), pltpu.SemaphoreType.DMA((count,))]


def layer_weights(own, other, layer, dst, sem):
    mine = lax.axis_index(S) == layer

    @pl.when(mine)
    def _():
        pltpu.make_async_copy(own, dst, sem).start()

    @pl.when(jnp.logical_not(mine))
    def _():
        pltpu.make_async_copy(other, dst, sem).start()

    return pltpu.make_async_copy(own, dst, sem)


def over_blocks(rows, fn):
    step = rows // 4

    def body(i, carry):
        fn(pl.ds(pl.multiple_of(i * step, step), step))
        return carry

    lax.fori_loop(0, 4, body, 0)


def mod_rows(sel, mod, which, width):
    cols = pl.ds(which * width, width)
    total = sel[:, 0:1] * mod[0:1, cols]
    for item in (1, 2):
        total = total + sel[:, item : item + 1] * mod[item : item + 1, cols]
    return total


def item_sums(sel, values):
    high = values.astype(BF)
    low = (values - high.astype(F32)).astype(BF)
    sel_b = sel.astype(BF)
    return tn(sel_b, high) + tn(sel_b, low)


def normed(values):
    inverse = lax.rsqrt(jnp.mean(values * values, axis=-1, keepdims=True) + EPS)
    return values * inverse, inverse


def norm_back(incoming, normal, inverse):
    return inverse * (incoming - normal * jnp.mean(incoming * normal, axis=-1, keepdims=True))


def qkv_kernel(layer, square, x, sel, mod, w_own, w_other, whole, proj, h, w, ssem, rsem, wsem):
    place = ring(square)
    width = x.shape[1]
    load = layer_weights(w_own, w_other, layer, w, wsem)
    greet(place)

    def prepare(rows):
        normal, _ = normed(x[rows].astype(F32))
        shift = mod_rows(sel[rows], mod, 0, width)
        scale = mod_rows(sel[rows], mod, 1, width)
        h[rows] = (normal * (1.0 + scale) + shift).astype(BF)

    over_blocks(x.shape[0], prepare)
    waited = []

    def use(chunk):
        if not waited:
            load.wait()
            waited.append(1)
        rows = chunk_rows(chunk, x.shape[0])
        for k in range(3):
            proj[k, rows] = nn(whole[rows], w[k])

    gather(place, h, whole, (ssem, rsem), 0, use)


def mlp_kernel(layer, square, att, x, sel, mod, wo0, wo1, wg0, wg1, wd0, wd1, br1, x1, whole,
               gate, up, hidden, br2, y, h, wo, wg, wd, o1, i1, k1, s1, o2, i2, k2, s2,
               ssem, rsem, wsem):
    place = ring(square)
    rows_here, width = x.shape
    load_o = layer_weights(wo0, wo1, layer, wo, wsem.at[0])
    load_g = layer_weights(wg0, wg1, layer, wg, wsem.at[1])
    load_d = layer_weights(wd0, wd1, layer, wd, wsem.at[2])
    greet(place)
    sems = (ssem, rsem)
    load_o.wait()
    first = (o1, i1, k1, s1)
    scatter(place, lambda c: nn(att[chunk_rows(c, rows_here)], wo[...]), first, sems, 0)

    def between(rows):
        branch = scattered(first, rows)
        br1[rows] = branch
        mixed = x[rows].astype(F32) + mod_rows(sel[rows], mod, 2, width) * branch
        x1[rows] = mixed
        normal, _ = normed(mixed)
        shift = mod_rows(sel[rows], mod, 3, width)
        scale = mod_rows(sel[rows], mod, 4, width)
        h[rows] = (normal * (1.0 + scale) + shift).astype(BF)

    over_blocks(rows_here, between)
    load_g.wait()

    def use(chunk):
        rows = chunk_rows(chunk, rows_here)
        gate[rows] = nn(whole[rows], wg[0])
        up[rows] = nn(whole[rows], wg[1])
        g = gate[rows]
        hidden[rows] = (g * jax.nn.sigmoid(g) * up[rows]).astype(BF)

    gather(place, h, whole, sems, 6, use)
    load_d.wait()
    second = (o2, i2, k2, s2)
    scatter(place, lambda c: nn(hidden[chunk_rows(c, rows_here)], wd[...]), second, sems, 12)

    def finish(rows):
        branch = scattered(second, rows)
        br2[rows] = branch
        y[rows] = (x1[rows] + mod_rows(sel[rows], mod, 5, width) * branch).astype(BF)

    over_blocks(rows_here, finish)


def mlp_back_kernel(layer, square, dy, br2, br1, x1, sel, mod, gate_h, up_h, wo0, wo1, wg0, wg1,
                    wd0, wd1, whole2, dgate, dup, whole1, datt, dx1, dmod, h, h1, gate, up, wo,
                    wg, wd, o1, i1, k1, s1, ssem, rsem, wsem):
    place = ring(square)
    rows_here, width = dy.shape
    load_d = layer_weights(wd0, wd1, layer, wd, wsem.at[0])
    load_gate = pltpu.make_async_copy(gate_h, gate, wsem.at[1])
    load_gate.start()
    load_up = pltpu.make_async_copy(up_h, up, wsem.at[2])
    load_up.start()
    load_g = layer_weights(wg0, wg1, layer, wg, wsem.at[3])
    load_o = layer_weights(wo0, wo1, layer, wo, wsem.at[4])
    greet(place)
    sems = (ssem, rsem)
    dmod[...] = jnp.zeros_like(dmod)

    def prepare(rows):
        incoming = dy[rows].astype(F32)
        h[rows] = (incoming * mod_rows(sel[rows], mod, 5, width)).astype(BF)
        dmod[3] += item_sums(sel[rows], incoming * br2[rows])

    over_blocks(rows_here, prepare)
    waited = []

    def use(chunk):
        if not waited:
            load_d.wait()
            load_gate.wait()
            load_up.wait()
            waited.append(1)
        rows = chunk_rows(chunk, rows_here)
        d_hidden = nt(whole2[rows], wd[...])
        g = gate[rows]
        s = jax.nn.sigmoid(g)
        dgate[rows] = (d_hidden * up[rows] * s * (1.0 + g * (1.0 - s))).astype(BF)
        dup[rows] = (d_hidden * g * s).astype(BF)

    gather(place, h, whole2, sems, 0, use)
    load_g.wait()
    bufs = (o1, i1, k1, s1)

    def term(chunk):
        rows = chunk_rows(chunk, rows_here)
        return nt(dgate[rows], wg[0]) + nt(dup[rows], wg[1])

    scatter(place, term, bufs, sems, 6)

    def between(rows):
        d_h = scattered(bufs, rows)
        normal, inverse = normed(x1[rows])
        scale = mod_rows(sel[rows], mod, 4, width)
        d_mixed = dy[rows].astype(F32) + norm_back(d_h * (1.0 + scale), normal, inverse)
        dx1[rows] = d_mixed
        h1[rows] = (d_mixed * mod_rows(sel[rows], mod, 2, width)).astype(BF)
        dmod[1] += item_sums(sel[rows], d_h)
        dmod[2] += item_sums(sel[rows], d_h * normal)
        dmod[0] += item_sums(sel[rows], d_mixed * br1[rows])

    over_blocks(rows_here, between)
    load_o.wait()

    def use_out(chunk):
        rows = chunk_rows(chunk, rows_here)
        datt[rows] = nt(whole1[rows], wo[...]).astype(BF)

    gather(place, h1, whole1, sems, 12, use_out)


def qkv_back_kernel(layer, square, dproj, x, dx1, sel, mod, w_own, w_other, du, du_b, dmod, w,
                    o1, i1, k1, s1, ssem, rsem, wsem):
    place = ring(square)
    rows_here, width = x.shape
    load = layer_weights(w_own, w_other, layer, w, wsem)
    greet(place)
    dmod[...] = jnp.zeros_like(dmod)
    load.wait()
    bufs = (o1, i1, k1, s1)

    def term(chunk):
        rows = chunk_rows(chunk, rows_here)
        return nt(dproj[0, rows], w[0]) + nt(dproj[1, rows], w[1]) + nt(dproj[2, rows], w[2])

    scatter(place, term, bufs, (ssem, rsem), 0)

    def finish(rows):
        d_h = scattered(bufs, rows)
        normal, inverse = normed(x[rows].astype(F32))
        scale = mod_rows(sel[rows], mod, 1, width)
        total = dx1[rows] + norm_back(d_h * (1.0 + scale), normal, inverse)
        du[rows] = total
        du_b[rows] = total.astype(BF)
        dmod[0] += item_sums(sel[rows], d_h)
        dmod[1] += item_sums(sel[rows], d_h * normal)

    over_blocks(rows_here, finish)


def ring_call(kernel, ident, outs, scratch, args, spaces):
    return pl.pallas_call(
        kernel,
        out_shape=outs,
        in_specs=[vmem() if s else anywhere() for s in spaces],
        out_specs=[vmem()] * len(outs),
        scratch_shapes=scratch,
        compiler_params=pltpu.CompilerParams(
            collective_id=ident, has_side_effects=True, vmem_limit_bytes=60 * 2**20
        ),
    )(*args)


def attention_kernel(spans, proj, gain, cosine, sine, turn, spread, ones, q, k, v, att, padded):
    heads = spread.shape[1] // PAD
    head = proj.shape[2] // heads
    scale = head ** (-0.5)
    rows = proj.shape[1]

    def units(at):
        for which, dst in ((0, q), (1, k)):
            normal, _ = unit(proj[which, at], ones[...], head)
            gained = normal * gain[which]
            turned = gained * cosine[at] + two(nn, gained, turn[...]) * sine[at]
            dst[at] = nn(turned.astype(BF), spread[...]).astype(BF)
        v[at] = nn(proj[2, at].astype(BF), spread[...]).astype(BF)

    over_blocks(rows, units)
    for item in range(3):
        start = pl.multiple_of(spans[item], 16)
        length = spans[4 + item]
        at = pl.ds(start, TILE)
        valid = lax.broadcasted_iota(jnp.int32, (TILE, TILE), 1) < length
        for n in range(heads):
            lanes = slice(n * PAD, (n + 1) * PAD)
            padded[at, lanes] = softmax_rows(q[at, lanes], k[at, lanes], v[at, lanes], valid, scale)
    first = rows - 48
    start = spans[3]
    at = pl.ds(first, 48)
    valid = first + lax.broadcasted_iota(jnp.int32, (48, 48), 1) >= start
    live = first + lax.broadcasted_iota(jnp.int32, (48, PAD), 0) >= start
    for n in range(heads):
        lanes = slice(n * PAD, (n + 1) * PAD)
        new = softmax_rows(q[at, lanes], k[at, lanes], v[at, lanes], valid, scale)
        padded[at, lanes] = jnp.where(live, new, padded[at, lanes])
    att[...] = nt(padded[...], spread[...]).astype(BF)


def unit(proj, ones, head):
    inverse = lax.rsqrt(two(nn, proj * proj, ones) * (1.0 / head) + EPS)
    return proj * inverse, inverse


def softmax_rows(query, key, value, valid, scale):
    scores = jnp.where(valid, nt(query, key) * scale, -1e30)
    raised = jnp.exp(scores - jnp.max(scores, axis=1, keepdims=True))
    probs = raised / jnp.sum(raised, axis=1, keepdims=True)
    return nn(probs.astype(BF), value).astype(BF)


def back_tile(query, key, value, grad, keys, queries, scale):
    scores = jnp.where(keys, nt(key, query) * scale, -1e30)
    raised = jnp.exp(scores - jnp.max(scores, axis=0, keepdims=True))
    probs = jnp.where(queries, raised / jnp.sum(raised, axis=0, keepdims=True), 0.0)
    d_value = nn(probs.astype(BF), grad)
    d_probs = nt(value, grad)
    inner = jnp.sum(probs * d_probs, axis=0, keepdims=True)
    d_scores = (probs * (d_probs - inner)).astype(BF)
    return tn(d_scores, key) * scale, nn(d_scores, query) * scale, d_value


def attention_back_kernel(spans, q, k, v, datt, proj, gain, cosine, sine, turn, spread, ones,
                          dproj, dgain, grad, dq, dk, dv):
    heads = spread.shape[1] // PAD
    rows, packed = datt.shape
    head = packed // heads
    scale = head ** (-0.5)
    grad[...] = nn(datt[...], spread[...]).astype(BF)
    for item in range(3):
        start = pl.multiple_of(spans[item], 16)
        length = spans[4 + item]
        at = pl.ds(start, TILE)
        keys = lax.broadcasted_iota(jnp.int32, (TILE, TILE), 0) < length
        queries = lax.broadcasted_iota(jnp.int32, (TILE, TILE), 1) < length
        for n in range(heads):
            lanes = slice(n * PAD, (n + 1) * PAD)
            parts = back_tile(
                q[at, lanes], k[at, lanes], v[at, lanes], grad[at, lanes], keys, queries, scale
            )
            dq[at, lanes], dk[at, lanes], dv[at, lanes] = parts
    first = rows - 48
    start = spans[3]
    at = pl.ds(first, 48)
    keys = first + lax.broadcasted_iota(jnp.int32, (48, 48), 0) >= start
    queries = first + lax.broadcasted_iota(jnp.int32, (48, 48), 1) >= start
    live = first + lax.broadcasted_iota(jnp.int32, (48, PAD), 0) >= start
    for n in range(heads):
        lanes = slice(n * PAD, (n + 1) * PAD)
        parts = back_tile(
            q[at, lanes], k[at, lanes], v[at, lanes], grad[at, lanes], keys, queries, scale
        )
        for new, dst in zip(parts, (dq, dk, dv)):
            dst[at, lanes] = jnp.where(live, new, dst[at, lanes])
    dgain[...] = jnp.zeros_like(dgain)

    def finish(at):
        for which, src in ((0, dq), (1, dk)):
            flat = two(nt, src[at], spread[...])
            back = flat * cosine[at] - two(nn, flat, turn[...]) * sine[at]
            normal, inverse = unit(proj[which, at], ones[...], head)
            dgain[which] += jnp.sum(back * normal, axis=0, keepdims=True)
            gained = back * gain[which]
            mean = two(nn, gained * normal, ones[...]) * (1.0 / head)
            dproj[which, at] = (inverse * (gained - normal * mean)).astype(BF)
        dproj[2, at] = nt(dv[at].astype(BF), spread[...]).astype(BF)

    over_blocks(rows, finish)


def local_call(kernel, outs, scratch, spans, args):
    return pl.pallas_call(
        kernel,
        out_shape=outs,
        in_specs=[pl.BlockSpec(memory_space=pltpu.SMEM)] + [vmem()] * len(args),
        out_specs=[vmem()] * len(outs),
        scratch_shapes=scratch,
        compiler_params=pltpu.CompilerParams(vmem_limit_bytes=60 * 2**20),
    )(spans, *args)


def swap(array):
    return lax.ppermute(array, S, [(0, 1), (1, 0)])


def head_tables(positions, packed, head):
    quarter = head // 4
    frequency = 10000.0 ** (-jnp.arange(quarter, dtype=F32) / quarter)
    lane = jnp.arange(packed) % head
    per_lane = frequency[lane % quarter][None, :]
    place = jnp.where((lane // (2 * quarter) == 0)[None, :], positions[0][:, None], positions[1][:, None])
    angle = place.astype(F32) * per_lane
    rows = jnp.arange(packed)[:, None]
    cols = jnp.arange(packed)[None, :]
    early = (cols % (2 * quarter)) < quarter
    turn = jnp.where(early & (rows == cols + quarter), -1.0, 0.0)
    turn = turn + jnp.where(~early & (rows == cols - quarter), 1.0, 0.0)
    heads = packed // head
    wide = jnp.arange(heads * PAD)[None, :]
    spread = (rows // head == wide // PAD) & (rows % head == wide % PAD)
    ones = rows // head == cols // head
    return jnp.cos(angle), jnp.sin(angle), turn.astype(BF), spread.astype(BF), ones.astype(BF)


def halves(pack, section, dp):
    wide = pack.reshape(dp, 2, -1, pack.shape[1])
    mine = lax.dynamic_index_in_dim(wide, section, 1, keepdims=False)
    theirs = lax.dynamic_index_in_dim(wide, 1 - section, 1, keepdims=False)
    return mine, theirs


def reduced(pack, section, dp):
    mine, theirs = halves(pack.astype(BF), section, dp)
    total = (mine.astype(F32) + swap(theirs).astype(F32)).astype(BF)
    return lax.psum_scatter(total, DP, scatter_dimension=0, tiled=True)[0]


def own_layer(section, pair):
    first = section == 0
    keep = jnp.where(first, pair[0], pair[1])
    got = swap(jnp.where(first, pair[1], pair[0]))
    return jnp.where(first, jnp.concatenate([keep, got]), jnp.concatenate([got, keep])).astype(F32)


def per_device(square, dp, tokens, cotangent, cond, patch_item, patch_pos, w_qkv, w_out, w_gate_up,
               w_down, qk_gain, ada_weight, ada_bias):
    section = lax.axis_index(S)
    first = section == 0
    rows, width = tokens.shape[1:]
    seq = patch_item.shape[1]
    items = cond.shape[0]
    per_micro = items // 2
    head = qk_gain.shape[-1]
    packed = w_qkv.shape[-1]
    heads = packed // head
    hidden_here = w_down.shape[1]
    own = (w_qkv[0], w_out[0], w_gate_up[0], w_down[0])
    other = tuple(swap(w) for w in own)

    cond_wide = cond.astype(F32)
    cond_sigmoid = jax.nn.sigmoid(cond_wide)
    lifted = (cond_wide * cond_sigmoid).astype(BF)
    mod_part = nn(lifted, ada_weight[0]) + ada_bias[0].astype(F32)[None, :]
    mod_all = lax.all_gather(mod_part, (S, T)).reshape(2, 4, 2, per_micro, -1)
    mod_mine = lax.dynamic_index_in_dim(mod_all, section, 2, keepdims=False)
    mod_mine = jnp.swapaxes(mod_mine, 1, 2).reshape(2, per_micro, -1)
    mod_mine = jnp.pad(mod_mine, ((0, 0), (0, 8 - per_micro), (0, 0)))
    gains = lax.all_gather(qk_gain[0], S).astype(F32)
    gains = jnp.tile(gains, (1, 1, heads)).reshape(2, 2, 1, packed)
    lifted_all = lax.all_gather(lifted, DP, tiled=True)

    ids = lax.dynamic_index_in_dim(patch_item, section, 0, keepdims=False)
    ids = jnp.where(ids >= 0, ids - lax.axis_index(DP) * items - section * per_micro, -1)
    counts = jnp.sum((ids[None, :] == jnp.arange(3)[:, None]).astype(jnp.int32), axis=1)
    starts = jnp.concatenate([jnp.zeros((1,), jnp.int32), jnp.cumsum(counts)]).astype(jnp.int32)
    spans = jnp.concatenate([starts, counts, jnp.zeros((1,), jnp.int32)])
    local_ids = lax.dynamic_slice_in_dim(ids, lax.axis_index(T) * rows, rows)
    sel = (local_ids[:, None] == jnp.arange(8)[None, :]).astype(F32)
    positions = lax.dynamic_index_in_dim(patch_pos, section, 1, keepdims=False)
    tables = head_tables(positions, packed, head)

    x = lax.dynamic_index_in_dim(tokens, section, 0, keepdims=False)
    kept = []
    for layer in range(2):
        mod = mod_mine[layer]
        whole1, proj = ring_call(
            functools.partial(qkv_kernel, layer, square),
            layer,
            [sds((seq, width), BF), sds((3, seq, packed), F32)],
            [pltpu.VMEM((rows, width), BF), pltpu.VMEM((3, width, packed), BF)]
            + dma_sems(6)
            + [pltpu.SemaphoreType.DMA],
            (x, sel, mod, own[0], other[0]),
            (1, 1, 1, 0, 0),
        )
        q, k, v, att = local_call(
            attention_kernel,
            [sds((seq, heads * PAD), BF)] * 3 + [sds((seq, packed), BF)],
            [pltpu.VMEM((seq, heads * PAD), BF)],
            spans,
            (proj, gains[layer]) + tables,
        )
        br1, x1, whole2, gate, up, hidden, br2, y = ring_call(
            functools.partial(mlp_kernel, layer, square),
            2 + layer,
            [
                sds((rows, width), F32),
                sds((rows, width), F32),
                sds((seq, width), BF),
                sds((seq, hidden_here), F32),
                sds((seq, hidden_here), F32),
                sds((seq, hidden_here), BF),
                sds((rows, width), F32),
                sds((rows, width), BF),
            ],
            [
                pltpu.VMEM((rows, width), BF),
                pltpu.VMEM((packed, width), BF),
                pltpu.VMEM((2, width, hidden_here), BF),
                pltpu.VMEM((hidden_here, width), BF),
            ]
            + scatter_scratch(rows, width)
            + scatter_scratch(rows, width)
            + dma_sems(18)
            + [pltpu.SemaphoreType.DMA((3,))],
            (att, x, sel, mod, own[1], other[1], own[2], other[2], own[3], other[3]),
            (1, 1, 1, 1) + (0,) * 6,
        )
        kept.append((x, whole1, proj, q, k, v, att, br1, x1, whole2, gate, up, hidden, br2, y))
        x = y

    dy = lax.dynamic_index_in_dim(cotangent, section, 0, keepdims=False)
    packs = [None, None]
    d_mods = [None, None]
    d_gains = [None, None]
    d_inputs = [None, None]
    for layer in (1, 0):
        x, whole1, proj, q, k, v, att, br1, x1, whole2, gate, up, hidden, br2, y = kept[layer]
        mod = mod_mine[layer]
        rows2, dgate, dup, rows1, datt, dx1, dmod_a = ring_call(
            functools.partial(mlp_back_kernel, layer, square),
            4 + layer,
            [
                sds((seq, width), BF),
                sds((seq, hidden_here), BF),
                sds((seq, hidden_here), BF),
                sds((seq, width), BF),
                sds((seq, packed), BF),
                sds((rows, width), F32),
                sds((4, 8, width), F32),
            ],
            [
                pltpu.VMEM((rows, width), BF),
                pltpu.VMEM((rows, width), BF),
                pltpu.VMEM((seq, hidden_here), F32),
                pltpu.VMEM((seq, hidden_here), F32),
                pltpu.VMEM((packed, width), BF),
                pltpu.VMEM((2, width, hidden_here), BF),
                pltpu.VMEM((hidden_here, width), BF),
            ]
            + scatter_scratch(rows, width)
            + dma_sems(18)
            + [pltpu.SemaphoreType.DMA((5,))],
            (dy, br2, br1, x1, sel, mod, gate, up, own[1], other[1], own[2], other[2], own[3],
             other[3]),
            (1,) * 6 + (0,) * 8,
        )
        grads_mlp = jnp.concatenate(
            [tn(whole2, dgate).astype(BF), tn(whole2, dup).astype(BF), tn(rows2, hidden).astype(BF)],
            axis=1,
        )
        pack_mlp = reduced(grads_mlp, section, dp)
        dproj, dgain = local_call(
            attention_back_kernel,
            [sds((3, seq, packed), BF), sds((2, 1, packed), F32)],
            [pltpu.VMEM((seq, heads * PAD), BF)] + [pltpu.VMEM((seq, heads * PAD), F32)] * 3,
            spans,
            (q, k, v, datt, proj, gains[layer]) + tables,
        )
        du, du_b, dmod_b = ring_call(
            functools.partial(qkv_back_kernel, layer, square),
            6 + layer,
            [sds((rows, width), F32), sds((rows, width), BF), sds((2, 8, width), F32)],
            [pltpu.VMEM((3, width, packed), BF)]
            + scatter_scratch(rows, width)
            + dma_sems(6)
            + [pltpu.SemaphoreType.DMA],
            (dproj, x, dx1, sel, mod, own[0], other[0]),
            (1,) * 5 + (0,) * 2,
        )
        grads_att = jnp.concatenate(
            [tn(whole1, dproj[0]).astype(BF), tn(whole1, dproj[1]).astype(BF),
             tn(whole1, dproj[2]).astype(BF), tn(rows1, att).astype(BF)],
            axis=1,
        )
        pack_att = reduced(grads_att, section, dp)
        packs[layer] = (pack_mlp, pack_att)
        d_mods[layer] = jnp.concatenate([dmod_b, dmod_a])[:, :per_micro]
        d_gains[layer] = dgain
        d_inputs[layer] = du_b if layer else du
        dy = du_b

    d_mod = jnp.stack(d_mods).swapaxes(1, 2).reshape(2 * per_micro, -1)
    d_mod = lax.psum_scatter(d_mod, T, scatter_dimension=1, tiled=True).reshape(2, per_micro, -1)
    keep = jnp.where(first, d_mod[0], d_mod[1])
    got = swap(jnp.where(first, d_mod[1], d_mod[0]))
    mod_grads = jnp.where(first, jnp.concatenate([keep, got]), jnp.concatenate([got, keep]))
    mod_grads_all = lax.all_gather(mod_grads, DP, tiled=True)
    dp_index = lax.axis_index(DP)
    part = width // dp
    lifted_part = lax.dynamic_slice_in_dim(lifted_all, dp_index * part, part, 1).astype(F32)
    g_ada_w = lax.dot_general(lifted_part, mod_grads_all, (((0,), (0,)), ((), ())), precision=PRECISE)
    bias_part = ada_bias.shape[1] // dp
    g_ada_b = lax.dynamic_slice_in_dim(jnp.sum(mod_grads_all, axis=0), dp_index * bias_part, bias_part)
    d_lifted = lax.dot_general(
        mod_grads, ada_weight[0].astype(F32), (((1,), (1,)), ((), ())), precision=PRECISE
    )
    cond_grad = (
        lax.psum(d_lifted, (S, T)) * cond_sigmoid * (1.0 + cond_wide * (1.0 - cond_sigmoid))
    )
    gain_sums = jnp.stack(d_gains).reshape(2, 2, heads, head).sum(axis=2)
    gain_sums = lax.psum(gain_sums, (S, DP, T))
    gain_total = lax.dynamic_index_in_dim(gain_sums, section, 0)

    mlp = own_layer(section, (packs[0][0], packs[1][0]))
    attn = own_layer(section, (packs[0][1], packs[1][1]))
    f = hidden_here
    g_gate_up = jnp.stack([mlp[:, :f], mlp[:, f : 2 * f]])[None]
    g_down = mlp[:, 2 * f :].T[None]
    g_qkv = jnp.stack([attn[:, k * packed : (k + 1) * packed] for k in range(3)])[None]
    g_out = attn[:, 3 * packed :].T[None]

    outs = jnp.where(first, kept[0][-1], kept[1][-1])
    outs_got = swap(jnp.where(first, kept[1][-1], kept[0][-1]))
    layer_out = jnp.where(first, jnp.stack([outs, outs_got]), jnp.stack([outs_got, outs]))
    wide_mid = d_inputs[1].astype(F32)
    back_keep = jnp.where(first, d_inputs[0], wide_mid)
    back_got = swap(jnp.where(first, wide_mid, d_inputs[0]))
    in_grads = jnp.where(first, jnp.stack([back_keep, back_got]), jnp.stack([back_got, back_keep]))
    return (
        layer_out[None],
        in_grads[None],
        cond_grad,
        g_qkv,
        g_out,
        g_gate_up,
        g_down,
        gain_total,
        g_ada_w[None],
        g_ada_b[None],
    )


def solution(mesh):
    both = (DP, T)
    in_specs = (
        P(None, both, None),
        P(None, both, None),
        P(DP, None),
        P(None, DP),
        P(None, None, DP),
        P(S, None, None, T),
        P(S, T, None),
        P(S, None, None, T),
        P(S, T, None),
        P(S, None, None),
        P(S, None, T),
        P(S, T),
    )
    out_specs = (
        P(S, None, both, None),
        P(S, None, both, None),
        P(DP, None),
        P(S, None, DP, T),
        P(S, T, DP),
        P(S, None, DP, T),
        P(S, T, DP),
        P(S, None, None),
        P(S, DP, T),
        P(S, (T, DP)),
    )
    dp = mesh.shape[DP]
    return jax.shard_map(
        functools.partial(per_device, dp <= 4, dp),
        mesh=mesh,
        in_specs=in_specs,
        out_specs=out_specs,
        check_vma=False,
    )
```

profile of v0, /device:TPU:1, one launch (start us, length us, event | category | flops | bytes accessed | tf_op | source)
XLA Modules:
  0.0 701.0 jit_solution(13290660678167869879)
XLA Ops:
  13.1 25.4 %all-gather.1 = f32[8,6,1728]{2,1,0:T(8,128)S(1)} all-gather(f32[1,6,1728]{2,1,0:T(8,128)S(1)} %fusion.11), channel_id=2, replica_groups=mesh['section'=2,'dp'=4,'tensor'=4] {'section','tensor'}, dimensions={0}, use_global_device_ids=true | all-gather | bytes 373248 | tf_op jit(solution)/shard_map/all_gather | solution.py:577
  44.5 4.3 copy.61
  53.8 4.3 fusion.68
  62.8 6.8 select_select_fusion
  71.3 5.9 fusion.15
  78.0 4.2 copy.63.w_other
  82.2 21.9 %shard_map.195 = (bf16[768,1152]{1,0:T(8,128)(2,1)}, f32[3,768,288]{2,1,0:T(8,128)}) custom-call(bf16[192,1152]{1,0:T(8,128)(2,1)} %dynamic-slice_bitcast_fusion.5.x, f32[192,8]{1,0:T(8,128)} %fusion.37.sel, f32[8,6912]{1,0:T(8,128)} %get-tuple-element.162.mod, bf16[3,1152,288]{2,1,0:T(8,128)(2,1)} %bitcast.180, bf16[3,1152,288]{2,1,0:T(8,128)(2,1)} %copy.63.w_other), custom_call_target="tpu_custom_call" | custom-call | tf_op jit(solution)/shard_map/pallas_call | solution.py:386
  104.1 12.9 %shard_map.196 = (bf16[768,512]{1,0:T(8,128)(2,1)}, bf16[768,512]{1,0:T(8,128)(2,1)}, bf16[768,512]{1,0:T(8,128)(2,1)}, bf16[768,288]{1,0:T(8,128)(2,1)}) custom-call(s32[8]{0:T(128)} %pad_add_fusion.spans, f32[3,768,288]{2,1,0:T(8,128)} %get-tuple-element.60.proj, f32[2,1,288]{2,1,0:T(1,128)} %tile.13.gain, f32[768,288]{1,0:T(8,128)} %get-tuple-element.168.cosine, ...), custom_call_target="tpu_custom_call" | custom-call | tf_op jit(solution)/shard_map/pallas_call | solution.py:505
  118.4 53.8 %shard_map.197 = (f32[192,1152]{1,0:T(8,128)}, f32[192,1152]{1,0:T(8,128)}, bf16[768,1152]{1,0:T(8,128)(2,1)}, f32[768,768]{1,0:T(8,128)}, f32[768,768]{1,0:T(8,...) custom-call(bf16[768,288]{1,0:T(8,128)(2,1)} %get-tuple-element.61.att, ...), custom_call_target="tpu_custom_call" | custom-call | tf_op jit(solution)/shard_map/pallas_call | solution.py:386
  172.2 19.0 %shard_map.198 = (bf16[768,1152]{1,0:T(8,128)(2,1)}, f32[3,768,288]{2,1,0:T(8,128)}) custom-call(bf16[192,1152]{1,0:T(8,128)(2,1)} %get-tuple-element.62.x, f32[192,8]{1,0:T(8,128)} %fusion.37.sel, f32[8,6912]{1,0:T(8,128)} %get-tuple-element.161.mod, bf16[3,1152,288]{2,1,0:T(8,128)(2,1)} %bitcast.181, bf16[3,1152,288]{2,1,0:T(8,128)(2,1)} %copy.63.w_other), custom_call_target="tpu_custom_call" | custom-call | tf_op jit(solution)/shard_map/pallas_call | solution.py:386
  191.2 13.3 %shard_map.199 = (bf16[768,512]{1,0:T(8,128)(2,1)}, bf16[768,512]{1,0:T(8,128)(2,1)}, bf16[768,512]{1,0:T(8,128)(2,1)}, bf16[768,288]{1,0:T(8,128)(2,1)}) custom-call(s32[8]{0:T(128)} %pad_add_fusion.spans, f32[3,768,288]{2,1,0:T(8,128)} %get-tuple-element.63.proj, f32[2,1,288]{2,1,0:T(1,128)} %tile.15.gain, f32[768,288]{1,0:T(8,128)} %get-tuple-element.168.cosine, ...), custom_call_target="tpu_custom_call" | custom-call | tf_op jit(solution)/shard_map/pallas_call | solution.py:505
  204.6 46.8 %shard_map.200 = (f32[192,1152]{1,0:T(8,128)}, f32[192,1152]{1,0:T(8,128)}, bf16[768,1152]{1,0:T(8,128)(2,1)}, f32[768,768]{1,0:T(8,128)}, f32[768,768]{1,0:T(8,...) custom-call(bf16[768,288]{1,0:T(8,128)(2,1)} %get-tuple-element.64.att, ...), custom_call_target="tpu_custom_call" | custom-call | tf_op jit(solution)/shard_map/pallas_call | solution.py:386
  251.4 46.6 %shard_map.201 = (bf16[768,1152]{1,0:T(8,128)(2,1)}, bf16[768,768]{1,0:T(8,128)(2,1)}, bf16[768,768]{1,0:T(8,128)(2,1)}, bf16[768,1152]{1,0:T(8,128)(2,1)}, bf16...) custom-call(bf16[192,1152]{1,0:T(8,128)(2,1)} %dynamic-slice_bitcast_fusion.4.dy, ...), custom_call_target="tpu_custom_call" | custom-call | tf_op jit(solution)/shard_map/pallas_call | solution.py:386
  298.0 22.2 %shard_map.202 = (bf16[3,768,288]{2,1,0:T(8,128)(2,1)}, f32[2,1,288]{2,1,0:T(1,128)}) custom-call(s32[8]{0:T(128)} %pad_add_fusion.spans, bf16[768,512]{1,0:T(8,128)(2,1)} %get-tuple-element.69.q, bf16[768,512]{1,0:T(8,128)(2,1)} %get-tuple-element.70.k, bf16[768,512]{1,0:T(8,128)(2,1)} %get-tuple-element.71.v, bf16[768,288]{1,0:T(8,128)(2,1)} %get-tuple-element.77.datt, ...), custom_call_target="tpu_custom_call" | custom-call | tf_op jit(solution)/shard_map/pallas_call | solution.py:505
  325.3 17.2 %shard_map.203 = (f32[192,1152]{1,0:T(8,128)}, bf16[192,1152]{1,0:T(8,128)(2,1)}, f32[2,8,1152]{2,1,0:T(8,128)}) custom-call(bf16[3,768,288]{2,1,0:T(8,128)(2,1)} %get-tuple-element.78.dproj, bf16[192,1152]{1,0:T(8,128)(2,1)} %get-tuple-element.62.x, f32[192,1152]{1,0:T(8,128)} %get-tuple-element.79.dx1, f32[192,8]{1,0:T(8,128)} %fusion.37.sel, ...), custom_call_target="tpu_custom_call" | custom-call | tf_op jit(solution)/shard_map/pallas_call | solution.py:386
  342.5 54.2 %shard_map.204 = (bf16[768,1152]{1,0:T(8,128)(2,1)}, bf16[768,768]{1,0:T(8,128)(2,1)}, bf16[768,768]{1,0:T(8,128)(2,1)}, bf16[768,1152]{1,0:T(8,128)(2,1)}, bf16...) custom-call(bf16[192,1152]{1,0:T(8,128)(2,1)} %get-tuple-element.80.dy, ...), custom_call_target="tpu_custom_call" | custom-call | tf_op jit(solution)/shard_map/pallas_call | solution.py:386
  396.8 21.9 %shard_map.205 = (bf16[3,768,288]{2,1,0:T(8,128)(2,1)}, f32[2,1,288]{2,1,0:T(1,128)}) custom-call(s32[8]{0:T(128)} %pad_add_fusion.spans, bf16[768,512]{1,0:T(8,128)(2,1)} %get-tuple-element.66.q, bf16[768,512]{1,0:T(8,128)(2,1)} %get-tuple-element.67.k, bf16[768,512]{1,0:T(8,128)(2,1)} %get-tuple-element.68.v, bf16[768,288]{1,0:T(8,128)(2,1)} %get-tuple-element.86.datt, ...), custom_call_target="tpu_custom_call" | custom-call | tf_op jit(solution)/shard_map/pallas_call | solution.py:505
  425.3 15.5 %shard_map.206 = (f32[192,1152]{1,0:T(8,128)}, bf16[192,1152]{1,0:T(8,128)(2,1)}, f32[2,8,1152]{2,1,0:T(8,128)}) custom-call(bf16[3,768,288]{2,1,0:T(8,128)(2,1)} %get-tuple-element.87.dproj, bf16[192,1152]{1,0:T(8,128)(2,1)} %dynamic-slice_bitcast_fusion.5.x, f32[192,1152]{1,0:T(8,128)} %get-tuple-element.88.dx1, f32[192,8]{1,0:T(8,128)} %fusion.37.sel, ...), custom_call_target="tpu_custom_call" | custom-call | tf_op jit(solution)/shard_map/pallas_call | solution.py:386
  447.8 6.3 pad_maximum_fusion.3
  454.1 4.1 copy.69
  459.4 14.1 %collective-permute-start.8 = (bf16[4,144,1152]{2,1,0:T(8,128)(2,1)}, bf16[4,144,1152]{2,1,0:T(8,128)(2,1)}, u32[]{:S(2)}, u32[]{:S(2)}) collective-permute-start(bf16[4,144,1152]{2,1,0:T(8,128)(2,1)} %dynamic-slice_bitcast_fusion.2), channel_id=1, source_target_pairs={{0,16},{16,0},{1,17},{17,1},{2,18},{18,2},{3,19},{19,3},{4,20},{20... | collective-permute-start | bytes 3981320 | tf_op jit(solution)/shard_map/ppermute | solution.py:516
  475.1 5.8 pad_maximum_fusion.2
  480.9 4.1 copy.68
  488.3 4.4 convolution_convert_fusion.1
  505.4 8.5 %copy.72 = bf16[1152,2304]{1,0:T(8,128)(2,1)} copy(bf16[1152,2304]{0,1:T(8,128)(2,1)} %pad_maximum_fusion.1) | data formatting | bytes 10616832 | tf_op jit(solution)/shard_map/concatenate | solution.py:681
  538.4 8.6 %copy.71 = bf16[1152,2304]{1,0:T(8,128)(2,1)} copy(bf16[1152,2304]{0,1:T(8,128)(2,1)} %pad_maximum_fusion) | data formatting | bytes 10616832 | tf_op jit(solution)/shard_map/concatenate | solution.py:681
  549.2 4.9 collective-permute-done.10
  558.8 40.8 %psum.15 = f32[2,2,72]{2,1,0:T(2,128)S(1)} all-reduce(f32[2,2,72]{2,1,0:T(2,128)S(1)} %maximum_reduce_fusion), channel_id=1, replica_groups=mesh['section'=2,'dp'=4,'tensor'=4] {'section','dp','tensor'}, use_global_device_ids=true, to_apply=%region_9.10 | all-reduce | flops 288 | bytes 2304 | tf_op jit(solution)/shard_map/psum | solution.py:735
  608.7 16.8 %all-gather.3 = f32[4,6,1728]{2,1,0:T(8,128)S(1)} all-gather(f32[1,6,1728]{2,1,0:T(8,128)S(1)} %fusion.44), channel_id=1, replica_groups=mesh['section'=2,'dp'=4,'tensor'=4] {'dp'}, dimensions={0}, use_global_device_ids=true | all-gather | bytes 207360 | tf_op jit(solution)/shard_map/all_gather | solution.py:721
  625.5 28.4 %psum.14 = f32[6,1152]{1,0:T(8,128)S(1)} all-reduce(f32[6,1152]{1,0:T(8,128)S(1)} %fusion.2), channel_id=1, replica_groups=mesh['section'=2,'dp'=4,'tensor'=4] {'section','tensor'}, use_global_device_ids=true, to_apply=%region_3.4 | all-reduce | flops 6912 | bytes 55296 | tf_op jit(solution)/shard_map/psum | solution.py:732
  654.6 11.8 %all-gather.2 = bf16[4,6,1152]{2,1,0:T(8,128)(2,1)S(1)} all-gather(bf16[1,6,1152]{2,1,0:T(8,128)(2,1)S(1)} %get-tuple-element.165), channel_id=1, replica_groups=mesh['section'=2,'dp'=4,'tensor'=4] {'dp'}, dimensions={0}, use_global_device_ids=true | all-gather | bytes 69120 | tf_op jit(solution)/shard_map/all_gather | solution.py:583
  677.3 8.1 %reduce-scatter.12.cloned.1.call-done = bf16[1,144,2304]{2,1,0:T(8,128)(2,1)} async-done(((bf16[4,144,2304]{2,1,0:T(8,128)(2,1)}), bf16[1,144,2304]{2,1,0:T(8,128)(2,1)}) %reduce-scatter.12.cloned.1.call-update) | async-done | bytes 663568 | tf_op jit(solution)/shard_map/reduce_scatter | solution.py:548
  (219 shorter events, 123.2 us)
Async XLA Ops:
  7.2 62.5 %copy-start = (bf16[2,192,1152]{2,1,0:T(8,128)(2,1)S(1)}, bf16[2,192,1152]{2,1,0:T(8,128)(2,1)}, u32[]{:S(2)}) copy-start(bf16[2,192,1152]{2,1,0:T(8,128)(2,1)} %param.12) | copy-start | bytes 2654212
  7.2 593.0 %reduce-scatter.16.cloned.1.call-start = ((), (), s32[]{:S(2)}) async-start(), calls=%async_computation.9 | async-start | bytes 4423680
  7.2 70.7 %collective-permute-start = (bf16[3,1152,288]{1,2,0:T(8,128)(2,1)}, bf16[3,1152,288]{1,2,0:T(8,128)(2,1)}, u32[]{:S(2)}, u32[]{:S(2)}) collective-permute-start(bf16[3,1152,288]{1,2,0:T(8,128)(2,1)} %bitcast.211), channel_id=1, source_target_pairs={{0,16},{16,0},{1,17},{17,1},{2,18},{18,2},{3,19},{19,3},{4,20},{20... | collective-permute-start | bytes 5971976 | tf_op jit(solution)/shard_map/ppermute | solution.py:516
  7.3 109.7 %collective-permute-start.2 = (bf16[2,1152,768]{2,1,0:T(8,128)(2,1)}, bf16[2,1152,768]{2,1,0:T(8,128)(2,1)}, u32[]{:S(2)}, u32[]{:S(2)}) collective-permute-start(bf16[2,1152,768]{2,1,0:T(8,128)(2,1)} %bitcast.184), channel_id=1, source_target_pairs={{0,16},{16,0},{1,17},{17,1},{2,18},{18,2},{3,19},{19,3},{4,20},{20... | collective-permute-start | bytes 10616840 | tf_op jit(solution)/shard_map/ppermute | solution.py:516
  7.8 109.2 %collective-permute-start.3 = (bf16[768,1152]{1,0:T(8,128)(2,1)}, bf16[768,1152]{1,0:T(8,128)(2,1)S(1)}, u32[]{:S(2)}, u32[]{:S(2)}) collective-permute-start(bf16[768,1152]{1,0:T(8,128)(2,1)} %bitcast.189), channel_id=1, source_target_pairs={{0,16},{16,0},{1,17},{17,1},{2,18},{18,2},{3,19},{19,3},{4,20},{20... | collective-permute-start | bytes 5308424 | tf_op jit(solution)/shard_map/ppermute | solution.py:516
  7.9 109.1 %collective-permute-start.1 = (bf16[288,1152]{1,0:T(8,128)(2,1)}, bf16[288,1152]{1,0:T(8,128)(2,1)S(1)}, u32[]{:S(2)}, u32[]{:S(2)}) collective-permute-start(bf16[288,1152]{1,0:T(8,128)(2,1)} %bitcast.201), channel_id=1, source_target_pairs={{0,16},{16,0},{1,17},{17,1},{2,18},{18,2},{3,19},{19,3},{4,20},{20... | collective-permute-start | bytes 1990664 | tf_op jit(solution)/shard_map/ppermute | solution.py:516
  13.1 28.1 %copy-start.37 = (bf16[1,2,72]{2,1,0:T(2,128)(2,1)S(1)}, bf16[1,2,72]{2,1,0:T(2,128)(2,1)}, u32[]{:S(2)}) copy-start(bf16[1,2,72]{2,1,0:T(2,128)(2,1)} %param.21) | copy-start | bytes 868
  13.1 31.3 %copy-start.29 = (s32[2,768]{1,0:T(2,128)S(1)}, s32[2,768]{1,0:T(2,128)}, u32[]{:S(2)}) copy-start(s32[2,768]{1,0:T(2,128)} %param.15) | copy-start | bytes 18436
  44.5 6.1 copy-start.28
  52.7 17.8 %copy-start.21 = (bf16[2,192,1152]{2,1,0:T(8,128)(2,1)S(1)}, bf16[2,192,1152]{2,1,0:T(8,128)(2,1)}, u32[]{:S(2)}) copy-start(bf16[2,192,1152]{2,1,0:T(8,128)(2,1)} %param.13) | copy-start | bytes 2654212
  425.3 15.6 %copy-start.23 = (f32[4,8,1152]{2,1,0:T(8,128)S(1)}, f32[4,8,1152]{2,1,0:T(8,128)}, u32[]{:S(2)}) copy-start(f32[4,8,1152]{2,1,0:T(8,128)} %get-tuple-element.91) | copy-start | bytes 442372
  425.3 16.5 %copy-start.22 = (f32[4,8,1152]{2,1,0:T(8,128)S(1)}, f32[4,8,1152]{2,1,0:T(8,128)}, u32[]{:S(2)}) copy-start(f32[4,8,1152]{2,1,0:T(8,128)} %get-tuple-element.93) | copy-start | bytes 442372
  425.3 16.5 %copy-start.25 = (f32[2,8,1152]{2,1,0:T(8,128)S(1)}, f32[2,8,1152]{2,1,0:T(8,128)}, u32[]{:S(2)}) copy-start(f32[2,8,1152]{2,1,0:T(8,128)} %get-tuple-element.92) | copy-start | bytes 221188
  444.5 228.9 %reduce-scatter.10.cloned.1.call-start = ((), (), s32[]{:S(2)}) async-start(), calls=%async_computation.6 | async-start | bytes 1658880 | tf_op jit(solution)/shard_map/reduce_scatter | solution.py:548
  458.2 16.2 %copy-start.5 = (bf16[1152,1152]{1,0:T(8,128)(2,1)}, bf16[1152,1152]{1,0:T(8,128)(2,1)S(1)}, u32[]{:S(2)}) copy-start(bf16[1152,1152]{1,0:T(8,128)(2,1)S(1)} %copy.69) | copy-start | bytes 7962628
  458.2 15.3 %copy-start.19 = (bf16[768,288]{1,0:T(8,128)(2,1)S(1)}, bf16[768,288]{1,0:T(8,128)(2,1)}, u32[]{:S(2)}) copy-start(bf16[768,288]{1,0:T(8,128)(2,1)} %get-tuple-element.61.att) | copy-start | bytes 1327108
  458.2 15.3 %copy-start.33 = (bf16[768,1152]{1,0:T(8,128)(2,1)S(1)}, bf16[768,1152]{1,0:T(8,128)(2,1)}, u32[]{:S(2)}) copy-start(bf16[768,1152]{1,0:T(8,128)(2,1)} %get-tuple-element.95) | copy-start | bytes 5308420
  459.4 36.3 %collective-permute-start.8 = (bf16[4,144,1152]{2,1,0:T(8,128)(2,1)}, bf16[4,144,1152]{2,1,0:T(8,128)(2,1)}, u32[]{:S(2)}, u32[]{:S(2)}) collective-permute-start(bf16[4,144,1152]{2,1,0:T(8,128)(2,1)} %dynamic-slice_bitcast_fusion.2), channel_id=1, source_target_pairs={{0,16},{16,0},{1,17},{17,1},{2,18},{18,2},{3,19},{19,3},{4,20},{20... | collective-permute-start | bytes 3981320 | tf_op jit(solution)/shard_map/ppermute | solution.py:516
  486.2 32.0 %collective-permute-start.7 = (bf16[4,144,1152]{2,1,0:T(8,128)(2,1)}, bf16[4,144,1152]{2,1,0:T(8,128)(2,1)}, u32[]{:S(2)}, u32[]{:S(2)}) collective-permute-start(bf16[4,144,1152]{2,1,0:T(8,128)(2,1)} %dynamic-slice_bitcast_fusion.3), channel_id=1, source_target_pairs={{0,16},{16,0},{1,17},{17,1},{2,18},{18,2},{3,19},{19,3},{4,20},{20... | collective-permute-start | bytes 3981320 | tf_op jit(solution)/shard_map/ppermute | solution.py:516
  498.5 174.9 %reduce-scatter.8.cloned.1.call-start = ((), (), s32[]{:S(2)}) async-start(), calls=%async_computation.5 | async-start | bytes 1658880 | tf_op jit(solution)/shard_map/reduce_scatter | solution.py:548
  517.5 10.3 %collective-permute-start.11 = (bf16[4,144,2304]{2,1,0:T(8,128)(2,1)}, bf16[4,144,2304]{2,1,0:T(8,128)(2,1)}, u32[]{:S(2)}, u32[]{:S(2)}) collective-permute-start(bf16[4,144,2304]{2,1,0:T(8,128)(2,1)} %dynamic-slice_bitcast_fusion), channel_id=1, source_target_pairs={{0,16},{16,0},{1,17},{17,1},{2,18},{18,2},{3,19},{19,3},{4,20},{20... | collective-permute-start | bytes 7962632 | tf_op jit(solution)/shard_map/ppermute | solution.py:516
  521.0 156.4 %reduce-scatter.14.cloned.1.call-start = ((), (), s32[]{:S(2)}) async-start(), calls=%async_computation.8 | async-start | bytes 3317760 | tf_op jit(solution)/shard_map/reduce_scatter | solution.py:548
  521.0 6.8 slice-start
  531.7 153.7 %reduce-scatter.12.cloned.1.call-start = ((), (), s32[]{:S(2)}) async-start(), calls=%async_computation.7 | async-start | bytes 3317760 | tf_op jit(solution)/shard_map/reduce_scatter | solution.py:548
  547.0 7.1 %copy-start.3 = (bf16[1152,2304]{1,0:T(8,128)(2,1)S(1)}, bf16[1152,2304]{1,0:T(8,128)(2,1)}, u32[]{:S(2)}) copy-start(bf16[1152,2304]{1,0:T(8,128)(2,1)} %copy.71) | copy-start | bytes 15925252
  549.1 5.0 collective-permute-start.10
  558.7 111.9 %collective-permute-start.5 = (f32[192,1152]{1,0:T(8,128)}, f32[192,1152]{1,0:T(8,128)}, u32[]{:S(2)}, u32[]{:S(2)}) collective-permute-start(f32[192,1152]{1,0:T(8,128)} %get-tuple-element.154), channel_id=1, source_target_pairs={{0,16},{16,0},{1,17},{17,1},{2,18},{18,2},{3,19},{19,3},{4,20},{20... | collective-permute-start | bytes 2654216 | tf_op jit(solution)/shard_map/ppermute | solution.py:516
  602.5 2.2 collective-permute-start.6
  604.4 65.1 %collective-permute-start.4 = (bf16[192,1152]{1,0:T(8,128)(2,1)S(1)}, bf16[192,1152]{1,0:T(8,128)(2,1)S(1)}, u32[]{:S(2)}, u32[]{:S(2)}) collective-permute-start(bf16[192,1152]{1,0:T(8,128)(2,1)S(1)} %get-tuple-element.158), channel_id=1, source_target_pairs={{0,16},{16,0},{1,17},{17,1},{2,18},{18,2},{3,19},{19,3},{4,20},{20... | collective-permute-start | bytes 1327112 | tf_op jit(solution)/shard_map/ppermute | solution.py:516
  604.8 49.1 %copy-start.24 = (bf16[6,1152]{1,0:T(8,128)(2,1)S(1)}, bf16[6,1152]{1,0:T(8,128)(2,1)}, u32[]{:S(2)}) copy-start(bf16[6,1152]{1,0:T(8,128)(2,1)} %param.14) | copy-start | bytes 41476
  674.5 14.2 %collective-permute-start.9 = (bf16[144,1152]{1,0:T(8,128)(2,1)S(1)}, bf16[144,1152]{1,0:T(8,128)(2,1)S(1)}, u32[]{:S(2)}, u32[]{:S(2)}) collective-permute-start(bf16[144,1152]{1,0:T(8,128)(2,1)S(1)} %get-tuple-element.160), channel_id=1, source_target_pairs={{0,16},{16,0},{1,17},{17,1},{2,18},{18,2},{3,19},{19,3},{4,20},{20... | collective-permute-start | bytes 995336 | tf_op jit(solution)/shard_map/ppermute | solution.py:516
  687.7 3.7 collective-permute-start.12
  (26 other events, 60.8 us)
Sparse Core Ops, SparseCore 0:
  444.6 60.4 reduce-scatter.15
  507.3 31.5 reduce-scatter.9
  541.8 30.4 reduce-scatter.7
  574.5 55.3 reduce-scatter.13
  632.1 53.3 reduce-scatter.11
where the time goes:
time: 710 us; the launch traced here: 701 us
  Pallas kernels  345 us (49%)
  blocking collectives  125 us (18%)
  other arithmetic  66.8 us (9%)
  local copies, waits for them, and re-layouts  66.1 us (9%)
  matrix products  45.8 us (6%)
  starting transfers between devices  23.6 us (3%)
  between operations  14.7 us (2%)
  waiting for transfers between devices  13.2 us (2%)
    pallas_call x8, Pallas kernels, ring_call(): pl.pallas_call(kernel, out_shape=outs, in_specs=[vmem() if s else anywher...  275 us
    pallas_call x4, Pallas kernels, local_call(): pl.pallas_call(kernel, out_shape=outs, in_specs=[pl.BlockSpec(memory_spac...  70.3 us
    psum x1, blocking collectives, per_device(): gain_sums = lax.psum(gain_sums, (S, DP, T))  40.8 us
    dot_general x14, matrix products, tn(): lax.dot_general(a, b, (((0,), (0,)), ((), ())), preferred_element_type=F32)  36.2 us
    psum x1, blocking collectives, per_device(): lax.psum(d_lifted, (S, T)) * cond_sigmoid  28.4 us
    all_gather x1, blocking collectives, per_device(): mod_all = lax.all_gather(mod_part, (S, T)).reshape(2, 4, 2, per_micro, -1)  25.4 us
    ppermute x13, starting transfers between devices, swap(): return lax.ppermute(array, S, [(0, 1), (1, 0)])  23.3 us
    concatenate x2, local copies, waits for them, and re-layouts, per_device(): jnp.concatenate([tn(whole2, dgate).astype(BF), tn(whole2, dup).astype(BF)...  17.1 us
  transfers between devices with their start and end apart: 18, of which 2 were waited for; matrix products, arithmetic and copies ran while one was open for 22% of the time, Pallas kernels for 5%

commit v1 on v0

--- a/solution.py
+++ b/solution.py
@@ -2,6 +2,7 @@
 
 import jax
 import jax.numpy as jnp
+import numpy as np
 from jax import lax
 from jax.experimental import pallas as pl
 from jax.experimental.pallas import tpu as pltpu
@@ -78,7 +79,7 @@
     return pl.ds(pl.multiple_of(chunk * rows, rows), rows)
 
 
-def gather(place, mine, whole, sems, base, use):
+def gather(place, mine, whole, sems, base, use, fill=()):
     me, a, b, d = place
     rows = mine.shape[0]
     half = rows // 2
@@ -95,6 +96,8 @@
         copy.start()
     whole[chunk_rows(me, rows), :] = mine[...]
     use(me)
+    for work in fill[:1]:
+        work()
     a0.wait_recv()
     b2 = remote(whole.at[part(a, 0)], whole.at[part(a, 0)], sems, base + 4, b)
     b2.start()
@@ -105,6 +108,8 @@
     use(a)
     b1.wait_recv()
     use(b)
+    for work in fill[1:]:
+        work()
     b2.wait_recv()
     a2.wait_recv()
     use(d)
@@ -112,7 +117,7 @@
         copy.wait_send()
 
 
-def scatter(place, term, bufs, sems, base):
+def scatter(place, term, bufs, sems, base, fill=()):
     me, a, b, d = place
     out, into, keep, own = bufs
     half = keep.shape[1]
@@ -133,6 +138,8 @@
     b0.start()
     keep[1] = total[:half]
     own[...] = term(me)
+    for work in fill[:1]:
+        work()
     d1.wait_recv()
     out[1, hi] = (keep[0] + into[0, hi].astype(F32)).astype(BF)
     a1 = remote(out.at[1, hi], into.at[1, hi], sems, base + 4, a)
@@ -141,6 +148,8 @@
     out[2, lo] = (keep[1] + into[0, lo].astype(F32)).astype(BF)
     b1 = remote(out.at[2, lo], into.at[2, lo], sems, base + 5, b)
     b1.start()
+    for work in fill[1:]:
+        work()
     for copy in (a0, b0, a1, b1):
         copy.wait_recv()
     for copy in (d0, d1, a0, b0, a1, b1):
@@ -188,12 +197,44 @@
     lax.fori_loop(0, 4, body, 0)
 
 
-def mod_rows(sel, mod, which, width):
-    cols = pl.ds(which * width, width)
-    total = sel[:, 0:1] * mod[0:1, cols]
+def mod_rows(sel, mod, which):
+    total = sel[:, 0:1] * mod[which, 0:1]
     for item in (1, 2):
-        total = total + sel[:, item : item + 1] * mod[item : item + 1, cols]
+        total = total + sel[:, item : item + 1] * mod[which, item : item + 1]
     return total
+
+
+def add_sums(dmod, block, sel, values):
+    sums = item_sums(sel, values)
+    half = dmod.shape[2]
+    dmod[2 * block] += sums[:, :half]
+    dmod[2 * block + 1] += sums[:, half:]
+
+
+def weight_grad(x, y, flipped, col, mine, theirs):
+    dp, part, _ = mine.shape
+    section = lax.axis_index(S)
+    width = y.shape[1]
+    block = 256 if width % 256 == 0 else width
+    if x is not None:
+        flipped[...] = x[...].T
+
+    def one(at, to):
+        grad = nn(flipped[...], y[:, at]).astype(BF).reshape(dp, 2, part, -1)
+        first = section == 0
+
+        for target, half in ((mine, 0), (theirs, 1)):
+
+            @pl.when(first)
+            def _(target=target, half=half):
+                target[:, :, to] = grad[:, half]
+
+            @pl.when(jnp.logical_not(first))
+            def _(target=target, half=half):
+                target[:, :, to] = grad[:, 1 - half]
+
+    for i in range(width // block):
+        one(pl.ds(i * block, block), pl.ds(col + i * block, block))
 
 
 def item_sums(sel, values):
@@ -220,8 +261,8 @@
 
     def prepare(rows):
         normal, _ = normed(x[rows].astype(F32))
-        shift = mod_rows(sel[rows], mod, 0, width)
-        scale = mod_rows(sel[rows], mod, 1, width)
+        shift = mod_rows(sel[rows], mod, 0)
+        scale = mod_rows(sel[rows], mod, 1)
         h[rows] = (normal * (1.0 + scale) + shift).astype(BF)
 
     over_blocks(x.shape[0], prepare)
@@ -233,7 +274,7 @@
             waited.append(1)
         rows = chunk_rows(chunk, x.shape[0])
         for k in range(3):
-            proj[k, rows] = nn(whole[rows], w[k])
+            proj[k, rows] = nt(whole[rows], w[k])
 
     gather(place, h, whole, (ssem, rsem), 0, use)
 
@@ -255,11 +296,11 @@
     def between(rows):
         branch = scattered(first, rows)
         br1[rows] = branch
-        mixed = x[rows].astype(F32) + mod_rows(sel[rows], mod, 2, width) * branch
+        mixed = x[rows].astype(F32) + mod_rows(sel[rows], mod, 2) * branch
         x1[rows] = mixed
         normal, _ = normed(mixed)
-        shift = mod_rows(sel[rows], mod, 3, width)
-        scale = mod_rows(sel[rows], mod, 4, width)
+        shift = mod_rows(sel[rows], mod, 3)
+        scale = mod_rows(sel[rows], mod, 4)
         h[rows] = (normal * (1.0 + scale) + shift).astype(BF)
 
     over_blocks(rows_here, between)
@@ -280,14 +321,15 @@
     def finish(rows):
         branch = scattered(second, rows)
         br2[rows] = branch
-        y[rows] = (x1[rows] + mod_rows(sel[rows], mod, 5, width) * branch).astype(BF)
+        y[rows] = (x1[rows] + mod_rows(sel[rows], mod, 5) * branch).astype(BF)
 
     over_blocks(rows_here, finish)
 
 
-def mlp_back_kernel(layer, square, dy, br2, br1, x1, sel, mod, gate_h, up_h, wo0, wo1, wg0, wg1,
-                    wd0, wd1, whole2, dgate, dup, whole1, datt, dx1, dmod, h, h1, gate, up, wo,
-                    wg, wd, o1, i1, k1, s1, ssem, rsem, wsem):
+def mlp_back_kernel(layer, square, dy, br2, br1, x1, sel, mod, gate_h, up_h, hidden_h, rows_h,
+                    wo0, wo1, wg0, wg1, wd0, wd1, whole1, datt, dx1, dmod, mine, theirs, h, h1,
+                    whole2, dgate, dup, gate, up, hidden, saved, flipped, wo, wg, wd, o1, i1, k1,
+                    s1, ssem, rsem, wsem):
     place = ring(square)
     rows_here, width = dy.shape
     load_d = layer_weights(wd0, wd1, layer, wd, wsem.at[0])
@@ -297,14 +339,18 @@
     load_up.start()
     load_g = layer_weights(wg0, wg1, layer, wg, wsem.at[3])
     load_o = layer_weights(wo0, wo1, layer, wo, wsem.at[4])
+    load_hidden = pltpu.make_async_copy(hidden_h, hidden, wsem.at[5])
+    load_hidden.start()
+    load_rows = pltpu.make_async_copy(rows_h, saved, wsem.at[6])
+    load_rows.start()
     greet(place)
     sems = (ssem, rsem)
     dmod[...] = jnp.zeros_like(dmod)
 
     def prepare(rows):
         incoming = dy[rows].astype(F32)
-        h[rows] = (incoming * mod_rows(sel[rows], mod, 5, width)).astype(BF)
-        dmod[3] += item_sums(sel[rows], incoming * br2[rows])
+        h[rows] = (incoming * mod_rows(sel[rows], mod, 5)).astype(BF)
+        add_sums(dmod, 3, sel[rows], incoming * br2[rows])
 
     over_blocks(rows_here, prepare)
     waited = []
@@ -324,62 +370,223 @@
 
     gather(place, h, whole2, sems, 0, use)
     load_g.wait()
+    load_hidden.wait()
     bufs = (o1, i1, k1, s1)
+    f = hidden.shape[1]
 
     def term(chunk):
         rows = chunk_rows(chunk, rows_here)
         return nt(dgate[rows], wg[0]) + nt(dup[rows], wg[1])
 
-    scatter(place, term, bufs, sems, 6)
+    def grad_down():
+        weight_grad(whole2, hidden, flipped, 2 * f, mine, theirs)
+
+    scatter(place, term, bufs, sems, 6, (grad_down,))
 
     def between(rows):
         d_h = scattered(bufs, rows)
         normal, inverse = normed(x1[rows])
-        scale = mod_rows(sel[rows], mod, 4, width)
+        scale = mod_rows(sel[rows], mod, 4)
         d_mixed = dy[rows].astype(F32) + norm_back(d_h * (1.0 + scale), normal, inverse)
         dx1[rows] = d_mixed
-        h1[rows] = (d_mixed * mod_rows(sel[rows], mod, 2, width)).astype(BF)
-        dmod[1] += item_sums(sel[rows], d_h)
-        dmod[2] += item_sums(sel[rows], d_h * normal)
-        dmod[0] += item_sums(sel[rows], d_mixed * br1[rows])
+        h1[rows] = (d_mixed * mod_rows(sel[rows], mod, 2)).astype(BF)
+        add_sums(dmod, 1, sel[rows], d_h)
+        add_sums(dmod, 2, sel[rows], d_h * normal)
+        add_sums(dmod, 0, sel[rows], d_mixed * br1[rows])
 
     over_blocks(rows_here, between)
     load_o.wait()
+    load_rows.wait()
 
     def use_out(chunk):
         rows = chunk_rows(chunk, rows_here)
         datt[rows] = nt(whole1[rows], wo[...]).astype(BF)
 
-    gather(place, h1, whole1, sems, 12, use_out)
-
-
-def qkv_back_kernel(layer, square, dproj, x, dx1, sel, mod, w_own, w_other, du, du_b, dmod, w,
-                    o1, i1, k1, s1, ssem, rsem, wsem):
+    def grad_gate():
+        weight_grad(saved, dgate, flipped, 0, mine, theirs)
+
+    def grad_up():
+        weight_grad(None, dup, flipped, f, mine, theirs)
+
+    gather(place, h1, whole1, sems, 12, use_out, (grad_gate, grad_up))
+
+
+def qkv_back_kernel(layer, square, dproj, x, dx1, sel, mod, part, prev, w_own, w_other, du, du_b,
+                    dmod, w, o1, i1, k1, s1, ssem, rsem, wsem):
     place = ring(square)
     rows_here, width = x.shape
     load = layer_weights(w_own, w_other, layer, w, wsem)
     greet(place)
-    dmod[...] = jnp.zeros_like(dmod)
+    here = dmod.at[layer]
+    dmod[1 - layer] = prev[...]
+    here[pl.ds(0, 4)] = jnp.zeros_like(prev[pl.ds(0, 4)])
+    here[pl.ds(4, 8)] = part[...]
     load.wait()
     bufs = (o1, i1, k1, s1)
 
     def term(chunk):
         rows = chunk_rows(chunk, rows_here)
-        return nt(dproj[0, rows], w[0]) + nt(dproj[1, rows], w[1]) + nt(dproj[2, rows], w[2])
+        return nn(dproj[0, rows], w[0]) + nn(dproj[1, rows], w[1]) + nn(dproj[2, rows], w[2])
 
     scatter(place, term, bufs, (ssem, rsem), 0)
 
     def finish(rows):
         d_h = scattered(bufs, rows)
         normal, inverse = normed(x[rows].astype(F32))
-        scale = mod_rows(sel[rows], mod, 1, width)
+        scale = mod_rows(sel[rows], mod, 1)
         total = dx1[rows] + norm_back(d_h * (1.0 + scale), normal, inverse)
         du[rows] = total
         du_b[rows] = total.astype(BF)
-        dmod[0] += item_sums(sel[rows], d_h)
-        dmod[1] += item_sums(sel[rows], d_h * normal)
+        add_sums(here, 0, sel[rows], d_h)
+        add_sums(here, 1, sel[rows], d_h * normal)
 
     over_blocks(rows_here, finish)
+
+
+def cell():
+    return 4 * lax.axis_index(S) + lax.axis_index(T)
+
+
+def cell_id(index):
+    return {S: index // 4, T: index % 4}
+
+
+def greet_all(dp):
+    sem = pltpu.get_barrier_semaphore()
+    here, shard = cell(), lax.axis_index(DP)
+    for k in range(1, 8):
+        pl.semaphore_signal(
+            sem, inc=1, device_id=cell_id((here + k) % 8), device_id_type=pl.DeviceIdType.MESH
+        )
+    for k in range(1, dp):
+        pl.semaphore_signal(
+            sem, inc=1, device_id={DP: (shard + k) % dp}, device_id_type=pl.DeviceIdType.MESH
+        )
+    pl.semaphore_wait(sem, 7 + dp - 1)
+
+
+def push(src, dst, sems, index, device):
+    copy = pltpu.make_async_remote_copy(
+        src_ref=src,
+        dst_ref=dst,
+        send_sem=sems[0].at[index],
+        recv_sem=sems[1].at[index],
+        device_id=device,
+        device_id_type=pl.DeviceIdType.MESH,
+    )
+    copy.start()
+    return copy
+
+
+def head_kernel(dp, lifted, ada_h, bias, mod, lifted_all, ada, parts, got, ssem, rsem, wsem):
+    load = pltpu.make_async_copy(ada_h, ada, wsem)
+    load.start()
+    greet_all(dp)
+    sems = (ssem, rsem)
+    here, shard = cell(), lax.axis_index(DP)
+    copies = []
+    lifted_all[shard] = lifted[...]
+    for k in range(1, dp):
+        copies.append(
+            push(lifted, lifted_all.at[shard], sems, 6 + k, {DP: (shard + k) % dp})
+        )
+    load.wait()
+    half = parts.shape[3]
+    for micro in range(2):
+        for j in range(3):
+            rows = lifted[pl.ds(micro * 8, 8)].astype(BF)
+            parts[micro, j] = nt(rows, ada[pl.ds(j * half, half)]) + bias[j]
+    for k in range(1, 8):
+        peer = (here + k) % 8
+        copies.append(push(parts.at[peer // 4], got.at[here], sems, k - 1, cell_id(peer)))
+    got[here] = parts[lax.axis_index(S)]
+    for copy in copies:
+        copy.wait_recv()
+    for layer in range(2):
+        for block in range(6):
+            for side in range(2):
+                n = 2 * block + side
+                mod[layer, block, :, pl.ds(side * half, half)] = got[4 * layer + n // 3, n % 3]
+    for copy in copies:
+        copy.wait_send()
+
+
+def tail_kernel(dp, dmod, dgain, lifted_part, ada_h, ada_grad, bias_grad, dl_sum, gain_sum, ada,
+                got, got_gain, total, total_gain, every, every_gain, lifts, ssem, rsem, wsem):
+    load = pltpu.make_async_copy(ada_h, ada, wsem)
+    load.start()
+    greet_all(dp)
+    sems = (ssem, rsem)
+    here, shard = cell(), lax.axis_index(DP)
+    section, place = lax.axis_index(S), lax.axis_index(T)
+    sends, arrivals = [], []
+    for k in range(1, 8):
+        peer = (here + k) % 8
+        to = cell_id(peer)
+        arrivals.append(
+            push(dmod.at[peer // 4, pl.ds(3 * (peer % 4), 3)], got.at[here], sems, k - 1, to)
+        )
+        arrivals.append(push(dgain.at[peer // 4], got_gain.at[here], sems, 6 + k, to))
+    got[here] = dmod[section, pl.ds(3 * place, 3)]
+    got_gain[here] = dgain[section]
+    for copy in arrivals:
+        copy.wait_recv()
+    sends += arrivals
+    for micro in range(2):
+        total[micro] = (got[4 * micro] + got[4 * micro + 1]) + (got[4 * micro + 2] + got[4 * micro + 3])
+    gain = got_gain[0]
+    for k in range(1, 8):
+        gain = gain + got_gain[k]
+    total_gain[...] = gain
+    arrivals = []
+    for k in range(1, dp):
+        to = {DP: (shard + k) % dp}
+        arrivals.append(push(total, every.at[shard], sems, 13 + k, to))
+        arrivals.append(push(total_gain, every_gain.at[shard], sems, 12 + dp + k, to))
+    every[shard] = total[...]
+    every_gain[shard] = total_gain[...]
+    load.wait()
+    half = total.shape[3]
+    for micro in range(2):
+        lift = two(nn, total[micro, 0], ada[pl.ds(0, half)])
+        for j in range(1, 3):
+            lift = lift + two(nn, total[micro, j], ada[pl.ds(j * half, half)])
+        lifts[here, micro] = lift
+    base = 13 + 2 * (dp - 1)
+    lift_copies = []
+    for k in range(1, 8):
+        lift_copies.append(
+            push(lifts.at[here], lifts.at[here], sems, base + k, cell_id((here + k) % 8))
+        )
+    for copy in arrivals:
+        copy.wait_recv()
+    sends += arrivals
+    gain = every_gain[0]
+    for k in range(1, dp):
+        gain = gain + every_gain[k]
+    gain_sum[...] = gain
+    for j in range(3):
+        bias = jnp.zeros((1, half), F32)
+        grad = jnp.zeros((lifted_part.shape[2], half), F32)
+        for k in range(dp):
+            for micro in range(2):
+                block = every[k, micro, j]
+                bias = bias + jnp.sum(block, axis=0, keepdims=True)
+                high = block.astype(BF)
+                low = (block - high.astype(F32)).astype(BF)
+                rows = lifted_part[2 * k + micro].astype(BF)
+                grad = grad + tn(rows, high) + tn(rows, low)
+        bias_grad[j] = bias
+        ada_grad[:, pl.ds(j * half, half)] = grad
+    for copy in lift_copies:
+        copy.wait_recv()
+    sends += lift_copies
+    lift = lifts[0]
+    for k in range(1, 8):
+        lift = lift + lifts[k]
+    dl_sum[...] = lift
+    for copy in sends:
+        copy.wait_send()
 
 
 def ring_call(kernel, ident, outs, scratch, args, spaces):
@@ -453,8 +660,8 @@
     return tn(d_scores, key) * scale, nn(d_scores, query) * scale, d_value
 
 
-def attention_back_kernel(spans, q, k, v, datt, proj, gain, cosine, sine, turn, spread, ones,
-                          dproj, dgain, grad, dq, dk, dv):
+def attention_back_kernel(spans, q, k, v, datt, proj, gain, whole, att, rows1, cosine, sine, turn,
+                          spread, ones, dproj, dgain, mine, theirs, grad, dq, dk, dv, flipped):
     heads = spread.shape[1] // PAD
     rows, packed = datt.shape
     head = packed // heads
@@ -499,6 +706,11 @@
         dproj[2, at] = nt(dv[at].astype(BF), spread[...]).astype(BF)
 
     over_blocks(rows, finish)
+    for which in range(3):
+        weight_grad(
+            None if which else whole, dproj.at[which], flipped, which * packed, mine, theirs
+        )
+    weight_grad(rows1, att, flipped, 3 * packed, mine, theirs)
 
 
 def local_call(kernel, outs, scratch, spans, args):
@@ -518,32 +730,32 @@
 
 def head_tables(positions, packed, head):
     quarter = head // 4
-    frequency = 10000.0 ** (-jnp.arange(quarter, dtype=F32) / quarter)
-    lane = jnp.arange(packed) % head
-    per_lane = frequency[lane % quarter][None, :]
-    place = jnp.where((lane // (2 * quarter) == 0)[None, :], positions[0][:, None], positions[1][:, None])
-    angle = place.astype(F32) * per_lane
-    rows = jnp.arange(packed)[:, None]
-    cols = jnp.arange(packed)[None, :]
+    frequency = np.float32(10000.0) ** (-np.arange(quarter, dtype=np.float32) / quarter)
+    lane = np.arange(packed) % head
+    angle = np.arange(32, dtype=np.float32)[:, None] * frequency[lane % quarter][None, :]
+    by_row = (lane // (2 * quarter) == 0)[None, :]
+    table = np.concatenate([np.where(by_row, t, 0.0) for t in (np.cos(angle), np.sin(angle))], axis=1)
+    other = np.concatenate([np.where(by_row, 0.0, t) for t in (np.cos(angle), np.sin(angle))], axis=1)
+    table = jnp.asarray(np.concatenate([table, other]).astype(np.float32))
+    slots = jnp.arange(32)[None, :]
+    hot = jnp.concatenate(
+        [positions[0][:, None] == slots, positions[1][:, None] == slots], axis=1
+    ).astype(F32)
+    both = jnp.dot(hot, table, precision=PRECISE)
+    rows = np.arange(packed)[:, None]
+    cols = np.arange(packed)[None, :]
     early = (cols % (2 * quarter)) < quarter
-    turn = jnp.where(early & (rows == cols + quarter), -1.0, 0.0)
-    turn = turn + jnp.where(~early & (rows == cols - quarter), 1.0, 0.0)
+    turn = np.where(early & (rows == cols + quarter), -1.0, 0.0)
+    turn = turn + np.where(~early & (rows == cols - quarter), 1.0, 0.0)
     heads = packed // head
-    wide = jnp.arange(heads * PAD)[None, :]
+    wide = np.arange(heads * PAD)[None, :]
     spread = (rows // head == wide // PAD) & (rows % head == wide % PAD)
     ones = rows // head == cols // head
-    return jnp.cos(angle), jnp.sin(angle), turn.astype(BF), spread.astype(BF), ones.astype(BF)
-
-
-def halves(pack, section, dp):
-    wide = pack.reshape(dp, 2, -1, pack.shape[1])
-    mine = lax.dynamic_index_in_dim(wide, section, 1, keepdims=False)
-    theirs = lax.dynamic_index_in_dim(wide, 1 - section, 1, keepdims=False)
-    return mine, theirs
-
-
-def reduced(pack, section, dp):
-    mine, theirs = halves(pack.astype(BF), section, dp)
+    lanes = tuple(jnp.asarray(m.astype(np.float32)).astype(BF) for m in (turn, spread, ones))
+    return (both[:, :packed], both[:, packed:]) + lanes
+
+
+def reduced(mine, theirs):
     total = (mine.astype(F32) + swap(theirs).astype(F32)).astype(BF)
     return lax.psum_scatter(total, DP, scatter_dimension=0, tiled=True)[0]
 
@@ -567,20 +779,36 @@
     packed = w_qkv.shape[-1]
     heads = packed // head
     hidden_here = w_down.shape[1]
-    own = (w_qkv[0], w_out[0], w_gate_up[0], w_down[0])
+    own = (jnp.swapaxes(w_qkv[0], 1, 2), w_out[0], w_gate_up[0], w_down[0])
     other = tuple(swap(w) for w in own)
 
     cond_wide = cond.astype(F32)
     cond_sigmoid = jax.nn.sigmoid(cond_wide)
-    lifted = (cond_wide * cond_sigmoid).astype(BF)
-    mod_part = nn(lifted, ada_weight[0]) + ada_bias[0].astype(F32)[None, :]
-    mod_all = lax.all_gather(mod_part, (S, T)).reshape(2, 4, 2, per_micro, -1)
-    mod_mine = lax.dynamic_index_in_dim(mod_all, section, 2, keepdims=False)
-    mod_mine = jnp.swapaxes(mod_mine, 1, 2).reshape(2, per_micro, -1)
-    mod_mine = jnp.pad(mod_mine, ((0, 0), (0, 8 - per_micro), (0, 0)))
+    lifted = (cond_wide * cond_sigmoid).astype(BF).astype(F32).reshape(2, per_micro, width)
+    lifted = jnp.pad(lifted, ((0, 0), (0, 8 - per_micro), (0, 0))).reshape(16, width)
+    ada = ada_weight[0].T
+    half = width // 2
+    bias = ada_bias.astype(F32).reshape(3, 1, half)
+    mods, lifted_all = ring_call(
+        functools.partial(head_kernel, dp),
+        8,
+        [sds((2, 6, 8, width), F32), sds((dp, 16, width), F32)],
+        [
+            pltpu.VMEM((3 * half, width), BF),
+            pltpu.VMEM((2, 3, 8, half), F32),
+            pltpu.VMEM((8, 3, 8, half), F32),
+        ]
+        + dma_sems(6 + dp)
+        + [pltpu.SemaphoreType.DMA],
+        (lifted, ada, bias),
+        (1, 0, 1),
+    )
     gains = lax.all_gather(qk_gain[0], S).astype(F32)
     gains = jnp.tile(gains, (1, 1, heads)).reshape(2, 2, 1, packed)
-    lifted_all = lax.all_gather(lifted, DP, tiled=True)
+    part = width // dp
+    shard = lax.axis_index(DP)
+    lifted_part = lax.dynamic_slice_in_dim(lifted_all, shard * part, part, 2)
+    lifted_part = lifted_part.reshape(2 * dp, 8, part)
 
     ids = lax.dynamic_index_in_dim(patch_item, section, 0, keepdims=False)
     ids = jnp.where(ids >= 0, ids - lax.axis_index(DP) * items - section * per_micro, -1)
@@ -595,12 +823,12 @@
     x = lax.dynamic_index_in_dim(tokens, section, 0, keepdims=False)
     kept = []
     for layer in range(2):
-        mod = mod_mine[layer]
+        mod = mods[layer]
         whole1, proj = ring_call(
             functools.partial(qkv_kernel, layer, square),
             layer,
             [sds((seq, width), BF), sds((3, seq, packed), F32)],
-            [pltpu.VMEM((rows, width), BF), pltpu.VMEM((3, width, packed), BF)]
+            [pltpu.VMEM((rows, width), BF), pltpu.VMEM((3, packed, width), BF)]
             + dma_sems(6)
             + [pltpu.SemaphoreType.DMA],
             (x, sel, mod, own[0], other[0]),
@@ -644,96 +872,108 @@
 
     dy = lax.dynamic_index_in_dim(cotangent, section, 0, keepdims=False)
     packs = [None, None]
-    d_mods = [None, None]
+    prev = jnp.zeros((12, 8, half), F32)
     d_gains = [None, None]
     d_inputs = [None, None]
     for layer in (1, 0):
         x, whole1, proj, q, k, v, att, br1, x1, whole2, gate, up, hidden, br2, y = kept[layer]
-        mod = mod_mine[layer]
-        rows2, dgate, dup, rows1, datt, dx1, dmod_a = ring_call(
+        mod = mods[layer]
+        rows1, datt, dx1, dmod_a, mine, theirs = ring_call(
             functools.partial(mlp_back_kernel, layer, square),
             4 + layer,
             [
                 sds((seq, width), BF),
-                sds((seq, hidden_here), BF),
-                sds((seq, hidden_here), BF),
-                sds((seq, width), BF),
                 sds((seq, packed), BF),
                 sds((rows, width), F32),
-                sds((4, 8, width), F32),
+                sds((8, 8, half), F32),
+                sds((dp, part // 2, 3 * hidden_here), BF),
+                sds((dp, part // 2, 3 * hidden_here), BF),
             ],
             [
                 pltpu.VMEM((rows, width), BF),
                 pltpu.VMEM((rows, width), BF),
+                pltpu.VMEM((seq, width), BF),
+                pltpu.VMEM((seq, hidden_here), BF),
+                pltpu.VMEM((seq, hidden_here), BF),
                 pltpu.VMEM((seq, hidden_here), F32),
                 pltpu.VMEM((seq, hidden_here), F32),
+                pltpu.VMEM((seq, hidden_here), BF),
+                pltpu.VMEM((seq, width), BF),
+                pltpu.VMEM((width, seq), BF),
                 pltpu.VMEM((packed, width), BF),
                 pltpu.VMEM((2, width, hidden_here), BF),
                 pltpu.VMEM((hidden_here, width), BF),
             ]
             + scatter_scratch(rows, width)
             + dma_sems(18)
-            + [pltpu.SemaphoreType.DMA((5,))],
-            (dy, br2, br1, x1, sel, mod, gate, up, own[1], other[1], own[2], other[2], own[3],
-             other[3]),
-            (1,) * 6 + (0,) * 8,
-        )
-        grads_mlp = jnp.concatenate(
-            [tn(whole2, dgate).astype(BF), tn(whole2, dup).astype(BF), tn(rows2, hidden).astype(BF)],
-            axis=1,
-        )
-        pack_mlp = reduced(grads_mlp, section, dp)
-        dproj, dgain = local_call(
+            + [pltpu.SemaphoreType.DMA((7,))],
+            (dy, br2, br1, x1, sel, mod, gate, up, hidden, whole2, own[1], other[1], own[2],
+             other[2], own[3], other[3]),
+            (1,) * 6 + (0,) * 10,
+        )
+        pack_mlp = reduced(mine, theirs)
+        dproj, dgain, mine, theirs = local_call(
             attention_back_kernel,
-            [sds((3, seq, packed), BF), sds((2, 1, packed), F32)],
-            [pltpu.VMEM((seq, heads * PAD), BF)] + [pltpu.VMEM((seq, heads * PAD), F32)] * 3,
+            [
+                sds((3, seq, packed), BF),
+                sds((2, 1, packed), F32),
+                sds((dp, part // 2, 4 * packed), BF),
+                sds((dp, part // 2, 4 * packed), BF),
+            ],
+            [pltpu.VMEM((seq, heads * PAD), BF)]
+            + [pltpu.VMEM((seq, heads * PAD), F32)] * 3
+            + [pltpu.VMEM((width, seq), BF)],
             spans,
-            (q, k, v, datt, proj, gains[layer]) + tables,
-        )
-        du, du_b, dmod_b = ring_call(
+            (q, k, v, datt, proj, gains[layer], whole1, att, rows1) + tables,
+        )
+        pack_att = reduced(mine, theirs)
+        du, du_b, d_mod = ring_call(
             functools.partial(qkv_back_kernel, layer, square),
             6 + layer,
-            [sds((rows, width), F32), sds((rows, width), BF), sds((2, 8, width), F32)],
-            [pltpu.VMEM((3, width, packed), BF)]
+            [sds((rows, width), F32), sds((rows, width), BF), sds((2, 12, 8, half), F32)],
+            [pltpu.VMEM((3, packed, width), BF)]
             + scatter_scratch(rows, width)
             + dma_sems(6)
             + [pltpu.SemaphoreType.DMA],
-            (dproj, x, dx1, sel, mod, own[0], other[0]),
-            (1,) * 5 + (0,) * 2,
-        )
-        grads_att = jnp.concatenate(
-            [tn(whole1, dproj[0]).astype(BF), tn(whole1, dproj[1]).astype(BF),
-             tn(whole1, dproj[2]).astype(BF), tn(rows1, att).astype(BF)],
-            axis=1,
-        )
-        pack_att = reduced(grads_att, section, dp)
+            (dproj, x, dx1, sel, mod, dmod_a, prev, own[0], other[0]),
+            (1,) * 7 + (0,) * 2,
+        )
+        prev = d_mod[1]
         packs[layer] = (pack_mlp, pack_att)
-        d_mods[layer] = jnp.concatenate([dmod_b, dmod_a])[:, :per_micro]
         d_gains[layer] = dgain
         d_inputs[layer] = du_b if layer else du
         dy = du_b
 
-    d_mod = jnp.stack(d_mods).swapaxes(1, 2).reshape(2 * per_micro, -1)
-    d_mod = lax.psum_scatter(d_mod, T, scatter_dimension=1, tiled=True).reshape(2, per_micro, -1)
-    keep = jnp.where(first, d_mod[0], d_mod[1])
-    got = swap(jnp.where(first, d_mod[1], d_mod[0]))
-    mod_grads = jnp.where(first, jnp.concatenate([keep, got]), jnp.concatenate([got, keep]))
-    mod_grads_all = lax.all_gather(mod_grads, DP, tiled=True)
-    dp_index = lax.axis_index(DP)
-    part = width // dp
-    lifted_part = lax.dynamic_slice_in_dim(lifted_all, dp_index * part, part, 1).astype(F32)
-    g_ada_w = lax.dot_general(lifted_part, mod_grads_all, (((0,), (0,)), ((), ())), precision=PRECISE)
+    gain_parts = jnp.pad(jnp.stack(d_gains).reshape(2, 2, packed), ((0, 0), (0, 6), (0, 0)))
+    g_ada_w, bias_grad, dl_sum, gain_sum = ring_call(
+        functools.partial(tail_kernel, dp),
+        9,
+        [
+            sds((part, 3 * half), F32),
+            sds((3, 1, half), F32),
+            sds((2, 8, width), F32),
+            sds((8, packed), F32),
+        ],
+        [
+            pltpu.VMEM((3 * half, width), BF),
+            pltpu.VMEM((8, 3, 8, half), F32),
+            pltpu.VMEM((8, 8, packed), F32),
+            pltpu.VMEM((2, 3, 8, half), F32),
+            pltpu.VMEM((8, packed), F32),
+            pltpu.VMEM((dp, 2, 3, 8, half), F32),
+            pltpu.VMEM((dp, 8, packed), F32),
+            pltpu.VMEM((8, 2, 8, width), F32),
+        ]
+        + dma_sems(13 + 2 * (dp - 1) + 8)
+        + [pltpu.SemaphoreType.DMA],
+        (d_mod, gain_parts, lifted_part, ada),
+        (1, 1, 1, 0),
+    )
     bias_part = ada_bias.shape[1] // dp
-    g_ada_b = lax.dynamic_slice_in_dim(jnp.sum(mod_grads_all, axis=0), dp_index * bias_part, bias_part)
-    d_lifted = lax.dot_general(
-        mod_grads, ada_weight[0].astype(F32), (((1,), (1,)), ((), ())), precision=PRECISE
-    )
-    cond_grad = (
-        lax.psum(d_lifted, (S, T)) * cond_sigmoid * (1.0 + cond_wide * (1.0 - cond_sigmoid))
-    )
-    gain_sums = jnp.stack(d_gains).reshape(2, 2, heads, head).sum(axis=2)
-    gain_sums = lax.psum(gain_sums, (S, DP, T))
-    gain_total = lax.dynamic_index_in_dim(gain_sums, section, 0)
+    g_ada_b = lax.dynamic_slice_in_dim(bias_grad.reshape(-1), shard * bias_part, bias_part)
+    cond_grad = dl_sum[:, :per_micro].reshape(items, width) * cond_sigmoid
+    cond_grad = cond_grad * (1.0 + cond_wide * (1.0 - cond_sigmoid))
+    gain_total = gain_sum[:2].reshape(1, 2, heads, head).sum(axis=2)
 
     mlp = own_layer(section, (packs[0][0], packs[1][0]))
     attn = own_layer(section, (packs[0][1], packs[1][1]))

time: 710 us -> 603 us (0.85)
  blocking collectives: 125 us -> 2.01 us
  Pallas kernels: 345 us -> 426 us
  waiting for transfers between devices: 13.2 us -> 69.5 us
  matrix products: 45.8 us -> 3.04 us
  other arithmetic: 66.8 us -> 30.2 us
  local copies, waits for them, and re-layouts: 66.1 us -> 30.5 us
    psum x2 -> x0, blocking collectives: 69.2 us -> none  [the longest x1 40.8 us: per_device(): gain_sums = lax.psum(gain_sums, (S, DP, T))]
    pallas_call x8 -> x10, Pallas kernels: 275 us -> 340 us  [ring_call(): pl.pallas_call(kernel, out_shape=outs, in_specs=[vmem() if s else anywher...]
    all_gather x3 -> x0, blocking collectives: 54 us -> none  [the longest x1 25.4 us: per_device(): mod_all = lax.all_gather(mod_part, (S, T)).reshape(2, 4, 2, per_micro, -1)]
    reduce_scatter x4, waiting for transfers between devices: 8.13 us -> 58 us  [reduced(): return lax.psum_scatter(total, DP, scatter_dimension=0, tiled=True)[0]]
    dot_general x17 -> x2, matrix products: 45.8 us -> 3.04 us  [head_tables(): both = jnp.dot(hot, table, precision=PRECISE)]
    concatenate x4 -> x0, local copies, waits for them, and re-layouts: 25.3 us -> none  [the longest x2 17.1 us: per_device(): jnp.concatenate([tn(whole2, dgate).astype(BF), tn(whole2, dup).astype(BF)...]
    concatenate x4 -> x0, other arithmetic: 18 us -> none  [the longest x2 12.1 us: per_device(): jnp.concatenate([tn(whole1, dproj[0]).astype(BF), tn(whole1, dproj[1]).as...]
    pallas_call x4, Pallas kernels: 70.3 us -> 85.6 us  [local_call(): pl.pallas_call(kernel, out_shape=outs, in_specs=[pl.BlockSpec(memory_spac...]
  transfers between devices with their start and end apart: 18 -> 16, of which waited for: 2 -> 6; matrix products, arithmetic and copies ran while one was open for 22% -> 9% of each run, Pallas kernels for 5% -> 36%
where the time goes in v1:
time: 603 us; the launch traced here: 598 us
  Pallas kernels  426 us (71%)
  waiting for transfers between devices  69.5 us (12%)
  local copies, waits for them, and re-layouts  30.5 us (5%)
  other arithmetic  30.2 us (5%)
  starting transfers between devices  23 us (4%)
  between operations  14.3 us (2%)
    pallas_call x10, Pallas kernels, ring_call(): pl.pallas_call(kernel, out_shape=outs, in_specs=[vmem() if s else anywher...  340 us
    pallas_call x4, Pallas kernels, local_call(): pl.pallas_call(kernel, out_shape=outs, in_specs=[pl.BlockSpec(memory_spac...  85.6 us
    reduce_scatter x4, waiting for transfers between devices, reduced(): return lax.psum_scatter(total, DP, scatter_dimension=0, tiled=True)[0]  58 us
    ppermute x12, starting transfers between devices, swap(): return lax.ppermute(array, S, [(0, 1), (1, 0)])  22.7 us
  transfers between devices with their start and end apart: 16, of which 6 were waited for; matrix products, arithmetic and copies ran while one was open for 9% of the time, Pallas kernels for 36%

profile of v1, /device:TPU:1, one launch (start us, length us, event | category | flops | bytes accessed | tf_op | source)
XLA Modules:
  0.0 598.3 jit_solution(11442723679916397612)
XLA Ops:
  9.8 1.9 fusion.3
  17.7 2.6 copy.43.cosine
  20.3 2.6 copy.44.sine
  22.9 2.0 all_gather.3
  27.7 15.7 %shard_map.231 = (f32[2,6,8,1152]{3,2,1,0:T(8,128)}, f32[4,16,1152]{2,1,0:T(8,128)}) custom-call(f32[16,1152]{1,0:T(8,128)} %bitcast_convert_fusion.lifted, bf16[1728,1152]{1,0:T(8,128)(2,1)} %bitcast.94, f32[3,1,576]{2,1,0:T(1,128)} %reshape.255.bias), custom_call_target="tpu_custom_call" | custom-call | tf_op jit(solution)/shard_map/pallas_call | solution.py:593
  44.9 1.8 dynamic-slice_bitcast_fusion.dy
  49.5 21.5 %shard_map.232 = (bf16[768,1152]{1,0:T(8,128)(2,1)}, f32[3,768,288]{2,1,0:T(8,128)}) custom-call(bf16[192,1152]{1,0:T(8,128)(2,1)} %dynamic-slice_bitcast_fusion.1.x, f32[192,8]{1,0:T(8,128)} %fusion.6.sel, f32[6,8,1152]{2,1,0:T(8,128)} %get-tuple-element.198.mod, bf16[3,288,1152]{2,1,0:T(8,128)(2,1)} %bitcast.85, bf16[3,288,1152]{2,1,0:T(8,128)(2,1)} %copy-done.2), custom_call_target="tpu_custom_call" | custom-call | tf_op jit(solution)/shard_map/pallas_call | solution.py:593
  71.1 12.9 %shard_map.233 = (bf16[768,512]{1,0:T(8,128)(2,1)}, bf16[768,512]{1,0:T(8,128)(2,1)}, bf16[768,512]{1,0:T(8,128)(2,1)}, bf16[768,288]{1,0:T(8,128)(2,1)}) custom-call(s32[8]{0:T(128)} %pad_add_fusion.spans, f32[3,768,288]{2,1,0:T(8,128)} %get-tuple-element.69.proj, f32[2,1,288]{2,1,0:T(1,128)} %tile.13.gain, f32[768,288]{1,0:T(8,128)} %copy.43.cosine, ...), custom_call_target="tpu_custom_call" | custom-call | tf_op jit(solution)/shard_map/pallas_call | solution.py:717
  84.8 50.4 %shard_map.234 = (f32[192,1152]{1,0:T(8,128)}, f32[192,1152]{1,0:T(8,128)}, bf16[768,1152]{1,0:T(8,128)(2,1)}, f32[768,768]{1,0:T(8,128)}, f32[768,768]{1,0:T(8,...) custom-call(bf16[768,288]{1,0:T(8,128)(2,1)} %get-tuple-element.70.att, ...), custom_call_target="tpu_custom_call" | custom-call | tf_op jit(solution)/shard_map/pallas_call | solution.py:593
  135.2 19.2 %shard_map.235 = (bf16[768,1152]{1,0:T(8,128)(2,1)}, f32[3,768,288]{2,1,0:T(8,128)}) custom-call(bf16[192,1152]{1,0:T(8,128)(2,1)} %get-tuple-element.71.x, f32[192,8]{1,0:T(8,128)} %fusion.6.sel, f32[6,8,1152]{2,1,0:T(8,128)} %get-tuple-element.197.mod, bf16[3,288,1152]{2,1,0:T(8,128)(2,1)} %bitcast.86, bf16[3,288,1152]{2,1,0:T(8,128)(2,1)} %copy-done.2), custom_call_target="tpu_custom_call" | custom-call | tf_op jit(solution)/shard_map/pallas_call | solution.py:593
  154.4 12.9 %shard_map.236 = (bf16[768,512]{1,0:T(8,128)(2,1)}, bf16[768,512]{1,0:T(8,128)(2,1)}, bf16[768,512]{1,0:T(8,128)(2,1)}, bf16[768,288]{1,0:T(8,128)(2,1)}) custom-call(s32[8]{0:T(128)} %pad_add_fusion.spans, f32[3,768,288]{2,1,0:T(8,128)} %get-tuple-element.72.proj, f32[2,1,288]{2,1,0:T(1,128)} %tile.15.gain, f32[768,288]{1,0:T(8,128)} %copy.43.cosine, ...), custom_call_target="tpu_custom_call" | custom-call | tf_op jit(solution)/shard_map/pallas_call | solution.py:717
  167.3 47.2 %shard_map.237 = (f32[192,1152]{1,0:T(8,128)}, f32[192,1152]{1,0:T(8,128)}, bf16[768,1152]{1,0:T(8,128)(2,1)}, f32[768,768]{1,0:T(8,128)}, f32[768,768]{1,0:T(8,...) custom-call(bf16[768,288]{1,0:T(8,128)(2,1)} %get-tuple-element.73.att, ...), custom_call_target="tpu_custom_call" | custom-call | tf_op jit(solution)/shard_map/pallas_call | solution.py:593
  214.5 48.6 %shard_map.238 = (bf16[768,1152]{1,0:T(8,128)(2,1)}, bf16[768,288]{1,0:T(8,128)(2,1)}, f32[192,1152]{1,0:T(8,128)}, f32[8,8,576]{2,1,0:T(8,128)}, bf16[4,144,230...) custom-call(bf16[192,1152]{1,0:T(8,128)(2,1)} %dynamic-slice_bitcast_fusion.dy, f32[192,1152]{1,0:T(8,128)} %get-tuple-element.81.br2, ...), custom_call_target="tpu_custom_call" | custom-call | tf_op jit(solution)/shard_map/pallas_call | solution.py:593
  263.1 30.0 %shard_map.239 = (bf16[3,768,288]{2,1,0:T(8,128)(2,1)}, f32[2,1,288]{2,1,0:T(1,128)}, bf16[4,144,1152]{2,1,0:T(8,128)(2,1)}, bf16[4,144,1152]{2,1,0:T(8,128)(2,1)}) custom-call(s32[8]{0:T(128)} %pad_add_fusion.spans, bf16[768,512]{1,0:T(8,128)(2,1)} %get-tuple-element.78.q, bf16[768,512]{1,0:T(8,128)(2,1)} %get-tuple-element.79.k, ...), custom_call_target="tpu_custom_call" | custom-call | tf_op jit(solution)/shard_map/pallas_call | solution.py:717
  293.1 11.9 %collective-permute-start.7 = (bf16[4,144,1152]{2,1,0:T(8,128)(2,1)}, bf16[4,144,1152]{2,1,0:T(8,128)(2,1)S(1)}, u32[]{:S(2)}, u32[]{:S(2)}) collective-permute-start(bf16[4,144,1152]{2,1,0:T(8,128)(2,1)} %get-tuple-element.118), channel_id=1, source_target_pairs={{0,16},{16,0},{1,17},{17,1},{2,18},{18,2},{3,19},{19,3},{4,20},{20... | collective-permute-start | bytes 3981320 | tf_op jit(solution)/shard_map/ppermute | solution.py:728
  305.0 2.9 collective-permute-done.7
  307.9 2.7 add_convert_fusion.2
  311.4 22.0 %shard_map.240 = (f32[192,1152]{1,0:T(8,128)}, bf16[192,1152]{1,0:T(8,128)(2,1)}, f32[2,12,8,576]{3,2,1,0:T(8,128)}) custom-call(bf16[3,768,288]{2,1,0:T(8,128)(2,1)} %get-tuple-element.91.dproj, bf16[192,1152]{1,0:T(8,128)(2,1)} %get-tuple-element.71.x, f32[192,1152]{1,0:T(8,128)} %get-tuple-element.92.dx1, f32[192,8]{1,0:T(8,128)} %fusion.6.sel, ...), custom_call_target="tpu_custom_call" | custom-call | tf_op jit(solution)/shard_map/pallas_call | solution.py:593
  333.4 56.4 %shard_map.241 = (bf16[768,1152]{1,0:T(8,128)(2,1)}, bf16[768,288]{1,0:T(8,128)(2,1)}, f32[192,1152]{1,0:T(8,128)}, f32[8,8,576]{2,1,0:T(8,128)}, bf16[4,144,230...) custom-call(bf16[192,1152]{1,0:T(8,128)(2,1)} %get-tuple-element.94.dy, f32[192,1152]{1,0:T(8,128)} %get-tuple-element.95.br2, ...), custom_call_target="tpu_custom_call" | custom-call | tf_op jit(solution)/shard_map/pallas_call | solution.py:593
  389.8 29.8 %shard_map.242 = (bf16[3,768,288]{2,1,0:T(8,128)(2,1)}, f32[2,1,288]{2,1,0:T(1,128)}, bf16[4,144,1152]{2,1,0:T(8,128)(2,1)}, bf16[4,144,1152]{2,1,0:T(8,128)(2,1)}) custom-call(s32[8]{0:T(128)} %pad_add_fusion.spans, bf16[768,512]{1,0:T(8,128)(2,1)} %get-tuple-element.75.q, bf16[768,512]{1,0:T(8,128)(2,1)} %get-tuple-element.76.k, ...), custom_call_target="tpu_custom_call" | custom-call | tf_op jit(solution)/shard_map/pallas_call | solution.py:717
  419.6 4.9 collective-permute-start.6
  424.6 2.8 collective-permute-done.6
  427.4 2.9 add_convert_fusion.3
  431.3 3.9 add_convert_fusion
  435.9 4.8 collective-permute-done.9
  440.7 2.2 add_convert_fusion.1
  445.4 23.8 %shard_map.243 = (f32[192,1152]{1,0:T(8,128)}, bf16[192,1152]{1,0:T(8,128)(2,1)}, f32[2,12,8,576]{3,2,1,0:T(8,128)}) custom-call(bf16[3,768,288]{2,1,0:T(8,128)(2,1)} %get-tuple-element.105.dproj, bf16[192,1152]{1,0:T(8,128)(2,1)} %dynamic-slice_bitcast_fusion.1.x, f32[192,1152]{1,0:T(8,128)} %get-tuple-element.106.dx1, f32[192,8]{1,0:T(8,128)} %fusion.6.sel, ...), custom_call_target="tpu_custom_call" | custom-call | tf_op jit(solution)/shard_map/pallas_call | solution.py:593
  473.2 35.4 %shard_map.244 = (f32[288,1728]{1,0:T(8,128)}, f32[3,1,576]{2,1,0:T(1,128)}, f32[2,8,1152]{2,1,0:T(8,128)}, f32[8,288]{1,0:T(8,128)}) custom-call(f32[2,12,8,576]{3,2,1,0:T(8,128)} %get-tuple-element.110.dmod, f32[2,8,288]{2,1,0:T(8,128)} %pad.10.dgain, f32[8,8,288]{2,1,0:T(8,128)} %bitcast.104, bf16[1728,1152]{1,0:T(8,128)(2,1)} %bitcast.95), custom_call_target="tpu_custom_call" | custom-call | tf_op jit(solution)/shard_map/pallas_call | solution.py:593
  514.3 2.1 collective-permute-start.4
  522.9 1.8 reduce-scatter.11.cloned.1.call-done
  524.7 56.1 %reduce-scatter.9.cloned.1.call-done = bf16[1,144,2304]{2,1,0:T(8,128)(2,1)} async-done(((bf16[4,144,2304]{2,1,0:T(8,128)(2,1)}), bf16[1,144,2304]{2,1,0:T(8,128)(2,1)}) %reduce-scatter.9.cloned.1.call-update) | async-done | bytes 663568 | tf_op jit(solution)/shard_map/reduce_scatter | solution.py:760
  580.8 2.2 select_bitcast_fusion.1
  (123 shorter events, 46.0 us)
Async XLA Ops:
  7.2 36.9 %copy-start = (bf16[2,192,1152]{2,1,0:T(8,128)(2,1)S(1)}, bf16[2,192,1152]{2,1,0:T(8,128)(2,1)}, u32[]{:S(2)}) copy-start(bf16[2,192,1152]{2,1,0:T(8,128)(2,1)} %param.16) | copy-start | bytes 2654212
  7.2 514.4 %reduce-scatter.7.cloned.1.call-start = ((), (), s32[]{:S(2)}) async-start(), calls=%async_computation.5 | async-start | bytes 1658880 | tf_op jit(solution)/shard_map/reduce_scatter | solution.py:760
  7.2 76.7 %collective-permute-start.2 = (bf16[2,1152,768]{2,1,0:T(8,128)(2,1)}, bf16[2,1152,768]{2,1,0:T(8,128)(2,1)}, u32[]{:S(2)}, u32[]{:S(2)}) collective-permute-start(bf16[2,1152,768]{2,1,0:T(8,128)(2,1)} %bitcast.79), channel_id=1, source_target_pairs={{0,16},{16,0},{1,17},{17,1},{2,18},{18,2},{3,19},{19,3},{4,20},{20... | collective-permute-start | bytes 10616840 | tf_op jit(solution)/shard_map/ppermute | solution.py:728
  7.3 40.9 %collective-permute-start = (bf16[3,288,1152]{2,1,0:T(8,128)(2,1)}, bf16[3,288,1152]{2,1,0:T(8,128)(2,1)S(1)}, u32[]{:S(2)}, u32[]{:S(2)}) collective-permute-start(bf16[3,288,1152]{2,1,0:T(8,128)(2,1)} %bitcast.84), channel_id=1, source_target_pairs={{0,16},{16,0},{1,17},{17,1},{2,18},{18,2},{3,19},{19,3},{4,20},{20... | collective-permute-start | bytes 5971976 | tf_op jit(solution)/shard_map/ppermute | solution.py:728
  7.8 76.2 %collective-permute-start.3 = (bf16[768,1152]{1,0:T(8,128)(2,1)}, bf16[768,1152]{1,0:T(8,128)(2,1)}, u32[]{:S(2)}, u32[]{:S(2)}) collective-permute-start(bf16[768,1152]{1,0:T(8,128)(2,1)} %bitcast.89), channel_id=1, source_target_pairs={{0,16},{16,0},{1,17},{17,1},{2,18},{18,2},{3,19},{19,3},{4,20},{20... | collective-permute-start | bytes 5308424 | tf_op jit(solution)/shard_map/ppermute | solution.py:728
  7.9 76.1 %collective-permute-start.1 = (bf16[288,1152]{1,0:T(8,128)(2,1)}, bf16[288,1152]{1,0:T(8,128)(2,1)S(1)}, u32[]{:S(2)}, u32[]{:S(2)}) collective-permute-start(bf16[288,1152]{1,0:T(8,128)(2,1)} %bitcast.96), channel_id=1, source_target_pairs={{0,16},{16,0},{1,17},{17,1},{2,18},{18,2},{3,19},{19,3},{4,20},{20... | collective-permute-start | bytes 1990664 | tf_op jit(solution)/shard_map/ppermute | solution.py:728
  8.3 3.4 copy-start.13
  17.0 5.9 copy-start.17
  17.7 5.2 copy-start.21
  27.7 15.7 %copy-start.18 = (s32[3]{0:T(128)S(1)}, s32[3]{0:T(128)}, u32[]{:S(2)}) copy-start(s32[3]{0:T(128)} %copy-done.17) | copy-start | bytes 40
  27.7 15.7 %copy-start.20 = (s32[3,1]{0,1:T(1,128)S(1)}, s32[3,1]{0,1:T(1,128)}, u32[]{:S(2)}) copy-start(s32[3,1]{0,1:T(1,128)} %reduce-window.9) | copy-start | bytes 40
  43.4 4.0 copy-start.9
  293.1 14.8 %collective-permute-start.7 = (bf16[4,144,1152]{2,1,0:T(8,128)(2,1)}, bf16[4,144,1152]{2,1,0:T(8,128)(2,1)S(1)}, u32[]{:S(2)}, u32[]{:S(2)}) collective-permute-start(bf16[4,144,1152]{2,1,0:T(8,128)(2,1)} %get-tuple-element.118), channel_id=1, source_target_pairs={{0,16},{16,0},{1,17},{17,1},{2,18},{18,2},{3,19},{19,3},{4,20},{20... | collective-permute-start | bytes 3981320 | tf_op jit(solution)/shard_map/ppermute | solution.py:728
  310.7 211.0 %reduce-scatter.5.cloned.1.call-start = ((), (), s32[]{:S(2)}) async-start(), calls=%async_computation.4 | async-start | bytes 1658880 | tf_op jit(solution)/shard_map/reduce_scatter | solution.py:760
  419.6 7.8 %collective-permute-start.6 = (bf16[4,144,1152]{2,1,0:T(8,128)(2,1)}, bf16[4,144,1152]{2,1,0:T(8,128)(2,1)S(1)}, u32[]{:S(2)}, u32[]{:S(2)}) collective-permute-start(bf16[4,144,1152]{2,1,0:T(8,128)(2,1)} %get-tuple-element.116), channel_id=1, source_target_pairs={{0,16},{16,0},{1,17},{17,1},{2,18},{18,2},{3,19},{19,3},{4,20},{20... | collective-permute-start | bytes 3981320 | tf_op jit(solution)/shard_map/ppermute | solution.py:728
  424.5 6.8 %collective-permute-start.10 = (bf16[4,144,2304]{2,1,0:T(8,128)(2,1)}, bf16[4,144,2304]{2,1,0:T(8,128)(2,1)}, u32[]{:S(2)}, u32[]{:S(2)}) collective-permute-start(bf16[4,144,2304]{2,1,0:T(8,128)(2,1)} %get-tuple-element.122), channel_id=1, source_target_pairs={{0,16},{16,0},{1,17},{17,1},{2,18},{18,2},{3,19},{19,3},{4,20},{20... | collective-permute-start | bytes 7962632 | tf_op jit(solution)/shard_map/ppermute | solution.py:728
  427.4 3.9 copy-start.5
  430.3 94.4 %reduce-scatter.11.cloned.1.call-start = ((), (), s32[]{:S(2)}) async-start(), calls=%async_computation.7 | async-start | bytes 3317760 | tf_op jit(solution)/shard_map/reduce_scatter | solution.py:760
  435.2 5.5 copy-start.6
  435.2 145.6 %reduce-scatter.9.cloned.1.call-start = ((), (), s32[]{:S(2)}) async-start(), calls=%async_computation.6 | async-start | bytes 3317760 | tf_op jit(solution)/shard_map/reduce_scatter | solution.py:760
  435.4 5.2 collective-permute-start.9
  445.4 23.8 %copy-start.8 = (bf16[192,1152]{1,0:T(8,128)(2,1)S(1)}, bf16[192,1152]{1,0:T(8,128)(2,1)}, u32[]{:S(2)}) copy-start(bf16[192,1152]{1,0:T(8,128)(2,1)} %get-tuple-element.94.dy) | copy-start | bytes 1327108
  469.1 2.6 copy-start.4
  469.1 2.6 copy-start.10
  469.2 3.4 copy-start.16
  469.2 3.4 copy-start.15
  470.7 49.6 %collective-permute-start.5 = (f32[192,1152]{1,0:T(8,128)S(1)}, f32[192,1152]{1,0:T(8,128)S(1)}, u32[]{:S(2)}, u32[]{:S(2)}) collective-permute-start(f32[192,1152]{1,0:T(8,128)S(1)} %get-tuple-element.192), channel_id=1, source_target_pairs={{0,16},{16,0},{1,17},{17,1},{2,18},{18,2},{3,19},{19,3},{4,20},{20... | collective-permute-start | bytes 2654216 | tf_op jit(solution)/shard_map/ppermute | solution.py:728
  473.2 41.1 %copy-start.11 = (bf16[192,1152]{1,0:T(8,128)(2,1)S(1)}, bf16[192,1152]{1,0:T(8,128)(2,1)}, u32[]{:S(2)}) copy-start(bf16[192,1152]{1,0:T(8,128)(2,1)} %get-tuple-element.194) | copy-start | bytes 1327108
  514.3 4.9 collective-permute-start.4
  522.8 61.3 %collective-permute-start.8 = (bf16[144,1152]{1,0:T(8,128)(2,1)S(1)}, bf16[144,1152]{1,0:T(8,128)(2,1)S(1)}, u32[]{:S(2)}, u32[]{:S(2)}) collective-permute-start(bf16[144,1152]{1,0:T(8,128)(2,1)S(1)} %get-tuple-element.196), channel_id=1, source_target_pairs={{0,16},{16,0},{1,17},{17,1},{2,18},{18,2},{3,19},{19,3},{4,20},{20... | collective-permute-start | bytes 995336 | tf_op jit(solution)/shard_map/ppermute | solution.py:728
  583.0 3.7 collective-permute-start.11
  588.1 2.2 copy-start.7
  (6 other events, 9.4 us)
Sparse Core Ops, SparseCore 0:
  310.8 31.6 reduce-scatter.6
  430.4 31.8 reduce-scatter.4
  464.6 60.0 reduce-scatter.10
  526.9 53.9 reduce-scatter.8

commit v2 on v1

--- a/solution.py
+++ b/solution.py
@@ -8,12 +8,13 @@
 from jax.experimental.pallas import tpu as pltpu
 from jax.sharding import PartitionSpec as P
 
+
 EPS = 1e-06
-PRECISE = lax.Precision.HIGHEST
 F32 = jnp.float32
 BF = jnp.bfloat16
 S, DP, T = "section", "dp", "tensor"
 PAD = 128
+LANES = 384
 TILE = 256
 
 
@@ -55,13 +56,17 @@
     return me, near, 3 - me, (me + 2) % 4
 
 
-def greet(place):
+def greet(place, partner=False):
     sem = pltpu.get_barrier_semaphore()
     for peer in (place[1], place[2]):
         pl.semaphore_signal(
             sem, inc=1, device_id={T: peer}, device_id_type=pl.DeviceIdType.MESH
         )
-    pl.semaphore_wait(sem, 2)
+    if partner:
+        pl.semaphore_signal(
+            sem, inc=1, device_id={S: 1 - lax.axis_index(S)}, device_id_type=pl.DeviceIdType.MESH
+        )
+    pl.semaphore_wait(sem, 3 if partner else 2)
 
 
 def remote(src, dst, sems, index, peer):
@@ -211,30 +216,47 @@
     dmod[2 * block + 1] += sums[:, half:]
 
 
-def weight_grad(x, y, flipped, col, mine, theirs):
+def weight_grad(x, y, flipped, col, packs, index):
+    mine, theirs, _ = packs
     dp, part, _ = mine.shape
-    section = lax.axis_index(S)
+    first = lax.axis_index(S) == 0
     width = y.shape[1]
     block = 256 if width % 256 == 0 else width
     if x is not None:
         flipped[...] = x[...].T
-
-    def one(at, to):
-        grad = nn(flipped[...], y[:, at]).astype(BF).reshape(dp, 2, part, -1)
-        first = section == 0
-
-        for target, half in ((mine, 0), (theirs, 1)):
-
-            @pl.when(first)
-            def _(target=target, half=half):
-                target[:, :, to] = grad[:, half]
-
-            @pl.when(jnp.logical_not(first))
-            def _(target=target, half=half):
-                target[:, :, to] = grad[:, 1 - half]
-
     for i in range(width // block):
-        one(pl.ds(i * block, block), pl.ds(col + i * block, block))
+        to = pl.ds(col + i * block, block)
+        grad = nn(flipped[...], y[:, pl.ds(i * block, block)]).astype(BF)
+        grad = grad.reshape(dp, 2, part, block)
+
+        @pl.when(first)
+        def _():
+            mine[:, :, to] = grad[:, 0]
+            theirs[:, :, to] = grad[:, 1]
+
+        @pl.when(jnp.logical_not(first))
+        def _():
+            mine[:, :, to] = grad[:, 1]
+            theirs[:, :, to] = grad[:, 0]
+
+    return index, col, width
+
+
+def send_half(packs, sems, job):
+    index, col, width = job
+    at = pl.ds(col, width)
+    return push(
+        packs[1].at[:, :, at], packs[2].at[:, :, at], sems, index, {S: 1 - lax.axis_index(S)}
+    )
+
+
+def add_halves(packs, copies, total):
+    for copy in copies:
+        copy.wait_recv()
+    for k in range(total.shape[0]):
+        total[k] = (packs[0][k].astype(F32) + packs[2][k].astype(F32)).astype(BF)
+    for copy in copies:
+        copy.wait_send()
 
 
 def item_sums(sel, values):
@@ -255,7 +277,6 @@
 
 def qkv_kernel(layer, square, x, sel, mod, w_own, w_other, whole, proj, h, w, ssem, rsem, wsem):
     place = ring(square)
-    width = x.shape[1]
     load = layer_weights(w_own, w_other, layer, w, wsem)
     greet(place)
 
@@ -283,7 +304,7 @@
                gate, up, hidden, br2, y, h, wo, wg, wd, o1, i1, k1, s1, o2, i2, k2, s2,
                ssem, rsem, wsem):
     place = ring(square)
-    rows_here, width = x.shape
+    rows_here, _ = x.shape
     load_o = layer_weights(wo0, wo1, layer, wo, wsem.at[0])
     load_g = layer_weights(wg0, wg1, layer, wg, wsem.at[1])
     load_d = layer_weights(wd0, wd1, layer, wd, wsem.at[2])
@@ -327,11 +348,11 @@
 
 
 def mlp_back_kernel(layer, square, dy, br2, br1, x1, sel, mod, gate_h, up_h, hidden_h, rows_h,
-                    wo0, wo1, wg0, wg1, wd0, wd1, whole1, datt, dx1, dmod, mine, theirs, h, h1,
-                    whole2, dgate, dup, gate, up, hidden, saved, flipped, wo, wg, wd, o1, i1, k1,
+                    wo0, wo1, wg0, wg1, wd0, wd1, whole1, datt, dx1, dmod, total, mine, theirs,
+                    got, h, h1, whole2, dgate, dup, gate, up, hidden, saved, flipped, wo, wg, wd, o1, i1, k1,
                     s1, ssem, rsem, wsem):
     place = ring(square)
-    rows_here, width = dy.shape
+    rows_here, _ = dy.shape
     load_d = layer_weights(wd0, wd1, layer, wd, wsem.at[0])
     load_gate = pltpu.make_async_copy(gate_h, gate, wsem.at[1])
     load_gate.start()
@@ -343,7 +364,7 @@
     load_hidden.start()
     load_rows = pltpu.make_async_copy(rows_h, saved, wsem.at[6])
     load_rows.start()
-    greet(place)
+    greet(place, True)
     sems = (ssem, rsem)
     dmod[...] = jnp.zeros_like(dmod)
 
@@ -378,8 +399,15 @@
         rows = chunk_rows(chunk, rows_here)
         return nt(dgate[rows], wg[0]) + nt(dup[rows], wg[1])
 
+    packs = (mine, theirs, got)
+    copies = []
+
+    def grad(index, x, y, col):
+        job = weight_grad(x, y, flipped, col, packs, index)
+        copies.append(send_half(packs, sems, job))
+
     def grad_down():
-        weight_grad(whole2, hidden, flipped, 2 * f, mine, theirs)
+        grad(18, whole2, hidden, 2 * f)
 
     scatter(place, term, bufs, sems, 6, (grad_down,))
 
@@ -403,44 +431,66 @@
         datt[rows] = nt(whole1[rows], wo[...]).astype(BF)
 
     def grad_gate():
-        weight_grad(saved, dgate, flipped, 0, mine, theirs)
+        grad(19, saved, dgate, 0)
 
     def grad_up():
-        weight_grad(None, dup, flipped, f, mine, theirs)
+        grad(20, None, dup, f)
 
     gather(place, h1, whole1, sems, 12, use_out, (grad_gate, grad_up))
-
-
-def qkv_back_kernel(layer, square, dproj, x, dx1, sel, mod, part, prev, w_own, w_other, du, du_b,
-                    dmod, w, o1, i1, k1, s1, ssem, rsem, wsem):
+    add_halves(packs, copies, total)
+
+
+def qkv_back_kernel(layer, square, dproj, x, dx1, sel, mod, part, prev, w_own, w_other, whole_h,
+                    att_h, rows1_h, du, du_b, dmod, total, w, whole, att, rows1, flipped, mine,
+                    theirs, got, o1, i1, k1, s1, ssem, rsem, wsem):
     place = ring(square)
-    rows_here, width = x.shape
-    load = layer_weights(w_own, w_other, layer, w, wsem)
-    greet(place)
+    rows_here, _ = x.shape
+    load = layer_weights(w_own, w_other, layer, w, wsem.at[0])
+    loads = []
+    for n, (src, dst) in enumerate(((whole_h, whole), (att_h, att), (rows1_h, rows1))):
+        loads.append(pltpu.make_async_copy(src, dst, wsem.at[1 + n]))
+        loads[n].start()
+    greet(place, True)
     here = dmod.at[layer]
     dmod[1 - layer] = prev[...]
     here[pl.ds(0, 4)] = jnp.zeros_like(prev[pl.ds(0, 4)])
     here[pl.ds(4, 8)] = part[...]
     load.wait()
     bufs = (o1, i1, k1, s1)
+    sems = (ssem, rsem)
+    packs = (mine, theirs, got)
+    packed = att.shape[1]
+    copies = []
 
     def term(chunk):
         rows = chunk_rows(chunk, rows_here)
         return nn(dproj[0, rows], w[0]) + nn(dproj[1, rows], w[1]) + nn(dproj[2, rows], w[2])
 
-    scatter(place, term, bufs, (ssem, rsem), 0)
+    def grad_in():
+        loads[0].wait()
+        for k in range(3):
+            weight_grad(None if k else whole, dproj.at[k], flipped, k * packed, packs, 6)
+
+    def grad_out():
+        loads[1].wait()
+        loads[2].wait()
+        weight_grad(rows1, att, flipped, 3 * packed, packs, 6)
+        copies.append(send_half(packs, sems, (6, 0, 4 * packed)))
+
+    scatter(place, term, bufs, sems, 0, (grad_in, grad_out))
 
     def finish(rows):
         d_h = scattered(bufs, rows)
         normal, inverse = normed(x[rows].astype(F32))
         scale = mod_rows(sel[rows], mod, 1)
-        total = dx1[rows] + norm_back(d_h * (1.0 + scale), normal, inverse)
-        du[rows] = total
-        du_b[rows] = total.astype(BF)
+        total_rows = dx1[rows] + norm_back(d_h * (1.0 + scale), normal, inverse)
+        du[rows] = total_rows
+        du_b[rows] = total_rows.astype(BF)
         add_sums(here, 0, sel[rows], d_h)
         add_sums(here, 1, sel[rows], d_h * normal)
 
     over_blocks(rows_here, finish)
+    add_halves(packs, copies, total)
 
 
 def cell():
@@ -478,13 +528,15 @@
     return copy
 
 
-def head_kernel(dp, lifted, ada_h, bias, mod, lifted_all, ada, parts, got, ssem, rsem, wsem):
+def head_kernel(dp, lifted, ada_h, bias, gain, items, pos, tables, mod, lifted_all, gains, sel,
+                both, spans, ada, parts, got, wide, tall, ssem, rsem, wsem):
     load = pltpu.make_async_copy(ada_h, ada, wsem)
     load.start()
     greet_all(dp)
     sems = (ssem, rsem)
-    here, shard = cell(), lax.axis_index(DP)
-    copies = []
+    here, shard, section = cell(), lax.axis_index(DP), lax.axis_index(S)
+    copies = [push(gain, gains.at[section], sems, 6 + dp, {S: 1 - section})]
+    gains[section] = gain[...]
     lifted_all[shard] = lifted[...]
     for k in range(1, dp):
         copies.append(
@@ -499,7 +551,31 @@
     for k in range(1, 8):
         peer = (here + k) % 8
         copies.append(push(parts.at[peer // 4], got.at[here], sems, k - 1, cell_id(peer)))
-    got[here] = parts[lax.axis_index(S)]
+    got[here] = parts[section]
+    rows_here = sel.shape[0]
+    base = shard * 6 + section * 3
+    seq = items.shape[1]
+    line = items[pl.ds(section, 1), :]
+    wide[...] = jnp.zeros_like(wide)
+    wide[0:1] = (line - base).astype(F32)
+    wide[1:2] = pos[0, pl.ds(section, 1), :].astype(F32)
+    wide[2:3] = pos[1, pl.ds(section, 1), :].astype(F32)
+    start = 0
+    spans[0] = 0
+    for j in range(3):
+        count = jnp.sum((wide[0:1] == j).astype(F32)).astype(jnp.int32)
+        spans[4 + j] = count
+        start = start + count
+        spans[1 + j] = start
+    spans[7] = 0
+    tall[...] = wide[...].T
+    own = tall[pl.ds(pl.multiple_of(lax.axis_index(T) * rows_here, rows_here), rows_here), :]
+    lane = lax.broadcasted_iota(jnp.int32, (rows_here, 8), 1).astype(F32)
+    sel[...] = ((own[:, 0:1] == lane) & (lane < 3.0)).astype(F32)
+    lane = lax.broadcasted_iota(jnp.int32, (seq, 64), 1).astype(F32)
+    hot = jnp.where(lane < 32.0, tall[:, 1:2], tall[:, 2:3] + 32.0) == lane
+    hot = hot.astype(F32).astype(BF)
+    both[...] = (nn(hot, tables[0]) + nn(hot, tables[1])) + nn(hot, tables[2])
     for copy in copies:
         copy.wait_recv()
     for layer in range(2):
@@ -589,30 +665,40 @@
         copy.wait_send()
 
 
-def ring_call(kernel, ident, outs, scratch, args, spaces):
+def price(micros):
+    return pl.CostEstimate(flops=0, bytes_accessed=int(micros * 3.5e6), transcendentals=0)
+
+
+def ring_call(kernel, ident, micros, outs, scratch, args, spaces, scalar=-1):
     return pl.pallas_call(
         kernel,
         out_shape=outs,
         in_specs=[vmem() if s else anywhere() for s in spaces],
-        out_specs=[vmem()] * len(outs),
+        out_specs=[
+            pl.BlockSpec(memory_space=pltpu.SMEM) if n == scalar else vmem()
+            for n in range(len(outs))
+        ],
         scratch_shapes=scratch,
         compiler_params=pltpu.CompilerParams(
             collective_id=ident, has_side_effects=True, vmem_limit_bytes=60 * 2**20
         ),
+        cost_estimate=price(micros),
     )(*args)
 
 
-def attention_kernel(spans, proj, gain, cosine, sine, turn, spread, ones, q, k, v, att, padded):
+def attention_kernel(spans, proj, gain, both, turn, spread, ones, q, k, v, att, padded):
     heads = spread.shape[1] // PAD
-    head = proj.shape[2] // heads
+    packed = proj.shape[2]
+    head = packed // heads
     scale = head ** (-0.5)
     rows = proj.shape[1]
 
     def units(at):
         for which, dst in ((0, q), (1, k)):
             normal, _ = unit(proj[which, at], ones[...], head)
-            gained = normal * gain[which]
-            turned = gained * cosine[at] + two(nn, gained, turn[...]) * sine[at]
+            gained = normal * gain[which : which + 1]
+            turned = gained * both[at, 0:packed]
+            turned = turned + two(nn, gained, turn[...]) * both[at, LANES : LANES + packed]
             dst[at] = nn(turned.astype(BF), spread[...]).astype(BF)
         v[at] = nn(proj[2, at].astype(BF), spread[...]).astype(BF)
 
@@ -660,8 +746,8 @@
     return tn(d_scores, key) * scale, nn(d_scores, query) * scale, d_value
 
 
-def attention_back_kernel(spans, q, k, v, datt, proj, gain, whole, att, rows1, cosine, sine, turn,
-                          spread, ones, dproj, dgain, mine, theirs, grad, dq, dk, dv, flipped):
+def attention_back_kernel(spans, q, k, v, datt, proj, gain, both, turn, spread, ones, dproj,
+                          dgain, grad, dq, dk, dv):
     heads = spread.shape[1] // PAD
     rows, packed = datt.shape
     head = packed // heads
@@ -697,23 +783,19 @@
     def finish(at):
         for which, src in ((0, dq), (1, dk)):
             flat = two(nt, src[at], spread[...])
-            back = flat * cosine[at] - two(nn, flat, turn[...]) * sine[at]
+            back = flat * both[at, 0:packed]
+            back = back - two(nn, flat, turn[...]) * both[at, LANES : LANES + packed]
             normal, inverse = unit(proj[which, at], ones[...], head)
             dgain[which] += jnp.sum(back * normal, axis=0, keepdims=True)
-            gained = back * gain[which]
+            gained = back * gain[which : which + 1]
             mean = two(nn, gained * normal, ones[...]) * (1.0 / head)
             dproj[which, at] = (inverse * (gained - normal * mean)).astype(BF)
         dproj[2, at] = nt(dv[at].astype(BF), spread[...]).astype(BF)
 
     over_blocks(rows, finish)
-    for which in range(3):
-        weight_grad(
-            None if which else whole, dproj.at[which], flipped, which * packed, mine, theirs
-        )
-    weight_grad(rows1, att, flipped, 3 * packed, mine, theirs)
-
-
-def local_call(kernel, outs, scratch, spans, args):
+
+
+def local_call(kernel, micros, outs, scratch, spans, args):
     return pl.pallas_call(
         kernel,
         out_shape=outs,
@@ -721,6 +803,7 @@
         out_specs=[vmem()] * len(outs),
         scratch_shapes=scratch,
         compiler_params=pltpu.CompilerParams(vmem_limit_bytes=60 * 2**20),
+        cost_estimate=price(micros),
     )(spans, *args)
 
 
@@ -728,20 +811,22 @@
     return lax.ppermute(array, S, [(0, 1), (1, 0)])
 
 
-def head_tables(positions, packed, head):
+def head_tables(packed, head):
     quarter = head // 4
     frequency = np.float32(10000.0) ** (-np.arange(quarter, dtype=np.float32) / quarter)
     lane = np.arange(packed) % head
     angle = np.arange(32, dtype=np.float32)[:, None] * frequency[lane % quarter][None, :]
     by_row = (lane // (2 * quarter) == 0)[None, :]
-    table = np.concatenate([np.where(by_row, t, 0.0) for t in (np.cos(angle), np.sin(angle))], axis=1)
-    other = np.concatenate([np.where(by_row, 0.0, t) for t in (np.cos(angle), np.sin(angle))], axis=1)
-    table = jnp.asarray(np.concatenate([table, other]).astype(np.float32))
-    slots = jnp.arange(32)[None, :]
-    hot = jnp.concatenate(
-        [positions[0][:, None] == slots, positions[1][:, None] == slots], axis=1
-    ).astype(F32)
-    both = jnp.dot(hot, table, precision=PRECISE)
+    table = np.zeros((64, 2 * LANES), np.float32)
+    for n, values in enumerate((np.cos(angle), np.sin(angle))):
+        at = slice(n * LANES, n * LANES + packed)
+        table[:32, at] = np.where(by_row, values, 0.0)
+        table[32:, at] = np.where(by_row, 0.0, values)
+    table = jnp.asarray(table)
+    parts = []
+    for _ in range(3):
+        parts.append(lax.reduce_precision(table, 8, 7).astype(BF))
+        table = table - parts[-1].astype(F32)
     rows = np.arange(packed)[:, None]
     cols = np.arange(packed)[None, :]
     early = (cols % (2 * quarter)) < quarter
@@ -752,11 +837,10 @@
     spread = (rows // head == wide // PAD) & (rows % head == wide % PAD)
     ones = rows // head == cols // head
     lanes = tuple(jnp.asarray(m.astype(np.float32)).astype(BF) for m in (turn, spread, ones))
-    return (both[:, :packed], both[:, packed:]) + lanes
-
-
-def reduced(mine, theirs):
-    total = (mine.astype(F32) + swap(theirs).astype(F32)).astype(BF)
+    return jnp.stack(parts), lanes
+
+
+def reduced(total):
     return lax.psum_scatter(total, DP, scatter_dimension=0, tiled=True)[0]
 
 
@@ -789,36 +873,39 @@
     ada = ada_weight[0].T
     half = width // 2
     bias = ada_bias.astype(F32).reshape(3, 1, half)
-    mods, lifted_all = ring_call(
+    gain = jnp.tile(qk_gain[0].astype(F32), (1, heads))
+    gain = jnp.pad(gain, ((0, 6), (0, 0)))
+    trig, lanes = head_tables(packed, head)
+    mods, lifted_all, gains, sel, both, spans = ring_call(
         functools.partial(head_kernel, dp),
         8,
-        [sds((2, 6, 8, width), F32), sds((dp, 16, width), F32)],
+        12,
+        [
+            sds((2, 6, 8, width), F32),
+            sds((dp, 16, width), F32),
+            sds((2, 8, packed), F32),
+            sds((rows, 8), F32),
+            sds((seq, 2 * LANES), F32),
+            sds((8,), jnp.int32),
+        ],
         [
             pltpu.VMEM((3 * half, width), BF),
             pltpu.VMEM((2, 3, 8, half), F32),
             pltpu.VMEM((8, 3, 8, half), F32),
+            pltpu.VMEM((8, seq), F32),
+            pltpu.VMEM((seq, 8), F32),
         ]
-        + dma_sems(6 + dp)
+        + dma_sems(7 + dp)
         + [pltpu.SemaphoreType.DMA],
-        (lifted, ada, bias),
-        (1, 0, 1),
+        (lifted, ada, bias, gain, patch_item, patch_pos, trig),
+        (1, 0, 1, 1, 1, 1, 1),
+        scalar=5,
     )
-    gains = lax.all_gather(qk_gain[0], S).astype(F32)
-    gains = jnp.tile(gains, (1, 1, heads)).reshape(2, 2, 1, packed)
+    tables = (both,) + lanes
     part = width // dp
     shard = lax.axis_index(DP)
     lifted_part = lax.dynamic_slice_in_dim(lifted_all, shard * part, part, 2)
     lifted_part = lifted_part.reshape(2 * dp, 8, part)
-
-    ids = lax.dynamic_index_in_dim(patch_item, section, 0, keepdims=False)
-    ids = jnp.where(ids >= 0, ids - lax.axis_index(DP) * items - section * per_micro, -1)
-    counts = jnp.sum((ids[None, :] == jnp.arange(3)[:, None]).astype(jnp.int32), axis=1)
-    starts = jnp.concatenate([jnp.zeros((1,), jnp.int32), jnp.cumsum(counts)]).astype(jnp.int32)
-    spans = jnp.concatenate([starts, counts, jnp.zeros((1,), jnp.int32)])
-    local_ids = lax.dynamic_slice_in_dim(ids, lax.axis_index(T) * rows, rows)
-    sel = (local_ids[:, None] == jnp.arange(8)[None, :]).astype(F32)
-    positions = lax.dynamic_index_in_dim(patch_pos, section, 1, keepdims=False)
-    tables = head_tables(positions, packed, head)
 
     x = lax.dynamic_index_in_dim(tokens, section, 0, keepdims=False)
     kept = []
@@ -827,6 +914,7 @@
         whole1, proj = ring_call(
             functools.partial(qkv_kernel, layer, square),
             layer,
+            20,
             [sds((seq, width), BF), sds((3, seq, packed), F32)],
             [pltpu.VMEM((rows, width), BF), pltpu.VMEM((3, packed, width), BF)]
             + dma_sems(6)
@@ -836,6 +924,7 @@
         )
         q, k, v, att = local_call(
             attention_kernel,
+            12,
             [sds((seq, heads * PAD), BF)] * 3 + [sds((seq, packed), BF)],
             [pltpu.VMEM((seq, heads * PAD), BF)],
             spans,
@@ -844,6 +933,7 @@
         br1, x1, whole2, gate, up, hidden, br2, y = ring_call(
             functools.partial(mlp_kernel, layer, square),
             2 + layer,
+            48,
             [
                 sds((rows, width), F32),
                 sds((rows, width), F32),
@@ -878,18 +968,19 @@
     for layer in (1, 0):
         x, whole1, proj, q, k, v, att, br1, x1, whole2, gate, up, hidden, br2, y = kept[layer]
         mod = mods[layer]
-        rows1, datt, dx1, dmod_a, mine, theirs = ring_call(
+        rows1, datt, dx1, dmod_a, total_mlp = ring_call(
             functools.partial(mlp_back_kernel, layer, square),
             4 + layer,
+            52,
             [
                 sds((seq, width), BF),
                 sds((seq, packed), BF),
                 sds((rows, width), F32),
                 sds((8, 8, half), F32),
                 sds((dp, part // 2, 3 * hidden_here), BF),
-                sds((dp, part // 2, 3 * hidden_here), BF),
             ],
-            [
+            [pltpu.VMEM((dp, part // 2, 3 * hidden_here), BF)] * 3
+            + [
                 pltpu.VMEM((rows, width), BF),
                 pltpu.VMEM((rows, width), BF),
                 pltpu.VMEM((seq, width), BF),
@@ -905,40 +996,50 @@
                 pltpu.VMEM((hidden_here, width), BF),
             ]
             + scatter_scratch(rows, width)
-            + dma_sems(18)
+            + dma_sems(21)
             + [pltpu.SemaphoreType.DMA((7,))],
             (dy, br2, br1, x1, sel, mod, gate, up, hidden, whole2, own[1], other[1], own[2],
              other[2], own[3], other[3]),
             (1,) * 6 + (0,) * 10,
         )
-        pack_mlp = reduced(mine, theirs)
-        dproj, dgain, mine, theirs = local_call(
+        pack_mlp = reduced(total_mlp)
+        dproj, dgain = local_call(
             attention_back_kernel,
+            28,
             [
                 sds((3, seq, packed), BF),
                 sds((2, 1, packed), F32),
-                sds((dp, part // 2, 4 * packed), BF),
+            ],
+            [pltpu.VMEM((seq, heads * PAD), BF)] + [pltpu.VMEM((seq, heads * PAD), F32)] * 3,
+            spans,
+            (q, k, v, datt, proj, gains[layer]) + tables,
+        )
+        du, du_b, d_mod, total_att = ring_call(
+            functools.partial(qkv_back_kernel, layer, square),
+            6 + layer,
+            22,
+            [
+                sds((rows, width), F32),
+                sds((rows, width), BF),
+                sds((2, 12, 8, half), F32),
                 sds((dp, part // 2, 4 * packed), BF),
             ],
-            [pltpu.VMEM((seq, heads * PAD), BF)]
-            + [pltpu.VMEM((seq, heads * PAD), F32)] * 3
-            + [pltpu.VMEM((width, seq), BF)],
-            spans,
-            (q, k, v, datt, proj, gains[layer], whole1, att, rows1) + tables,
-        )
-        pack_att = reduced(mine, theirs)
-        du, du_b, d_mod = ring_call(
-            functools.partial(qkv_back_kernel, layer, square),
-            6 + layer,
-            [sds((rows, width), F32), sds((rows, width), BF), sds((2, 12, 8, half), F32)],
-            [pltpu.VMEM((3, packed, width), BF)]
+            [
+                pltpu.VMEM((3, packed, width), BF),
+                pltpu.VMEM((seq, width), BF),
+                pltpu.VMEM((seq, packed), BF),
+                pltpu.VMEM((seq, width), BF),
+                pltpu.VMEM((width, seq), BF),
+            ]
+            + [pltpu.VMEM((dp, part // 2, 4 * packed), BF)] * 3
             + scatter_scratch(rows, width)
-            + dma_sems(6)
-            + [pltpu.SemaphoreType.DMA],
-            (dproj, x, dx1, sel, mod, dmod_a, prev, own[0], other[0]),
-            (1,) * 7 + (0,) * 2,
+            + dma_sems(7)
+            + [pltpu.SemaphoreType.DMA((4,))],
+            (dproj, x, dx1, sel, mod, dmod_a, prev, own[0], other[0], whole1, att, rows1),
+            (1,) * 7 + (0,) * 5,
         )
         prev = d_mod[1]
+        pack_att = reduced(total_att)
         packs[layer] = (pack_mlp, pack_att)
         d_gains[layer] = dgain
         d_inputs[layer] = du_b if layer else du
@@ -948,6 +1049,7 @@
     g_ada_w, bias_grad, dl_sum, gain_sum = ring_call(
         functools.partial(tail_kernel, dp),
         9,
+        15,
         [
             sds((part, 3 * half), F32),
             sds((3, 1, half), F32),
@@ -1033,10 +1135,10 @@
         P(S, (T, DP)),
     )
     dp = mesh.shape[DP]
+
+    def program(*args):
+        return per_device(dp <= 4, dp, *args)
+
     return jax.shard_map(
-        functools.partial(per_device, dp <= 4, dp),
-        mesh=mesh,
-        in_specs=in_specs,
-        out_specs=out_specs,
-        check_vma=False,
+        program, mesh=mesh, in_specs=in_specs, out_specs=out_specs, check_vma=False
     )

time: 603 us -> 637 us (1.056)
  waiting for transfers between devices: 69.5 us -> 127 us
  starting transfers between devices: 23 us -> 4.86 us
  Pallas kernels: 426 us -> 441 us
  other arithmetic: 30.2 us -> 17.3 us
  local copies, waits for them, and re-layouts: 30.5 us -> 23.9 us
    reduce_scatter x4, waiting for transfers between devices: 58 us -> 125 us  [reduced(): return lax.psum_scatter(total, DP, scatter_dimension=0, tiled=True)[0]]
    pallas_call x10, Pallas kernels: 340 us -> 371 us  [ring_call(): pl.pallas_call(kernel, out_shape=outs, in_specs=[vmem() if s else anywher...]
    ppermute x12 -> x8, starting transfers between devices: 22.7 us -> 4.45 us  [swap(): return lax.ppermute(array, S, [(0, 1), (1, 0)])]
    pallas_call x4, Pallas kernels: 85.6 us -> 70.2 us  [local_call(): pl.pallas_call(kernel, out_shape=outs, in_specs=[pl.BlockSpec(memory_spac...]
    convert_element_type x6 -> x1, other arithmetic: 12.5 us -> 0.66 us  [per_device(): gain = jnp.tile(qk_gain[0].astype(F32), (1, heads))]
    ppermute x12 -> x8, waiting for transfers between devices: 11.5 us -> 0.02 us  [swap(): return lax.ppermute(array, S, [(0, 1), (1, 0)])]
  transfers between devices with their start and end apart: 16 -> 12, of which waited for: 6 -> 3; matrix products, arithmetic and copies ran while one was open for 9% -> 5% of each run, Pallas kernels for 36% -> 14%
where the time goes in v2:
time: 637 us; the launch traced here: 628 us
  Pallas kernels  441 us (69%)
  waiting for transfers between devices  127 us (20%)
  local copies, waits for them, and re-layouts  23.9 us (4%)
  other arithmetic  17.3 us (3%)
  between operations  14.5 us (2%)
    pallas_call x10, Pallas kernels, ring_call(): pl.pallas_call(kernel, out_shape=outs, in_specs=[vmem() if s else anywher...  371 us
    reduce_scatter x4, waiting for transfers between devices, reduced(): return lax.psum_scatter(total, DP, scatter_dimension=0, tiled=True)[0]  125 us
    pallas_call x4, Pallas kernels, local_call(): pl.pallas_call(kernel, out_shape=outs, in_specs=[pl.BlockSpec(memory_spac...  70.2 us
  transfers between devices with their start and end apart: 12, of which 3 were waited for; matrix products, arithmetic and copies ran while one was open for 5% of the time, Pallas kernels for 14%

profile of v2, /device:TPU:1, one launch (start us, length us, event | category | flops | bytes accessed | tf_op | source)
XLA Modules:
  0.0 628.1 jit_solution(7141912950723892419)
XLA Ops:
  8.3 1.3 fusion.6
  9.7 1.3 reshape.186
  13.8 1.4 bitcast_convert_fusion.lifted
  15.1 16.5 %shard_map.231 = (f32[2,6,8,1152]{3,2,1,0:T(8,128)}, f32[4,16,1152]{2,1,0:T(8,128)}, f32[2,8,288]{2,1,0:T(8,128)}, f32[192,8]{1,0:T(8,128)}, f32[768,768]{1,0:T(8,128)}, /*index=5*/s32[8]{0:T(128)}) custom-call(f32[16,1152]{1,0:T(8,128)} %bitcast_convert_fusion.lifted, bf16[1728,1152]{1,0:T(8,128)(2,1)} %bitcast.92, f32[3,1,576]{2,1,0:T(1,128)} %reshape.199.bias, ...), custom_call_target="tpu_custom_call" | custom-call | bytes 42000000 | tf_op jit(solution)/shard_map/pallas_call | solution.py:673
  32.5 1.8 dynamic-slice_bitcast_fusion.dy
  37.0 21.6 %shard_map.232 = (bf16[768,1152]{1,0:T(8,128)(2,1)}, f32[3,768,288]{2,1,0:T(8,128)}) custom-call(bf16[192,1152]{1,0:T(8,128)(2,1)} %dynamic-slice_bitcast_fusion.1.x, f32[192,8]{1,0:T(8,128)} %get-tuple-element.69.sel, f32[6,8,1152]{2,1,0:T(8,128)} %get-tuple-element.162.mod, bf16[3,288,1152]{2,1,0:T(8,128)(2,1)} %bitcast.83, bf16[3,288,1152]{2,1,0:T(8,128)(2,1)} %copy-done.2), custom_call_target="tpu_custom_call" | custom-call | bytes 70000000 | tf_op jit(solution)/shard_map/pallas_call | solution.py:673
  58.6 13.0 %shard_map.233 = (bf16[768,512]{1,0:T(8,128)(2,1)}, bf16[768,512]{1,0:T(8,128)(2,1)}, bf16[768,512]{1,0:T(8,128)(2,1)}, bf16[768,288]{1,0:T(8,128)(2,1)}) custom-call(s32[8]{0:T(128)} %get-tuple-element.68.spans, f32[3,768,288]{2,1,0:T(8,128)} %get-tuple-element.71.proj, f32[8,288]{1,0:T(8,128)} %get-tuple-element.164.gain, ...), custom_call_target="tpu_custom_call" | custom-call | bytes 42000000 | tf_op jit(solution)/shard_map/pallas_call | solution.py:799
  72.4 50.1 %shard_map.234 = (f32[192,1152]{1,0:T(8,128)}, f32[192,1152]{1,0:T(8,128)}, bf16[768,1152]{1,0:T(8,128)(2,1)}, f32[768,768]{1,0:T(8,128)}, f32[768,768]{1,0:T(8,...) custom-call(bf16[768,288]{1,0:T(8,128)(2,1)} %get-tuple-element.74.att.att_h, ...), custom_call_target="tpu_custom_call" | custom-call | bytes 168000000 | tf_op jit(solution)/shard_map/pallas_call | solution.py:673
  122.6 19.2 %shard_map.235 = (bf16[768,1152]{1,0:T(8,128)(2,1)}, f32[3,768,288]{2,1,0:T(8,128)}) custom-call(bf16[192,1152]{1,0:T(8,128)(2,1)} %get-tuple-element.75.x, f32[192,8]{1,0:T(8,128)} %get-tuple-element.69.sel, f32[6,8,1152]{2,1,0:T(8,128)} %get-tuple-element.161.mod, bf16[3,288,1152]{2,1,0:T(8,128)(2,1)} %bitcast.84, bf16[3,288,1152]{2,1,0:T(8,128)(2,1)} %copy-done.2), custom_call_target="tpu_custom_call" | custom-call | bytes 70000000 | tf_op jit(solution)/shard_map/pallas_call | solution.py:673
  141.7 13.0 %shard_map.236 = (bf16[768,512]{1,0:T(8,128)(2,1)}, bf16[768,512]{1,0:T(8,128)(2,1)}, bf16[768,512]{1,0:T(8,128)(2,1)}, bf16[768,288]{1,0:T(8,128)(2,1)}) custom-call(s32[8]{0:T(128)} %get-tuple-element.68.spans, f32[3,768,288]{2,1,0:T(8,128)} %get-tuple-element.76.proj, f32[8,288]{1,0:T(8,128)} %get-tuple-element.163.gain, ...), custom_call_target="tpu_custom_call" | custom-call | bytes 42000000 | tf_op jit(solution)/shard_map/pallas_call | solution.py:799
  154.7 47.0 %shard_map.237 = (f32[192,1152]{1,0:T(8,128)}, f32[192,1152]{1,0:T(8,128)}, bf16[768,1152]{1,0:T(8,128)(2,1)}, f32[768,768]{1,0:T(8,128)}, f32[768,768]{1,0:T(8,...) custom-call(bf16[768,288]{1,0:T(8,128)(2,1)} %get-tuple-element.77.att.att_h, ...), custom_call_target="tpu_custom_call" | custom-call | bytes 168000000 | tf_op jit(solution)/shard_map/pallas_call | solution.py:673
  201.7 68.4 %shard_map.238 = (bf16[768,1152]{1,0:T(8,128)(2,1)}, bf16[768,288]{1,0:T(8,128)(2,1)}, f32[192,1152]{1,0:T(8,128)}, f32[8,8,576]{2,1,0:T(8,128)}, bf16[4,144,2304]{2,1,0:T(8,128)(2,1)}) custom-call(bf16[192,1152]{1,0:T(8,128)(2,1)} %dynamic-slice_bitcast_fusion.dy, f32[192,1152]{1,0:T(8,128)} %get-tuple-element.85.br2, f32[192,1152]{1,0:T(8,128)} %get-tuple-element.86.br1, ...), custom_call_target="tpu_custom_call" | custom-call | bytes 182000000 | tf_op jit(solution)/shard_map/pallas_call | solution.py:673
  270.1 22.1 %shard_map.239 = (bf16[3,768,288]{2,1,0:T(8,128)(2,1)}, f32[2,1,288]{2,1,0:T(1,128)}) custom-call(s32[8]{0:T(128)} %get-tuple-element.68.spans, bf16[768,512]{1,0:T(8,128)(2,1)} %get-tuple-element.82.q, bf16[768,512]{1,0:T(8,128)(2,1)} %get-tuple-element.83.k, bf16[768,512]{1,0:T(8,128)(2,1)} %get-tuple-element.84.v, ...), custom_call_target="tpu_custom_call" | custom-call | bytes 98000000 | tf_op jit(solution)/shard_map/pallas_call | solution.py:799
  292.9 23.8 %shard_map.240 = (f32[192,1152]{1,0:T(8,128)}, bf16[192,1152]{1,0:T(8,128)(2,1)}, f32[2,12,8,576]{3,2,1,0:T(8,128)}, bf16[4,144,1152]{2,1,0:T(8,128)(2,1)}) custom-call(bf16[3,768,288]{2,1,0:T(8,128)(2,1)} %get-tuple-element.93.dproj, bf16[192,1152]{1,0:T(8,128)(2,1)} %get-tuple-element.75.x, f32[192,1152]{1,0:T(8,128)} %get-tuple-element.94.dx1, ...), custom_call_target="tpu_custom_call" | custom-call | bytes 77000000 | tf_op jit(solution)/shard_map/pallas_call | solution.py:673
  316.7 1.7 slice_bitcast_fusion.7.prev
  318.3 62.6 %shard_map.241 = (bf16[768,1152]{1,0:T(8,128)(2,1)}, bf16[768,288]{1,0:T(8,128)(2,1)}, f32[192,1152]{1,0:T(8,128)}, f32[8,8,576]{2,1,0:T(8,128)}, bf16[4,144,2304]{2,1,0:T(8,128)(2,1)}) custom-call(bf16[192,1152]{1,0:T(8,128)(2,1)} %get-tuple-element.98.dy, f32[192,1152]{1,0:T(8,128)} %get-tuple-element.99.br2, f32[192,1152]{1,0:T(8,128)} %get-tuple-element.100.br1, ...), custom_call_target="tpu_custom_call" | custom-call | bytes 182000000 | tf_op jit(solution)/shard_map/pallas_call | solution.py:673
  380.9 22.1 %shard_map.242 = (bf16[3,768,288]{2,1,0:T(8,128)(2,1)}, f32[2,1,288]{2,1,0:T(1,128)}) custom-call(s32[8]{0:T(128)} %get-tuple-element.68.spans, bf16[768,512]{1,0:T(8,128)(2,1)} %get-tuple-element.79.q, bf16[768,512]{1,0:T(8,128)(2,1)} %get-tuple-element.80.k, bf16[768,512]{1,0:T(8,128)(2,1)} %get-tuple-element.81.v, ...), custom_call_target="tpu_custom_call" | custom-call | bytes 98000000 | tf_op jit(solution)/shard_map/pallas_call | solution.py:799
  403.0 24.1 %shard_map.243 = (f32[192,1152]{1,0:T(8,128)}, bf16[192,1152]{1,0:T(8,128)(2,1)}, f32[2,12,8,576]{3,2,1,0:T(8,128)}, bf16[4,144,1152]{2,1,0:T(8,128)(2,1)}) custom-call(bf16[3,768,288]{2,1,0:T(8,128)(2,1)} %get-tuple-element.107.dproj, bf16[192,1152]{1,0:T(8,128)(2,1)} %dynamic-slice_bitcast_fusion.1.x, f32[192,1152]{1,0:T(8,128)} %get-tuple-element.108.dx1, ...), custom_call_target="tpu_custom_call" | custom-call | bytes 77000000 | tf_op jit(solution)/shard_map/pallas_call | solution.py:673
  429.3 1.7 constant_dynamic-slice_fusion
  431.6 1.9 select_bitcast_fusion.2
  434.1 37.6 %shard_map.244 = (f32[288,1728]{1,0:T(8,128)}, f32[3,1,576]{2,1,0:T(1,128)}, f32[2,8,1152]{2,1,0:T(8,128)}, f32[8,288]{1,0:T(8,128)}) custom-call(f32[2,12,8,576]{3,2,1,0:T(8,128)} %get-tuple-element.114.dmod, f32[2,8,288]{2,1,0:T(8,128)} %pad.15.dgain, f32[8,8,288]{2,1,0:T(8,128)} %bitcast.102, bf16[1728,1152]{1,0:T(8,128)(2,1)} %bitcast.93), custom_call_target="tpu_custom_call" | custom-call | bytes 52500000 | tf_op jit(solution)/shard_map/pallas_call | solution.py:673
  471.7 1.5 slice.51
  473.2 1.4 reshape.193
  478.1 1.3 dynamic_slice.16
  479.5 1.4 fusion.8
  482.0 1.3 maximum_select_fusion
  483.3 18.8 %reduce-scatter.7.cloned.1.call-done = bf16[1,144,1152]{2,1,0:T(8,128)(2,1)} async-done(((bf16[4,144,1152]{2,1,0:T(8,128)(2,1)}), bf16[1,144,1152]{2,1,0:T(8,128)(2,1)}) %reduce-scatter.7.cloned.1.call-update) | async-done | bytes 331792 | tf_op jit(solution)/shard_map/reduce_scatter | solution.py:844
  504.3 51.5 %reduce-scatter.9.cloned.1.call-done = bf16[1,144,2304]{2,1,0:T(8,128)(2,1)} async-done(((bf16[4,144,2304]{2,1,0:T(8,128)(2,1)}), bf16[1,144,2304]{2,1,0:T(8,128)(2,1)}) %reduce-scatter.9.cloned.1.call-update) | async-done | bytes 663568 | tf_op jit(solution)/shard_map/reduce_scatter | solution.py:844
  555.9 54.5 %reduce-scatter.11.cloned.1.call-done = bf16[1,144,2304]{2,1,0:T(8,128)(2,1)} async-done(((bf16[4,144,2304]{2,1,0:T(8,128)(2,1)}), bf16[1,144,2304]{2,1,0:T(8,128)(2,1)}) %reduce-scatter.11.cloned.1.call-update) | async-done | bytes 663568 | tf_op jit(solution)/shard_map/reduce_scatter | solution.py:844
  610.4 2.2 select_bitcast_fusion.1
  617.6 1.3 maximum_bitcast_fusion
  619.8 1.3 copy.35
  (79 shorter events, 24.9 us)
Async XLA Ops:
  7.2 24.5 %copy-start = (bf16[2,192,1152]{2,1,0:T(8,128)(2,1)S(1)}, bf16[2,192,1152]{2,1,0:T(8,128)(2,1)}, u32[]{:S(2)}) copy-start(bf16[2,192,1152]{2,1,0:T(8,128)(2,1)} %param.16) | copy-start | bytes 2654212
  7.2 476.1 %reduce-scatter.5.cloned.1.call-start = ((), (), s32[]{:S(2)}) async-start(), calls=%async_computation.4 | async-start | bytes 1658880 | tf_op jit(solution)/shard_map/reduce_scatter | solution.py:844
  7.2 64.4 %collective-permute-start.2 = (bf16[2,1152,768]{2,1,0:T(8,128)(2,1)}, bf16[2,1152,768]{2,1,0:T(8,128)(2,1)}, u32[]{:S(2)}, u32[]{:S(2)}) collective-permute-start(bf16[2,1152,768]{2,1,0:T(8,128)(2,1)} %bitcast.77), channel_id=1, source_target_pairs={{0,16},{16,0},{1,17},{17,1},{2,18},{18,2},{3,19},{19,3},{4,20},{20... | collective-permute-start | bytes 10616840 | tf_op jit(solution)/shard_map/ppermute | solution.py:811
  7.3 28.4 %collective-permute-start = (bf16[3,288,1152]{2,1,0:T(8,128)(2,1)}, bf16[3,288,1152]{2,1,0:T(8,128)(2,1)S(1)}, u32[]{:S(2)}, u32[]{:S(2)}) collective-permute-start(bf16[3,288,1152]{2,1,0:T(8,128)(2,1)} %bitcast.82), channel_id=1, source_target_pairs={{0,16},{16,0},{1,17},{17,1},{2,18},{18,2},{3,19},{19,3},{4,20},{20... | collective-permute-start | bytes 5971976 | tf_op jit(solution)/shard_map/ppermute | solution.py:811
  7.8 63.8 %collective-permute-start.3 = (bf16[768,1152]{1,0:T(8,128)(2,1)}, bf16[768,1152]{1,0:T(8,128)(2,1)}, u32[]{:S(2)}, u32[]{:S(2)}) collective-permute-start(bf16[768,1152]{1,0:T(8,128)(2,1)} %bitcast.87), channel_id=1, source_target_pairs={{0,16},{16,0},{1,17},{17,1},{2,18},{18,2},{3,19},{19,3},{4,20},{20... | collective-permute-start | bytes 5308424 | tf_op jit(solution)/shard_map/ppermute | solution.py:811
  7.9 63.7 %collective-permute-start.1 = (bf16[288,1152]{1,0:T(8,128)(2,1)}, bf16[288,1152]{1,0:T(8,128)(2,1)S(1)}, u32[]{:S(2)}, u32[]{:S(2)}) collective-permute-start(bf16[288,1152]{1,0:T(8,128)(2,1)} %bitcast.94), channel_id=1, source_target_pairs={{0,16},{16,0},{1,17},{17,1},{2,18},{18,2},{3,19},{19,3},{4,20},{20... | collective-permute-start | bytes 1990664 | tf_op jit(solution)/shard_map/ppermute | solution.py:811
  31.7 2.6 copy-start.10
  31.7 3.2 copy-start.8
  35.7 1.3 copy-start.2
  71.6 0.8 copy-start.3
  427.2 74.9 %reduce-scatter.7.cloned.1.call-start = ((), (), s32[]{:S(2)}) async-start(), calls=%async_computation.5 | async-start | bytes 1658880 | tf_op jit(solution)/shard_map/reduce_scatter | solution.py:844
  427.9 128.0 %reduce-scatter.9.cloned.1.call-start = ((), (), s32[]{:S(2)}) async-start(), calls=%async_computation.6 | async-start | bytes 3317760 | tf_op jit(solution)/shard_map/reduce_scatter | solution.py:844
  428.6 2.3 copy-start.6
  428.7 2.3 copy-start.7
  428.7 181.7 %reduce-scatter.11.cloned.1.call-start = ((), (), s32[]{:S(2)}) async-start(), calls=%async_computation.7 | async-start | bytes 3317760 | tf_op jit(solution)/shard_map/reduce_scatter | solution.py:844
  429.2 2.3 copy-start.4
  431.0 2.5 copy-start.12
  431.0 2.5 copy-start.11
  431.1 50.9 %collective-permute-start.5 = (f32[192,1152]{1,0:T(8,128)S(1)}, f32[192,1152]{1,0:T(8,128)S(1)}, u32[]{:S(2)}, u32[]{:S(2)}) collective-permute-start(f32[192,1152]{1,0:T(8,128)S(1)} %get-tuple-element.156), channel_id=1, source_target_pairs={{0,16},{16,0},{1,17},{17,1},{2,18},{18,2},{3,19},{19,3},{4,20},{20... | collective-permute-start | bytes 2654216 | tf_op jit(solution)/shard_map/ppermute | solution.py:811
  434.1 43.3 %copy-start.9 = (bf16[192,1152]{1,0:T(8,128)(2,1)S(1)}, bf16[192,1152]{1,0:T(8,128)(2,1)}, u32[]{:S(2)}) copy-start(bf16[192,1152]{1,0:T(8,128)(2,1)} %get-tuple-element.158) | copy-start | bytes 1327108
  477.4 3.5 collective-permute-start.4
  503.2 110.5 %collective-permute-start.6 = (bf16[144,1152]{1,0:T(8,128)(2,1)S(1)}, bf16[144,1152]{1,0:T(8,128)(2,1)S(1)}, u32[]{:S(2)}, u32[]{:S(2)}) collective-permute-start(bf16[144,1152]{1,0:T(8,128)(2,1)S(1)} %get-tuple-element.160), channel_id=1, source_target_pairs={{0,16},{16,0},{1,17},{17,1},{2,18},{18,2},{3,19},{19,3},{4,20},{20... | collective-permute-start | bytes 995336 | tf_op jit(solution)/shard_map/ppermute | solution.py:811
  612.6 3.7 collective-permute-start.7
  617.6 2.2 copy-start.5
  619.0 2.2 copy-start.1
Sparse Core Ops, SparseCore 0:
  427.3 39.8 reduce-scatter.4
  469.5 32.5 reduce-scatter.6
  504.4 51.4 reduce-scatter.8
  558.0 52.3 reduce-scatter.10

commit v3 on v2

--- a/solution.py
+++ b/solution.py
@@ -14,7 +14,6 @@
 BF = jnp.bfloat16
 S, DP, T = "section", "dp", "tensor"
 PAD = 128
-LANES = 384
 TILE = 256
 
 
@@ -192,6 +191,48 @@
     return pltpu.make_async_copy(own, dst, sem)
 
 
+def head_weights(own, other, layer, dst, sems, parts):
+    mine = lax.axis_index(S) == layer
+    spread = len(parts) > 1
+    heads = dst.shape[-2] // PAD
+    head = own.shape[-2] // heads
+    clean = head // 16 * 16
+    copies = ([], [])
+    for n, part in enumerate(parts):
+        for h in range(heads):
+            to = dst.at[part] if spread else dst
+            to[pl.ds(h * PAD + clean, PAD - clean)] = jnp.zeros((PAD - clean, dst.shape[-1]), BF)
+            to = to.at[pl.ds(h * PAD, head)]
+            for which, src in enumerate((own, other)):
+                src = src.at[part] if spread else src
+                copies[which].append(
+                    pltpu.make_async_copy(
+                        src.at[pl.ds(h * head, head)], to, sems.at[n * heads + h]
+                    )
+                )
+
+    @pl.when(mine)
+    def _():
+        for copy in copies[0]:
+            copy.start()
+
+    @pl.when(jnp.logical_not(mine))
+    def _():
+        for copy in copies[1]:
+            copy.start()
+
+    return copies[0]
+
+
+def arrive(copies):
+    for copy in copies:
+        copy.wait()
+
+
+def twice(row):
+    return jnp.concatenate([row, row], axis=-1)
+
+
 def over_blocks(rows, fn):
     step = rows // 4
 
@@ -275,9 +316,11 @@
     return inverse * (incoming - normal * jnp.mean(incoming * normal, axis=-1, keepdims=True))
 
 
-def qkv_kernel(layer, square, x, sel, mod, w_own, w_other, whole, proj, h, w, ssem, rsem, wsem):
+def qkv_kernel(layer, square, x, sel, mod, gain, both, turn, ones, w_own, w_other, whole, proj, q,
+               k, v, h, w, ssem, rsem, wsem):
     place = ring(square)
-    load = layer_weights(w_own, w_other, layer, w, wsem)
+    head = w_own.shape[1] * PAD // w.shape[1]
+    load = head_weights(w_own, w_other, layer, w, wsem, range(3))
     greet(place)
 
     def prepare(rows):
@@ -291,26 +334,35 @@
 
     def use(chunk):
         if not waited:
-            load.wait()
+            arrive(load)
             waited.append(1)
         rows = chunk_rows(chunk, x.shape[0])
-        for k in range(3):
-            proj[k, rows] = nt(whole[rows], w[k])
+        cosine = twice(both[rows, 0:PAD])
+        sine = twice(both[rows, PAD : 2 * PAD])
+        for which, dst in ((0, q), (1, k)):
+            full = nt(whole[rows], w[which])
+            proj[which, rows] = full.astype(BF)
+            for pair in range(full.shape[1] // (2 * PAD)):
+                lanes = slice(pair * 2 * PAD, (pair + 1) * 2 * PAD)
+                normal, _ = unit(full[:, lanes], ones[...], head)
+                gained = normal * twice(gain[which : which + 1])
+                dst[rows, lanes] = (gained * cosine + two(nn, gained, turn[...]) * sine).astype(BF)
+        v[rows] = nt(whole[rows], w[2]).astype(BF)
 
     gather(place, h, whole, (ssem, rsem), 0, use)
 
 
 def mlp_kernel(layer, square, att, x, sel, mod, wo0, wo1, wg0, wg1, wd0, wd1, br1, x1, whole,
                gate, up, hidden, br2, y, h, wo, wg, wd, o1, i1, k1, s1, o2, i2, k2, s2,
-               ssem, rsem, wsem):
+               ssem, rsem, wsem, osem):
     place = ring(square)
     rows_here, _ = x.shape
-    load_o = layer_weights(wo0, wo1, layer, wo, wsem.at[0])
+    load_o = head_weights(wo0, wo1, layer, wo, osem, range(1))
     load_g = layer_weights(wg0, wg1, layer, wg, wsem.at[1])
     load_d = layer_weights(wd0, wd1, layer, wd, wsem.at[2])
     greet(place)
     sems = (ssem, rsem)
-    load_o.wait()
+    arrive(load_o)
     first = (o1, i1, k1, s1)
     scatter(place, lambda c: nn(att[chunk_rows(c, rows_here)], wo[...]), first, sems, 0)
 
@@ -350,7 +402,7 @@
 def mlp_back_kernel(layer, square, dy, br2, br1, x1, sel, mod, gate_h, up_h, hidden_h, rows_h,
                     wo0, wo1, wg0, wg1, wd0, wd1, whole1, datt, dx1, dmod, total, mine, theirs,
                     got, h, h1, whole2, dgate, dup, gate, up, hidden, saved, flipped, wo, wg, wd, o1, i1, k1,
-                    s1, ssem, rsem, wsem):
+                    s1, ssem, rsem, wsem, osem):
     place = ring(square)
     rows_here, _ = dy.shape
     load_d = layer_weights(wd0, wd1, layer, wd, wsem.at[0])
@@ -359,7 +411,7 @@
     load_up = pltpu.make_async_copy(up_h, up, wsem.at[2])
     load_up.start()
     load_g = layer_weights(wg0, wg1, layer, wg, wsem.at[3])
-    load_o = layer_weights(wo0, wo1, layer, wo, wsem.at[4])
+    load_o = head_weights(wo0, wo1, layer, wo, osem, range(1))
     load_hidden = pltpu.make_async_copy(hidden_h, hidden, wsem.at[5])
     load_hidden.start()
     load_rows = pltpu.make_async_copy(rows_h, saved, wsem.at[6])
@@ -423,7 +475,7 @@
         add_sums(dmod, 0, sel[rows], d_mixed * br1[rows])
 
     over_blocks(rows_here, between)
-    load_o.wait()
+    arrive(load_o)
     load_rows.wait()
 
     def use_out(chunk):
@@ -440,41 +492,58 @@
     add_halves(packs, copies, total)
 
 
-def qkv_back_kernel(layer, square, dproj, x, dx1, sel, mod, part, prev, w_own, w_other, whole_h,
-                    att_h, rows1_h, du, du_b, dmod, total, w, whole, att, rows1, flipped, mine,
-                    theirs, got, o1, i1, k1, s1, ssem, rsem, wsem):
+def qkv_back_kernel(layer, square, dq, dk, dv, proj, gain, both, turn, ones, spread, x, dx1, sel,
+                    mod, part, prev, w_own, w_other, whole_h, att_h, rows1_h, du, du_b, dmod, total,
+                    dgain, w, whole, att, rows1, flipped, dproj, flat, mine, theirs, got, o1, i1,
+                    k1, s1, ssem, rsem, wsem, hsem):
     place = ring(square)
     rows_here, _ = x.shape
-    load = layer_weights(w_own, w_other, layer, w, wsem.at[0])
+    packed = spread.shape[0]
+    head = packed * PAD // spread.shape[1]
+    load = head_weights(w_own, w_other, layer, w, hsem, range(3))
     loads = []
     for n, (src, dst) in enumerate(((whole_h, whole), (att_h, att), (rows1_h, rows1))):
-        loads.append(pltpu.make_async_copy(src, dst, wsem.at[1 + n]))
+        loads.append(pltpu.make_async_copy(src, dst, wsem.at[n]))
         loads[n].start()
     greet(place, True)
     here = dmod.at[layer]
     dmod[1 - layer] = prev[...]
     here[pl.ds(0, 4)] = jnp.zeros_like(prev[pl.ds(0, 4)])
     here[pl.ds(4, 8)] = part[...]
-    load.wait()
+    dgain[...] = jnp.zeros_like(dgain)
+    arrive(load)
     bufs = (o1, i1, k1, s1)
     sems = (ssem, rsem)
     packs = (mine, theirs, got)
-    packed = att.shape[1]
     copies = []
 
     def term(chunk):
         rows = chunk_rows(chunk, rows_here)
-        return nn(dproj[0, rows], w[0]) + nn(dproj[1, rows], w[1]) + nn(dproj[2, rows], w[2])
+        cosine = twice(both[rows, 0:PAD])
+        sine = twice(both[rows, PAD : 2 * PAD])
+        for which, src in ((0, dq), (1, dk)):
+            for pair in range(src.shape[1] // (2 * PAD)):
+                lanes = slice(pair * 2 * PAD, (pair + 1) * 2 * PAD)
+                turned = src[rows, lanes]
+                back = turned.astype(F32) * cosine - nn(turned, turn[...]) * sine
+                normal, inverse = unit(proj[which, rows, lanes].astype(F32), ones[...], head)
+                dgain[which, :, lanes] += jnp.sum(back * normal, axis=0, keepdims=True)
+                gained = back * twice(gain[which : which + 1])
+                mean = two(nn, gained * normal, ones[...]) * (1.0 / head)
+                dproj[which, rows, lanes] = (inverse * (gained - normal * mean)).astype(BF)
+        return nn(dproj[0, rows], w[0]) + nn(dproj[1, rows], w[1]) + nn(dv[rows], w[2])
 
     def grad_in():
         loads[0].wait()
         for k in range(3):
-            weight_grad(None if k else whole, dproj.at[k], flipped, k * packed, packs, 6)
+            flat[...] = nt(dproj[k] if k < 2 else dv[...], spread[...]).astype(BF)
+            weight_grad(None if k else whole, flat, flipped, k * packed, packs, 6)
 
     def grad_out():
         loads[1].wait()
         loads[2].wait()
-        weight_grad(rows1, att, flipped, 3 * packed, packs, 6)
+        flat[...] = nt(att[...], spread[...]).astype(BF)
+        weight_grad(rows1, flat, flipped, 3 * packed, packs, 6)
         copies.append(send_half(packs, sems, (6, 0, 4 * packed)))
 
     scatter(place, term, bufs, sems, 0, (grad_in, grad_out))
@@ -686,41 +755,33 @@
     )(*args)
 
 
-def attention_kernel(spans, proj, gain, both, turn, spread, ones, q, k, v, att, padded):
-    heads = spread.shape[1] // PAD
-    packed = proj.shape[2]
-    head = packed // heads
+def attention_kernel(head, spans, q, k, v, att):
+    rows, wide = q.shape
     scale = head ** (-0.5)
-    rows = proj.shape[1]
-
-    def units(at):
-        for which, dst in ((0, q), (1, k)):
-            normal, _ = unit(proj[which, at], ones[...], head)
-            gained = normal * gain[which : which + 1]
-            turned = gained * both[at, 0:packed]
-            turned = turned + two(nn, gained, turn[...]) * both[at, LANES : LANES + packed]
-            dst[at] = nn(turned.astype(BF), spread[...]).astype(BF)
-        v[at] = nn(proj[2, at].astype(BF), spread[...]).astype(BF)
-
-    over_blocks(rows, units)
+
+    def each_head(fn):
+        for n in range(wide // PAD):
+            fn(slice(n * PAD, (n + 1) * PAD))
+
     for item in range(3):
-        start = pl.multiple_of(spans[item], 16)
-        length = spans[4 + item]
-        at = pl.ds(start, TILE)
-        valid = lax.broadcasted_iota(jnp.int32, (TILE, TILE), 1) < length
-        for n in range(heads):
-            lanes = slice(n * PAD, (n + 1) * PAD)
-            padded[at, lanes] = softmax_rows(q[at, lanes], k[at, lanes], v[at, lanes], valid, scale)
+        at = pl.ds(pl.multiple_of(spans[item], 16), TILE)
+        valid = lax.broadcasted_iota(jnp.int32, (TILE, TILE), 1) < spans[4 + item]
+
+        def tile(lanes, at=at, valid=valid):
+            att[at, lanes] = softmax_rows(q[at, lanes], k[at, lanes], v[at, lanes], valid, scale)
+
+        each_head(tile)
     first = rows - 48
     start = spans[3]
     at = pl.ds(first, 48)
     valid = first + lax.broadcasted_iota(jnp.int32, (48, 48), 1) >= start
     live = first + lax.broadcasted_iota(jnp.int32, (48, PAD), 0) >= start
-    for n in range(heads):
-        lanes = slice(n * PAD, (n + 1) * PAD)
+
+    def rest(lanes):
         new = softmax_rows(q[at, lanes], k[at, lanes], v[at, lanes], valid, scale)
-        padded[at, lanes] = jnp.where(live, new, padded[at, lanes])
-    att[...] = nt(padded[...], spread[...]).astype(BF)
+        att[at, lanes] = jnp.where(live, new, att[at, lanes])
+
+    each_head(rest)
 
 
 def unit(proj, ones, head):
@@ -746,53 +807,42 @@
     return tn(d_scores, key) * scale, nn(d_scores, query) * scale, d_value
 
 
-def attention_back_kernel(spans, q, k, v, datt, proj, gain, both, turn, spread, ones, dproj,
-                          dgain, grad, dq, dk, dv):
-    heads = spread.shape[1] // PAD
-    rows, packed = datt.shape
-    head = packed // heads
+def attention_back_kernel(head, spans, q, k, v, grad, dq, dk, dv):
+    rows, wide = q.shape
     scale = head ** (-0.5)
-    grad[...] = nn(datt[...], spread[...]).astype(BF)
+
+    def each_head(fn):
+        for n in range(wide // PAD):
+            fn(slice(n * PAD, (n + 1) * PAD))
+
     for item in range(3):
-        start = pl.multiple_of(spans[item], 16)
-        length = spans[4 + item]
-        at = pl.ds(start, TILE)
-        keys = lax.broadcasted_iota(jnp.int32, (TILE, TILE), 0) < length
-        queries = lax.broadcasted_iota(jnp.int32, (TILE, TILE), 1) < length
-        for n in range(heads):
-            lanes = slice(n * PAD, (n + 1) * PAD)
+        at = pl.ds(pl.multiple_of(spans[item], 16), TILE)
+        keys = lax.broadcasted_iota(jnp.int32, (TILE, TILE), 0) < spans[4 + item]
+        queries = lax.broadcasted_iota(jnp.int32, (TILE, TILE), 1) < spans[4 + item]
+
+        def tile(lanes, at=at, keys=keys, queries=queries):
             parts = back_tile(
                 q[at, lanes], k[at, lanes], v[at, lanes], grad[at, lanes], keys, queries, scale
             )
-            dq[at, lanes], dk[at, lanes], dv[at, lanes] = parts
+            for new, dst in zip(parts, (dq, dk, dv)):
+                dst[at, lanes] = new.astype(BF)
+
+        each_head(tile)
     first = rows - 48
     start = spans[3]
     at = pl.ds(first, 48)
     keys = first + lax.broadcasted_iota(jnp.int32, (48, 48), 0) >= start
     queries = first + lax.broadcasted_iota(jnp.int32, (48, 48), 1) >= start
     live = first + lax.broadcasted_iota(jnp.int32, (48, PAD), 0) >= start
-    for n in range(heads):
-        lanes = slice(n * PAD, (n + 1) * PAD)
+
+    def rest(lanes):
         parts = back_tile(
             q[at, lanes], k[at, lanes], v[at, lanes], grad[at, lanes], keys, queries, scale
         )
         for new, dst in zip(parts, (dq, dk, dv)):
-            dst[at, lanes] = jnp.where(live, new, dst[at, lanes])
-    dgain[...] = jnp.zeros_like(dgain)
-
-    def finish(at):
-        for which, src in ((0, dq), (1, dk)):
-            flat = two(nt, src[at], spread[...])
-            back = flat * both[at, 0:packed]
-            back = back - two(nn, flat, turn[...]) * both[at, LANES : LANES + packed]
-            normal, inverse = unit(proj[which, at], ones[...], head)
-            dgain[which] += jnp.sum(back * normal, axis=0, keepdims=True)
-            gained = back * gain[which : which + 1]
-            mean = two(nn, gained * normal, ones[...]) * (1.0 / head)
-            dproj[which, at] = (inverse * (gained - normal * mean)).astype(BF)
-        dproj[2, at] = nt(dv[at].astype(BF), spread[...]).astype(BF)
-
-    over_blocks(rows, finish)
+            dst[at, lanes] = jnp.where(live, new.astype(BF), dst[at, lanes])
+
+    each_head(rest)
 
 
 def local_call(kernel, micros, outs, scratch, spans, args):
@@ -814,12 +864,12 @@
 def head_tables(packed, head):
     quarter = head // 4
     frequency = np.float32(10000.0) ** (-np.arange(quarter, dtype=np.float32) / quarter)
-    lane = np.arange(packed) % head
+    lane = np.arange(head)
     angle = np.arange(32, dtype=np.float32)[:, None] * frequency[lane % quarter][None, :]
     by_row = (lane // (2 * quarter) == 0)[None, :]
-    table = np.zeros((64, 2 * LANES), np.float32)
+    table = np.zeros((64, 2 * PAD), np.float32)
     for n, values in enumerate((np.cos(angle), np.sin(angle))):
-        at = slice(n * LANES, n * LANES + packed)
+        at = slice(n * PAD, n * PAD + head)
         table[:32, at] = np.where(by_row, values, 0.0)
         table[32:, at] = np.where(by_row, 0.0, values)
     table = jnp.asarray(table)
@@ -827,16 +877,18 @@
     for _ in range(3):
         parts.append(lax.reduce_precision(table, 8, 7).astype(BF))
         table = table - parts[-1].astype(F32)
+    rows = np.arange(2 * PAD)[:, None]
+    cols = np.arange(2 * PAD)[None, :]
+    inside = (rows // PAD == cols // PAD) & (rows % PAD < head) & (cols % PAD < head)
+    row, col = rows % PAD, cols % PAD
+    early = (col % (2 * quarter)) < quarter
+    turn = np.where(inside & early & (row == col + quarter), -1.0, 0.0)
+    turn = turn + np.where(inside & ~early & (row == col - quarter), 1.0, 0.0)
+    heads = packed // head
     rows = np.arange(packed)[:, None]
-    cols = np.arange(packed)[None, :]
-    early = (cols % (2 * quarter)) < quarter
-    turn = np.where(early & (rows == cols + quarter), -1.0, 0.0)
-    turn = turn + np.where(~early & (rows == cols - quarter), 1.0, 0.0)
-    heads = packed // head
     wide = np.arange(heads * PAD)[None, :]
     spread = (rows // head == wide // PAD) & (rows % head == wide % PAD)
-    ones = rows // head == cols // head
-    lanes = tuple(jnp.asarray(m.astype(np.float32)).astype(BF) for m in (turn, spread, ones))
+    lanes = tuple(jnp.asarray(m.astype(np.float32)).astype(BF) for m in (turn, inside, spread))
     return jnp.stack(parts), lanes
 
 
@@ -873,9 +925,9 @@
     ada = ada_weight[0].T
     half = width // 2
     bias = ada_bias.astype(F32).reshape(3, 1, half)
-    gain = jnp.tile(qk_gain[0].astype(F32), (1, heads))
-    gain = jnp.pad(gain, ((0, 6), (0, 0)))
-    trig, lanes = head_tables(packed, head)
+    gain = jnp.pad(qk_gain[0].astype(F32), ((0, 6), (0, PAD - head)))
+    trig, (turn, ones, spread) = head_tables(packed, head)
+    wide = heads * PAD
     mods, lifted_all, gains, sel, both, spans = ring_call(
         functools.partial(head_kernel, dp),
         8,
@@ -883,9 +935,9 @@
         [
             sds((2, 6, 8, width), F32),
             sds((dp, 16, width), F32),
-            sds((2, 8, packed), F32),
+            sds((2, 8, PAD), F32),
             sds((rows, 8), F32),
-            sds((seq, 2 * LANES), F32),
+            sds((seq, 2 * PAD), F32),
             sds((8,), jnp.int32),
         ],
         [
@@ -901,7 +953,6 @@
         (1, 0, 1, 1, 1, 1, 1),
         scalar=5,
     )
-    tables = (both,) + lanes
     part = width // dp
     shard = lax.axis_index(DP)
     lifted_part = lax.dynamic_slice_in_dim(lifted_all, shard * part, part, 2)
@@ -911,24 +962,24 @@
     kept = []
     for layer in range(2):
         mod = mods[layer]
-        whole1, proj = ring_call(
+        whole1, proj, q, k, v = ring_call(
             functools.partial(qkv_kernel, layer, square),
             layer,
             20,
-            [sds((seq, width), BF), sds((3, seq, packed), F32)],
-            [pltpu.VMEM((rows, width), BF), pltpu.VMEM((3, packed, width), BF)]
+            [sds((seq, width), BF), sds((2, seq, wide), BF)] + [sds((seq, wide), BF)] * 3,
+            [pltpu.VMEM((rows, width), BF), pltpu.VMEM((3, wide, width), BF)]
             + dma_sems(6)
-            + [pltpu.SemaphoreType.DMA],
-            (x, sel, mod, own[0], other[0]),
-            (1, 1, 1, 0, 0),
-        )
-        q, k, v, att = local_call(
-            attention_kernel,
-            12,
-            [sds((seq, heads * PAD), BF)] * 3 + [sds((seq, packed), BF)],
-            [pltpu.VMEM((seq, heads * PAD), BF)],
+            + [pltpu.SemaphoreType.DMA((3 * heads,))],
+            (x, sel, mod, gains[layer], both, turn, ones, own[0], other[0]),
+            (1,) * 7 + (0, 0),
+        )
+        (att,) = local_call(
+            functools.partial(attention_kernel, head),
+            6,
+            [sds((seq, wide), BF)],
+            [],
             spans,
-            (proj, gains[layer]) + tables,
+            (q, k, v),
         )
         br1, x1, whole2, gate, up, hidden, br2, y = ring_call(
             functools.partial(mlp_kernel, layer, square),
@@ -946,14 +997,14 @@
             ],
             [
                 pltpu.VMEM((rows, width), BF),
-                pltpu.VMEM((packed, width), BF),
+                pltpu.VMEM((wide, width), BF),
                 pltpu.VMEM((2, width, hidden_here), BF),
                 pltpu.VMEM((hidden_here, width), BF),
             ]
             + scatter_scratch(rows, width)
             + scatter_scratch(rows, width)
             + dma_sems(18)
-            + [pltpu.SemaphoreType.DMA((3,))],
+            + [pltpu.SemaphoreType.DMA((3,)), pltpu.SemaphoreType.DMA((heads,))],
             (att, x, sel, mod, own[1], other[1], own[2], other[2], own[3], other[3]),
             (1, 1, 1, 1) + (0,) * 6,
         )
@@ -974,7 +1025,7 @@
             52,
             [
                 sds((seq, width), BF),
-                sds((seq, packed), BF),
+                sds((seq, wide), BF),
                 sds((rows, width), F32),
                 sds((8, 8, half), F32),
                 sds((dp, part // 2, 3 * hidden_here), BF),
@@ -991,30 +1042,27 @@
                 pltpu.VMEM((seq, hidden_here), BF),
                 pltpu.VMEM((seq, width), BF),
                 pltpu.VMEM((width, seq), BF),
-                pltpu.VMEM((packed, width), BF),
+                pltpu.VMEM((wide, width), BF),
                 pltpu.VMEM((2, width, hidden_here), BF),
                 pltpu.VMEM((hidden_here, width), BF),
             ]
             + scatter_scratch(rows, width)
             + dma_sems(21)
-            + [pltpu.SemaphoreType.DMA((7,))],
+            + [pltpu.SemaphoreType.DMA((7,)), pltpu.SemaphoreType.DMA((heads,))],
             (dy, br2, br1, x1, sel, mod, gate, up, hidden, whole2, own[1], other[1], own[2],
              other[2], own[3], other[3]),
             (1,) * 6 + (0,) * 10,
         )
         pack_mlp = reduced(total_mlp)
-        dproj, dgain = local_call(
-            attention_back_kernel,
-            28,
-            [
-                sds((3, seq, packed), BF),
-                sds((2, 1, packed), F32),
-            ],
-            [pltpu.VMEM((seq, heads * PAD), BF)] + [pltpu.VMEM((seq, heads * PAD), F32)] * 3,
+        dq, dk, dv = local_call(
+            functools.partial(attention_back_kernel, head),
+            10,
+            [sds((seq, wide), BF)] * 3,
+            [],
             spans,
-            (q, k, v, datt, proj, gains[layer]) + tables,
-        )
-        du, du_b, d_mod, total_att = ring_call(
+            (q, k, v, datt),
+        )
+        du, du_b, d_mod, total_att, dgain = ring_call(
             functools.partial(qkv_back_kernel, layer, square),
             6 + layer,
             22,
@@ -1023,20 +1071,24 @@
                 sds((rows, width), BF),
                 sds((2, 12, 8, half), F32),
                 sds((dp, part // 2, 4 * packed), BF),
+                sds((2, 1, wide), F32),
             ],
             [
-                pltpu.VMEM((3, packed, width), BF),
+                pltpu.VMEM((3, wide, width), BF),
                 pltpu.VMEM((seq, width), BF),
-                pltpu.VMEM((seq, packed), BF),
+                pltpu.VMEM((seq, wide), BF),
                 pltpu.VMEM((seq, width), BF),
                 pltpu.VMEM((width, seq), BF),
+                pltpu.VMEM((2, seq, wide), BF),
+                pltpu.VMEM((seq, packed), BF),
             ]
             + [pltpu.VMEM((dp, part // 2, 4 * packed), BF)] * 3
             + scatter_scratch(rows, width)
             + dma_sems(7)
-            + [pltpu.SemaphoreType.DMA((4,))],
-            (dproj, x, dx1, sel, mod, dmod_a, prev, own[0], other[0], whole1, att, rows1),
-            (1,) * 7 + (0,) * 5,
+            + [pltpu.SemaphoreType.DMA((3,)), pltpu.SemaphoreType.DMA((3 * heads,))],
+            (dq, dk, dv, proj, gains[layer], both, turn, ones, spread, x, dx1, sel, mod, dmod_a,
+             prev, own[0], other[0], whole1, att, rows1),
+            (1,) * 15 + (0,) * 5,
         )
         prev = d_mod[1]
         pack_att = reduced(total_att)
@@ -1045,7 +1097,7 @@
         d_inputs[layer] = du_b if layer else du
         dy = du_b
 
-    gain_parts = jnp.pad(jnp.stack(d_gains).reshape(2, 2, packed), ((0, 0), (0, 6), (0, 0)))
+    gain_parts = jnp.pad(jnp.stack(d_gains).reshape(2, 2, wide), ((0, 0), (0, 6), (0, 0)))
     g_ada_w, bias_grad, dl_sum, gain_sum = ring_call(
         functools.partial(tail_kernel, dp),
         9,
@@ -1054,16 +1106,16 @@
             sds((part, 3 * half), F32),
             sds((3, 1, half), F32),
             sds((2, 8, width), F32),
-            sds((8, packed), F32),
+            sds((8, wide), F32),
         ],
         [
             pltpu.VMEM((3 * half, width), BF),
             pltpu.VMEM((8, 3, 8, half), F32),
-            pltpu.VMEM((8, 8, packed), F32),
+            pltpu.VMEM((8, 8, wide), F32),
             pltpu.VMEM((2, 3, 8, half), F32),
-            pltpu.VMEM((8, packed), F32),
+            pltpu.VMEM((8, wide), F32),
             pltpu.VMEM((dp, 2, 3, 8, half), F32),
-            pltpu.VMEM((dp, 8, packed), F32),
+            pltpu.VMEM((dp, 8, wide), F32),
             pltpu.VMEM((8, 2, 8, width), F32),
         ]
         + dma_sems(13 + 2 * (dp - 1) + 8)
@@ -1075,7 +1127,7 @@
     g_ada_b = lax.dynamic_slice_in_dim(bias_grad.reshape(-1), shard * bias_part, bias_part)
     cond_grad = dl_sum[:, :per_micro].reshape(items, width) * cond_sigmoid
     cond_grad = cond_grad * (1.0 + cond_wide * (1.0 - cond_sigmoid))
-    gain_total = gain_sum[:2].reshape(1, 2, heads, head).sum(axis=2)
+    gain_total = gain_sum[:2].reshape(1, 2, heads, PAD)[..., :head].sum(axis=2)
 
     mlp = own_layer(section, (packs[0][0], packs[1][0]))
     attn = own_layer(section, (packs[0][1], packs[1][1]))

time: 637 us -> 608 us (0.954)
  Pallas kernels: 441 us -> 419 us
    pallas_call x4, Pallas kernels: 70.2 us -> 30 us  [local_call(): pl.pallas_call(kernel, out_shape=outs, in_specs=[pl.BlockSpec(memory_spac...]
    pallas_call x10, Pallas kernels: 371 us -> 389 us  [ring_call(): pl.pallas_call(kernel, out_shape=outs, in_specs=[vmem() if s else anywher...]
  transfers between devices with their start and end apart: 12 -> 12, of which waited for: 3 -> 3; matrix products, arithmetic and copies ran while one was open for 5% -> 5% of each run, Pallas kernels for 14% -> 13%
where the time goes in v3:
time: 608 us; the launch traced here: 605 us
  Pallas kernels  419 us (69%)
  waiting for transfers between devices  126 us (21%)
  local copies, waits for them, and re-layouts  22.3 us (4%)
  other arithmetic  17.9 us (3%)
  between operations  14.3 us (2%)
    pallas_call x10, Pallas kernels, ring_call(): pl.pallas_call(kernel, out_shape=outs, in_specs=[vmem() if s else anywher...  389 us
    reduce_scatter x4, waiting for transfers between devices, reduced(): return lax.psum_scatter(total, DP, scatter_dimension=0, tiled=True)[0]  124 us
    pallas_call x4, Pallas kernels, local_call(): pl.pallas_call(kernel, out_shape=outs, in_specs=[pl.BlockSpec(memory_spac...  30 us
  transfers between devices with their start and end apart: 12, of which 3 were waited for; matrix products, arithmetic and copies ran while one was open for 5% of the time, Pallas kernels for 13%

profile of v3, /device:TPU:1, one launch (start us, length us, event | category | flops | bytes accessed | tf_op | source)
XLA Modules:
  0.0 604.6 jit_solution(15008736052066663685)
XLA Ops:
  8.3 1.3 fusion.6
  9.7 1.3 reshape.178
  13.7 1.4 bitcast_convert_fusion.lifted
  15.0 15.9 %shard_map.231 = (f32[2,6,8,1152]{3,2,1,0:T(8,128)}, f32[4,16,1152]{2,1,0:T(8,128)}, f32[2,8,128]{2,1,0:T(8,128)}, f32[192,8]{1,0:T(8,128)}, f32[768,256]{1,0:T(8,128)}, /*index=5*/s32[8]{0:T(128)}) custom-call(f32[16,1152]{1,0:T(8,128)} %bitcast_convert_fusion.lifted, bf16[1728,1152]{1,0:T(8,128)(2,1)} %bitcast.90, f32[3,1,576]{2,1,0:T(1,128)} %reshape.191.bias, ...), custom_call_target="tpu_custom_call" | custom-call | bytes 42000000 | tf_op jit(solution)/shard_map/pallas_call | solution.py:742
  31.8 1.8 dynamic-slice_bitcast_fusion.dy
  35.0 1.3 copy-done.2
  36.3 24.0 %shard_map.232 = (bf16[768,1152]{1,0:T(8,128)(2,1)}, bf16[2,768,512]{2,1,0:T(8,128)(2,1)}, bf16[768,512]{1,0:T(8,128)(2,1)}, bf16[768,512]{1,0:T(8,128)(2,1)}, bf16[768,512]{1,0:T(8,128)(2,1)}) custom-call(bf16[192,1152]{1,0:T(8,128)(2,1)} %dynamic-slice_bitcast_fusion.1.x, f32[192,8]{1,0:T(8,128)} %get-tuple-element.71.sel, ...), custom_call_target="tpu_custom_call" | custom-call | bytes 70000000 | tf_op jit(solution)/shard_map/pallas_call | solution.py:742
  60.3 5.1 shard_map.233.att.att_h
  66.2 48.7 %shard_map.234 = (f32[192,1152]{1,0:T(8,128)}, f32[192,1152]{1,0:T(8,128)}, bf16[768,1152]{1,0:T(8,128)(2,1)}, f32[768,768]{1,0:T(8,128)}, f32[768,768]{1,0:T(8,...) custom-call(bf16[768,512]{1,0:T(8,128)(2,1)} %shard_map.233.att.att_h, ...), custom_call_target="tpu_custom_call" | custom-call | bytes 168000000 | tf_op jit(solution)/shard_map/pallas_call | solution.py:742
  114.9 19.6 %shard_map.235 = (bf16[768,1152]{1,0:T(8,128)(2,1)}, bf16[2,768,512]{2,1,0:T(8,128)(2,1)}, bf16[768,512]{1,0:T(8,128)(2,1)}, bf16[768,512]{1,0:T(8,128)(2,1)}, bf16[768,512]{1,0:T(8,128)(2,1)}) custom-call(bf16[192,1152]{1,0:T(8,128)(2,1)} %get-tuple-element.78.x, f32[192,8]{1,0:T(8,128)} %get-tuple-element.71.sel, f32[6,8,1152]{2,1,0:T(8,128)} %get-tuple-element.165.mod, ...), custom_call_target="tpu_custom_call" | custom-call | bytes 70000000 | tf_op jit(solution)/shard_map/pallas_call | solution.py:742
  134.5 5.1 shard_map.236.att.att_h
  139.7 49.1 %shard_map.237 = (f32[192,1152]{1,0:T(8,128)}, f32[192,1152]{1,0:T(8,128)}, bf16[768,1152]{1,0:T(8,128)(2,1)}, f32[768,768]{1,0:T(8,128)}, f32[768,768]{1,0:T(8,...) custom-call(bf16[768,512]{1,0:T(8,128)(2,1)} %shard_map.236.att.att_h, ...), custom_call_target="tpu_custom_call" | custom-call | bytes 168000000 | tf_op jit(solution)/shard_map/pallas_call | solution.py:742
  188.8 74.0 %shard_map.238 = (bf16[768,1152]{1,0:T(8,128)(2,1)}, bf16[768,512]{1,0:T(8,128)(2,1)}, f32[192,1152]{1,0:T(8,128)}, f32[8,8,576]{2,1,0:T(8,128)}, bf16[4,144,2304]{2,1,0:T(8,128)(2,1)}) custom-call(bf16[192,1152]{1,0:T(8,128)(2,1)} %dynamic-slice_bitcast_fusion.dy, f32[192,1152]{1,0:T(8,128)} %get-tuple-element.83.br2, f32[192,1152]{1,0:T(8,128)} %get-tuple-element.84.br1, ...), custom_call_target="tpu_custom_call" | custom-call | bytes 182000000 | tf_op jit(solution)/shard_map/pallas_call | solution.py:742
  262.9 9.9 %shard_map.239 = (bf16[768,512]{1,0:T(8,128)(2,1)}, bf16[768,512]{1,0:T(8,128)(2,1)}, bf16[768,512]{1,0:T(8,128)(2,1)}) custom-call(s32[8]{0:T(128)} %get-tuple-element.70.spans, bf16[768,512]{1,0:T(8,128)(2,1)} %get-tuple-element.79.q, bf16[768,512]{1,0:T(8,128)(2,1)} %get-tuple-element.80.k, bf16[768,512]{1,0:T(8,128)(2,1)} %get-tuple-element.81.v, ...), custom_call_target="tpu_custom_call" | custom-call | bytes 35000000 | tf_op jit(solution)/shard_map/pallas_call | solution.py:849
  273.4 28.7 %shard_map.240 = (f32[192,1152]{1,0:T(8,128)}, bf16[192,1152]{1,0:T(8,128)(2,1)}, f32[2,12,8,576]{3,2,1,0:T(8,128)}, bf16[4,144,1152]{2,1,0:T(8,128)(2,1)}, f32[2,1,512]{2,1,0:T(1,128)}) custom-call(bf16[768,512]{1,0:T(8,128)(2,1)} %get-tuple-element.91.dq, bf16[768,512]{1,0:T(8,128)(2,1)} %get-tuple-element.92.dk, bf16[768,512]{1,0:T(8,128)(2,1)} %get-tuple-element.93.dv, ...), custom_call_target="tpu_custom_call" | custom-call | bytes 77000000 | tf_op jit(solution)/shard_map/pallas_call | solution.py:742
  302.1 64.4 %shard_map.241 = (bf16[768,1152]{1,0:T(8,128)(2,1)}, bf16[768,512]{1,0:T(8,128)(2,1)}, f32[192,1152]{1,0:T(8,128)}, f32[8,8,576]{2,1,0:T(8,128)}, bf16[4,144,2304]{2,1,0:T(8,128)(2,1)}) custom-call(bf16[192,1152]{1,0:T(8,128)(2,1)} %get-tuple-element.99.dy, f32[192,1152]{1,0:T(8,128)} %get-tuple-element.100.br2, f32[192,1152]{1,0:T(8,128)} %get-tuple-element.101.br1, ...), custom_call_target="tpu_custom_call" | custom-call | bytes 182000000 | tf_op jit(solution)/shard_map/pallas_call | solution.py:742
  366.6 9.9 %shard_map.242 = (bf16[768,512]{1,0:T(8,128)(2,1)}, bf16[768,512]{1,0:T(8,128)(2,1)}, bf16[768,512]{1,0:T(8,128)(2,1)}) custom-call(s32[8]{0:T(128)} %get-tuple-element.70.spans, bf16[768,512]{1,0:T(8,128)(2,1)} %get-tuple-element.75.q, bf16[768,512]{1,0:T(8,128)(2,1)} %get-tuple-element.76.k, bf16[768,512]{1,0:T(8,128)(2,1)} %get-tuple-element.77.v, ...), custom_call_target="tpu_custom_call" | custom-call | bytes 35000000 | tf_op jit(solution)/shard_map/pallas_call | solution.py:849
  377.2 28.6 %shard_map.243 = (f32[192,1152]{1,0:T(8,128)}, bf16[192,1152]{1,0:T(8,128)(2,1)}, f32[2,12,8,576]{3,2,1,0:T(8,128)}, bf16[4,144,1152]{2,1,0:T(8,128)(2,1)}, f32[2,1,512]{2,1,0:T(1,128)}) custom-call(bf16[768,512]{1,0:T(8,128)(2,1)} %get-tuple-element.108.dq, bf16[768,512]{1,0:T(8,128)(2,1)} %get-tuple-element.109.dk, ...), custom_call_target="tpu_custom_call" | custom-call | bytes 77000000 | tf_op jit(solution)/shard_map/pallas_call | solution.py:742
  407.9 1.7 constant_dynamic-slice_fusion
  410.1 1.9 select_bitcast_fusion.2
  412.6 36.4 %shard_map.244 = (f32[288,1728]{1,0:T(8,128)}, f32[3,1,576]{2,1,0:T(1,128)}, f32[2,8,1152]{2,1,0:T(8,128)}, f32[8,512]{1,0:T(8,128)}) custom-call(f32[2,12,8,576]{3,2,1,0:T(8,128)} %get-tuple-element.118.dmod, f32[2,8,512]{2,1,0:T(8,128)} %pad.18.dgain, f32[8,8,288]{2,1,0:T(8,128)} %bitcast.100, bf16[1728,1152]{1,0:T(8,128)(2,1)} %bitcast.91), custom_call_target="tpu_custom_call" | custom-call | bytes 52500000 | tf_op jit(solution)/shard_map/pallas_call | solution.py:742
  449.0 1.5 slice.54
  450.5 1.4 reshape.185
  455.3 1.3 dynamic_slice.16
  457.2 1.4 fusion.8
  459.7 1.3 maximum_select_fusion
  461.0 17.7 %reduce-scatter.7.cloned.1.call-done = bf16[1,144,1152]{2,1,0:T(8,128)(2,1)} async-done(((bf16[4,144,1152]{2,1,0:T(8,128)(2,1)}), bf16[1,144,1152]{2,1,0:T(8,128)(2,1)}) %reduce-scatter.7.cloned.1.call-update) | async-done | bytes 331792 | tf_op jit(solution)/shard_map/reduce_scatter | solution.py:896
  481.0 51.5 %reduce-scatter.9.cloned.1.call-done = bf16[1,144,2304]{2,1,0:T(8,128)(2,1)} async-done(((bf16[4,144,2304]{2,1,0:T(8,128)(2,1)}), bf16[1,144,2304]{2,1,0:T(8,128)(2,1)}) %reduce-scatter.9.cloned.1.call-update) | async-done | bytes 663568 | tf_op jit(solution)/shard_map/reduce_scatter | solution.py:896
  532.5 54.5 %reduce-scatter.11.cloned.1.call-done = bf16[1,144,2304]{2,1,0:T(8,128)(2,1)} async-done(((bf16[4,144,2304]{2,1,0:T(8,128)(2,1)}), bf16[1,144,2304]{2,1,0:T(8,128)(2,1)}) %reduce-scatter.11.cloned.1.call-update) | async-done | bytes 663568 | tf_op jit(solution)/shard_map/reduce_scatter | solution.py:896
  587.1 2.2 select_bitcast_fusion.1
  594.3 1.3 maximum_bitcast_fusion
  596.5 1.3 copy.35
  (78 shorter events, 24.5 us)
Async XLA Ops:
  7.2 23.8 %copy-start = (bf16[2,192,1152]{2,1,0:T(8,128)(2,1)S(1)}, bf16[2,192,1152]{2,1,0:T(8,128)(2,1)}, u32[]{:S(2)}) copy-start(bf16[2,192,1152]{2,1,0:T(8,128)(2,1)} %param.16) | copy-start | bytes 2654212
  7.2 453.8 %reduce-scatter.5.cloned.1.call-start = ((), (), s32[]{:S(2)}) async-start(), calls=%async_computation.4 | async-start | bytes 1658880 | tf_op jit(solution)/shard_map/reduce_scatter | solution.py:896
  7.2 58.2 %collective-permute-start.2 = (bf16[2,1152,768]{2,1,0:T(8,128)(2,1)}, bf16[2,1152,768]{2,1,0:T(8,128)(2,1)}, u32[]{:S(2)}, u32[]{:S(2)}) collective-permute-start(bf16[2,1152,768]{2,1,0:T(8,128)(2,1)} %bitcast.75), channel_id=1, source_target_pairs={{0,16},{16,0},{1,17},{17,1},{2,18},{18,2},{3,19},{19,3},{4,20},{20... | collective-permute-start | bytes 10616840 | tf_op jit(solution)/shard_map/ppermute | solution.py:861
  7.3 27.7 %collective-permute-start = (bf16[3,288,1152]{2,1,0:T(8,128)(2,1)}, bf16[3,288,1152]{2,1,0:T(8,128)(2,1)S(1)}, u32[]{:S(2)}, u32[]{:S(2)}) collective-permute-start(bf16[3,288,1152]{2,1,0:T(8,128)(2,1)} %bitcast.80), channel_id=1, source_target_pairs={{0,16},{16,0},{1,17},{17,1},{2,18},{18,2},{3,19},{19,3},{4,20},{20... | collective-permute-start | bytes 5971976 | tf_op jit(solution)/shard_map/ppermute | solution.py:861
  7.8 57.6 %collective-permute-start.3 = (bf16[768,1152]{1,0:T(8,128)(2,1)}, bf16[768,1152]{1,0:T(8,128)(2,1)}, u32[]{:S(2)}, u32[]{:S(2)}) collective-permute-start(bf16[768,1152]{1,0:T(8,128)(2,1)} %bitcast.85), channel_id=1, source_target_pairs={{0,16},{16,0},{1,17},{17,1},{2,18},{18,2},{3,19},{19,3},{4,20},{20... | collective-permute-start | bytes 5308424 | tf_op jit(solution)/shard_map/ppermute | solution.py:861
  7.9 57.5 %collective-permute-start.1 = (bf16[288,1152]{1,0:T(8,128)(2,1)}, bf16[288,1152]{1,0:T(8,128)(2,1)S(1)}, u32[]{:S(2)}, u32[]{:S(2)}) collective-permute-start(bf16[288,1152]{1,0:T(8,128)(2,1)} %bitcast.92), channel_id=1, source_target_pairs={{0,16},{16,0},{1,17},{17,1},{2,18},{18,2},{3,19},{19,3},{4,20},{20... | collective-permute-start | bytes 1990664 | tf_op jit(solution)/shard_map/ppermute | solution.py:861
  31.0 2.6 copy-start.11
  31.0 3.2 copy-start.8
  35.0 1.3 copy-start.2
  65.4 0.8 copy-start.3
  366.6 9.9 %copy-start.10 = (f32[2,12,8,576]{3,2,1,0:T(8,128)S(1)}, f32[2,12,8,576]{3,2,1,0:T(8,128)}, u32[]{:S(2)}) copy-start(f32[2,12,8,576]{3,2,1,0:T(8,128)} %get-tuple-element.114) | copy-start | bytes 1327108
  405.8 72.9 %reduce-scatter.7.cloned.1.call-start = ((), (), s32[]{:S(2)}) async-start(), calls=%async_computation.5 | async-start | bytes 1658880 | tf_op jit(solution)/shard_map/reduce_scatter | solution.py:896
  406.6 126.0 %reduce-scatter.9.cloned.1.call-start = ((), (), s32[]{:S(2)}) async-start(), calls=%async_computation.6 | async-start | bytes 3317760 | tf_op jit(solution)/shard_map/reduce_scatter | solution.py:896
  407.3 2.3 copy-start.13
  407.3 2.3 copy-start.12
  407.3 2.3 copy-start.6
  407.3 2.3 copy-start.7
  407.3 179.7 %reduce-scatter.11.cloned.1.call-start = ((), (), s32[]{:S(2)}) async-start(), calls=%async_computation.7 | async-start | bytes 3317760 | tf_op jit(solution)/shard_map/reduce_scatter | solution.py:896
  407.9 2.1 copy-start.4
  409.8 49.9 %collective-permute-start.5 = (f32[192,1152]{1,0:T(8,128)S(1)}, f32[192,1152]{1,0:T(8,128)S(1)}, u32[]{:S(2)}, u32[]{:S(2)}) collective-permute-start(f32[192,1152]{1,0:T(8,128)S(1)} %get-tuple-element.160), channel_id=1, source_target_pairs={{0,16},{16,0},{1,17},{17,1},{2,18},{18,2},{3,19},{19,3},{4,20},{20... | collective-permute-start | bytes 2654216 | tf_op jit(solution)/shard_map/ppermute | solution.py:861
  412.6 41.4 %copy-start.9 = (bf16[192,1152]{1,0:T(8,128)(2,1)S(1)}, bf16[192,1152]{1,0:T(8,128)(2,1)}, u32[]{:S(2)}) copy-start(bf16[192,1152]{1,0:T(8,128)(2,1)} %get-tuple-element.162) | copy-start | bytes 1327108
  454.0 4.6 collective-permute-start.4
  479.9 110.5 %collective-permute-start.6 = (bf16[144,1152]{1,0:T(8,128)(2,1)S(1)}, bf16[144,1152]{1,0:T(8,128)(2,1)S(1)}, u32[]{:S(2)}, u32[]{:S(2)}) collective-permute-start(bf16[144,1152]{1,0:T(8,128)(2,1)S(1)} %get-tuple-element.164), channel_id=1, source_target_pairs={{0,16},{16,0},{1,17},{17,1},{2,18},{18,2},{3,19},{19,3},{4,20},{20... | collective-permute-start | bytes 995336 | tf_op jit(solution)/shard_map/ppermute | solution.py:861
  589.3 3.7 collective-permute-start.7
  594.3 2.2 copy-start.5
  595.6 2.2 copy-start.1
Sparse Core Ops, SparseCore 0:
  405.9 37.9 reduce-scatter.4
  446.3 32.3 reduce-scatter.6
  481.0 51.4 reduce-scatter.8
  534.7 52.3 reduce-scatter.10

commit v4 on v3

--- a/solution.py
+++ b/solution.py
@@ -51,13 +51,35 @@
     me = lax.axis_index(T)
     near = me + 1 - 2 * (me % 2)
     if square:
-        return me, near, me + 2 - 4 * (me // 2), 3 - me
-    return me, near, 3 - me, (me + 2) % 4
+        return me, near, me + 2 - 4 * (me // 2), 3 - me, True
+    return me, near, 3 - me, (me + 2) % 4, False
+
+
+def nearest_first(place, step):
+    me, low = place[0], ((step + 1) // 2) % 2
+    if place[4]:
+        low = step % 2
+    return (me % 2 + low) % 2 + 2 * ((me // 2 + step // 2) % 2)
+
+
+def farthest_first(place, step):
+    me, low = place[0], ((step + 1) // 2) % 2
+    if place[4]:
+        low = (3 - step) // 2
+    return (me % 2 + low) % 2 + 2 * ((me // 2 + (step + 1) % 2) % 2)
+
+
+def near_first(place, step):
+    me, low = place[0], (3 - step) // 2
+    if place[4]:
+        low = (step + 1) % 2
+    return (me % 2 + low) % 2 + 2 * ((me // 2 + ((step + 1) // 2) % 2) % 2)
 
 
 def greet(place, partner=False):
     sem = pltpu.get_barrier_semaphore()
-    for peer in (place[1], place[2]):
+    peers = (place[1], place[2]) if place else ()
+    for peer in peers:
         pl.semaphore_signal(
             sem, inc=1, device_id={T: peer}, device_id_type=pl.DeviceIdType.MESH
         )
@@ -65,7 +87,7 @@
         pl.semaphore_signal(
             sem, inc=1, device_id={S: 1 - lax.axis_index(S)}, device_id_type=pl.DeviceIdType.MESH
         )
-    pl.semaphore_wait(sem, 3 if partner else 2)
+    pl.semaphore_wait(sem, len(peers) + partner)
 
 
 def remote(src, dst, sems, index, peer):
@@ -83,81 +105,129 @@
     return pl.ds(pl.multiple_of(chunk * rows, rows), rows)
 
 
-def gather(place, mine, whole, sems, base, use, fill=()):
-    me, a, b, d = place
+def repeat(body, times):
+    def one(step, carry):
+        body(step)
+        return carry
+
+    lax.fori_loop(0, times, one, 0)
+
+
+def gather(place, mine, whole, sems, base, use, ready=lambda: None, late=lambda: None, last=None):
+    me, a, b, _, _ = place
     rows = mine.shape[0]
     half = rows // 2
     lo, hi = pl.ds(0, half), pl.ds(half, half)
 
     def part(chunk, upper):
-        return pl.ds(pl.multiple_of(chunk * rows + upper * half, half), half)
-
-    a0 = remote(mine.at[lo], whole.at[part(me, 0)], sems, base, a)
-    b0 = remote(mine.at[hi], whole.at[part(me, 1)], sems, base + 1, b)
-    a1 = remote(mine.at[hi], whole.at[part(me, 1)], sems, base + 2, a)
-    b1 = remote(mine.at[lo], whole.at[part(me, 0)], sems, base + 3, b)
+        return whole.at[pl.ds(pl.multiple_of(chunk * rows + upper * half, half), half)]
+
+    a0 = remote(mine.at[lo], part(me, 0), sems, base, a)
+    b0 = remote(mine.at[hi], part(me, 1), sems, base + 1, b)
+    a1 = remote(mine.at[hi], part(me, 1), sems, base + 2, a)
+    b1 = remote(mine.at[lo], part(me, 0), sems, base + 3, b)
+    b2 = remote(part(a, 0), part(a, 0), sems, base + 4, b)
+    a2 = remote(part(b, 1), part(b, 1), sems, base + 5, a)
     for copy in (a0, b0, a1, b1):
         copy.start()
     whole[chunk_rows(me, rows), :] = mine[...]
-    use(me)
-    for work in fill[:1]:
-        work()
-    a0.wait_recv()
-    b2 = remote(whole.at[part(a, 0)], whole.at[part(a, 0)], sems, base + 4, b)
-    b2.start()
-    b0.wait_recv()
-    a2 = remote(whole.at[part(b, 1)], whole.at[part(b, 1)], sems, base + 5, a)
-    a2.start()
-    a1.wait_recv()
-    use(a)
-    b1.wait_recv()
-    use(b)
-    for work in fill[1:]:
-        work()
-    b2.wait_recv()
-    a2.wait_recv()
-    use(d)
+    ready()
+
+    def final():
+        b2.wait_recv()
+        a2.wait_recv()
+
+    def body(step):
+        @pl.when(step == 1)
+        def _():
+            a0.wait_recv()
+            b2.start()
+            b0.wait_recv()
+            a2.start()
+            a1.wait_recv()
+
+        @pl.when(step == 2)
+        def _():
+            b1.wait_recv()
+
+        if last is None:
+
+            @pl.when(step == 3)
+            def _():
+                late()
+                final()
+
+        use(nearest_first(place, step))
+
+    repeat(body, 4 if last is None else 3)
+    if last is not None:
+        last(final)
     for copy in (a0, b0, a1, b1, a2, b2):
         copy.wait_send()
 
 
-def scatter(place, term, bufs, sems, base, fill=()):
-    me, a, b, d = place
+def scatter(place, term, bufs, sems, base, fill=lambda: None, before=None):
+    _, a, b, _, _ = place
     out, into, keep, own = bufs
     half = keep.shape[1]
     lo, hi = pl.ds(0, half), pl.ds(half, half)
-    out[0] = term(d).astype(BF)
     d0 = remote(out.at[0, lo], into.at[0, lo], sems, base, a)
     d1 = remote(out.at[0, hi], into.at[0, hi], sems, base + 1, b)
-    d0.start()
-    d1.start()
-    total = term(a)
-    out[1, lo] = total[:half].astype(BF)
     a0 = remote(out.at[1, lo], into.at[1, lo], sems, base + 2, a)
-    a0.start()
-    keep[0] = total[half:]
-    total = term(b)
-    out[2, hi] = total[half:].astype(BF)
     b0 = remote(out.at[2, hi], into.at[2, hi], sems, base + 3, b)
-    b0.start()
-    keep[1] = total[:half]
-    own[...] = term(me)
-    for work in fill[:1]:
-        work()
+    a1 = remote(out.at[1, hi], into.at[1, hi], sems, base + 4, a)
+    b1 = remote(out.at[2, lo], into.at[2, lo], sems, base + 5, b)
+    at = (0, 1, 2) if before is None else (2, 0, 1)
+
+    def body(step):
+        if before is None:
+            chunk = farthest_first(place, step)
+        else:
+            chunk = near_first(place, step)
+            pl.when(step == 2)(before)
+        own[...] = term(chunk)
+
+        @pl.when(step == at[0])
+        def _():
+            out[0] = own[...].astype(BF)
+            d0.start()
+            d1.start()
+
+        @pl.when(step == at[1])
+        def _():
+            out[1, lo] = own[lo].astype(BF)
+            a0.start()
+            keep[0] = own[hi]
+
+        @pl.when(step == at[2])
+        def _():
+            out[2, hi] = own[hi].astype(BF)
+            b0.start()
+            keep[1] = own[lo]
+
+    repeat(body, 4)
     d1.wait_recv()
     out[1, hi] = (keep[0] + into[0, hi].astype(F32)).astype(BF)
-    a1 = remote(out.at[1, hi], into.at[1, hi], sems, base + 4, a)
     a1.start()
     d0.wait_recv()
     out[2, lo] = (keep[1] + into[0, lo].astype(F32)).astype(BF)
-    b1 = remote(out.at[2, lo], into.at[2, lo], sems, base + 5, b)
     b1.start()
-    for work in fill[1:]:
-        work()
+    fill()
     for copy in (a0, b0, a1, b1):
         copy.wait_recv()
     for copy in (d0, d1, a0, b0, a1, b1):
         copy.wait_send()
+
+
+def gather_scatter(place, mine, whole, sems, base, use, term, bufs, ready, fill=lambda: None):
+    def last(final):
+        def before():
+            final()
+            use(place[3])
+
+        scatter(place, term, bufs, sems, base + 6, fill, before)
+
+    gather(place, mine, whole, sems, base, use, ready, last=last)
 
 
 def scattered(bufs, rows):
@@ -257,18 +327,17 @@
     dmod[2 * block + 1] += sums[:, half:]
 
 
-def weight_grad(x, y, flipped, col, packs, index):
+def weight_grad(x, y, flipped, col, packs):
     mine, theirs, _ = packs
     dp, part, _ = mine.shape
     first = lax.axis_index(S) == 0
     width = y.shape[1]
-    block = 256 if width % 256 == 0 else width
     if x is not None:
         flipped[...] = x[...].T
-    for i in range(width // block):
-        to = pl.ds(col + i * block, block)
-        grad = nn(flipped[...], y[:, pl.ds(i * block, block)]).astype(BF)
-        grad = grad.reshape(dp, 2, part, block)
+
+    def one(to, columns):
+        grad = nn(flipped[...], columns).astype(BF)
+        grad = grad.reshape(dp, 2, part, columns.shape[1])
 
         @pl.when(first)
         def _():
@@ -280,22 +349,34 @@
             mine[:, :, to] = grad[:, 1]
             theirs[:, :, to] = grad[:, 0]
 
-    return index, col, width
-
-
-def send_half(packs, sems, job):
-    index, col, width = job
+    if width % 256:
+        one(pl.ds(col, width), y[...])
+        return
+
+    def body(i, carry):
+        at = pl.multiple_of(i * 256, 256)
+        one(pl.ds(pl.multiple_of(col + at, 256), 256), y[:, pl.ds(at, 256)])
+        return carry
+
+    lax.fori_loop(0, width // 256, body, 0)
+
+
+def send_half(packs, sems, index, col, width):
     at = pl.ds(col, width)
     return push(
         packs[1].at[:, :, at], packs[2].at[:, :, at], sems, index, {S: 1 - lax.axis_index(S)}
     )
 
 
-def add_halves(packs, copies, total):
+def add_halves(packs, copies, total, col, width):
+    at = pl.ds(col, width)
     for copy in copies:
         copy.wait_recv()
-    for k in range(total.shape[0]):
-        total[k] = (packs[0][k].astype(F32) + packs[2][k].astype(F32)).astype(BF)
+
+    def body(k):
+        total[k, :, at] = (packs[0][k, :, at].astype(F32) + packs[2][k, :, at].astype(F32)).astype(BF)
+
+    repeat(body, total.shape[0])
     for copy in copies:
         copy.wait_send()
 
@@ -330,12 +411,8 @@
         h[rows] = (normal * (1.0 + scale) + shift).astype(BF)
 
     over_blocks(x.shape[0], prepare)
-    waited = []
 
     def use(chunk):
-        if not waited:
-            arrive(load)
-            waited.append(1)
         rows = chunk_rows(chunk, x.shape[0])
         cosine = twice(both[rows, 0:PAD])
         sine = twice(both[rows, PAD : 2 * PAD])
@@ -349,11 +426,11 @@
                 dst[rows, lanes] = (gained * cosine + two(nn, gained, turn[...]) * sine).astype(BF)
         v[rows] = nt(whole[rows], w[2]).astype(BF)
 
-    gather(place, h, whole, (ssem, rsem), 0, use)
-
-
-def mlp_kernel(layer, square, att, x, sel, mod, wo0, wo1, wg0, wg1, wd0, wd1, br1, x1, whole,
-               gate, up, hidden, br2, y, h, wo, wg, wd, o1, i1, k1, s1, o2, i2, k2, s2,
+    gather(place, h, whole, (ssem, rsem), 0, use, lambda: arrive(load))
+
+
+def mlp_kernel(layer, square, att, x, sel, mod, wo0, wo1, wg0, wg1, wd0, wd1, br1, x1, br2, y,
+               whole_h, gate_h, up_h, hidden_h, whole, gate, up, hidden, h, wo, wg, wd, o1, i1, k1, s1, o2, i2, k2, s2,
                ssem, rsem, wsem, osem):
     place = ring(square)
     rows_here, _ = x.shape
@@ -377,7 +454,6 @@
         h[rows] = (normal * (1.0 + scale) + shift).astype(BF)
 
     over_blocks(rows_here, between)
-    load_g.wait()
 
     def use(chunk):
         rows = chunk_rows(chunk, rows_here)
@@ -386,10 +462,25 @@
         g = gate[rows]
         hidden[rows] = (g * jax.nn.sigmoid(g) * up[rows]).astype(BF)
 
-    gather(place, h, whole, sems, 6, use)
-    load_d.wait()
     second = (o2, i2, k2, s2)
-    scatter(place, lambda c: nn(hidden[chunk_rows(c, rows_here)], wd[...]), second, sems, 12)
+    stores = []
+    for n, (src, dst) in enumerate(
+        ((whole, whole_h), (gate, gate_h), (up, up_h), (hidden, hidden_h))
+    ):
+        stores.append(pltpu.make_async_copy(src, dst, wsem.at[3 + n]))
+
+    def ready():
+        load_g.wait()
+        load_d.wait()
+
+    def fill():
+        for copy in stores:
+            copy.start()
+
+    def term(chunk):
+        return nn(hidden[chunk_rows(chunk, rows_here)], wd[...])
+
+    gather_scatter(place, h, whole, sems, 6, use, term, second, ready, fill)
 
     def finish(rows):
         branch = scattered(second, rows)
@@ -397,6 +488,7 @@
         y[rows] = (x1[rows] + mod_rows(sel[rows], mod, 5) * branch).astype(BF)
 
     over_blocks(rows_here, finish)
+    arrive(stores)
 
 
 def mlp_back_kernel(layer, square, dy, br2, br1, x1, sel, mod, gate_h, up_h, hidden_h, rows_h,
@@ -426,14 +518,11 @@
         add_sums(dmod, 3, sel[rows], incoming * br2[rows])
 
     over_blocks(rows_here, prepare)
-    waited = []
+
+    def ready():
+        arrive((load_d, load_gate, load_up, load_g, load_hidden))
 
     def use(chunk):
-        if not waited:
-            load_d.wait()
-            load_gate.wait()
-            load_up.wait()
-            waited.append(1)
         rows = chunk_rows(chunk, rows_here)
         d_hidden = nt(whole2[rows], wd[...])
         g = gate[rows]
@@ -441,9 +530,6 @@
         dgate[rows] = (d_hidden * up[rows] * s * (1.0 + g * (1.0 - s))).astype(BF)
         dup[rows] = (d_hidden * g * s).astype(BF)
 
-    gather(place, h, whole2, sems, 0, use)
-    load_g.wait()
-    load_hidden.wait()
     bufs = (o1, i1, k1, s1)
     f = hidden.shape[1]
 
@@ -455,13 +541,13 @@
     copies = []
 
     def grad(index, x, y, col):
-        job = weight_grad(x, y, flipped, col, packs, index)
-        copies.append(send_half(packs, sems, job))
+        weight_grad(x, y, flipped, col, packs)
+        copies.append(send_half(packs, sems, index, col, f))
 
     def grad_down():
         grad(18, whole2, hidden, 2 * f)
 
-    scatter(place, term, bufs, sems, 6, (grad_down,))
+    gather_scatter(place, h, whole2, sems, 0, use, term, bufs, ready, grad_down)
 
     def between(rows):
         d_h = scattered(bufs, rows)
@@ -470,26 +556,34 @@
         d_mixed = dy[rows].astype(F32) + norm_back(d_h * (1.0 + scale), normal, inverse)
         dx1[rows] = d_mixed
         h1[rows] = (d_mixed * mod_rows(sel[rows], mod, 2)).astype(BF)
-        add_sums(dmod, 1, sel[rows], d_h)
-        add_sums(dmod, 2, sel[rows], d_h * normal)
-        add_sums(dmod, 0, sel[rows], d_mixed * br1[rows])
 
     over_blocks(rows_here, between)
-    arrive(load_o)
-    load_rows.wait()
 
     def use_out(chunk):
         rows = chunk_rows(chunk, rows_here)
         datt[rows] = nt(whole1[rows], wo[...]).astype(BF)
 
-    def grad_gate():
+    def sums():
+        def one(rows):
+            d_h = scattered(bufs, rows)
+            normal, _ = normed(x1[rows])
+            add_sums(dmod, 1, sel[rows], d_h)
+            add_sums(dmod, 2, sel[rows], d_h * normal)
+            add_sums(dmod, 0, sel[rows], dx1[rows] * br1[rows])
+
+        over_blocks(rows_here, one)
+        arrive(load_o)
+        load_rows.wait()
         grad(19, saved, dgate, 0)
 
-    def grad_up():
-        grad(20, None, dup, f)
-
-    gather(place, h1, whole1, sems, 12, use_out, (grad_gate, grad_up))
-    add_halves(packs, copies, total)
+    def late():
+        weight_grad(None, dup, flipped, f, packs)
+
+    gather(place, h1, whole1, sems, 12, use_out, sums, late)
+    copies.append(send_half(packs, sems, 20, f, f))
+    add_halves(packs, copies[:1], total, 2 * f, f)
+    add_halves(packs, copies[1:2], total, 0, f)
+    add_halves(packs, copies[2:], total, f, f)
 
 
 def qkv_back_kernel(layer, square, dq, dk, dv, proj, gain, both, turn, ones, spread, x, dx1, sel,
@@ -537,16 +631,20 @@
         loads[0].wait()
         for k in range(3):
             flat[...] = nt(dproj[k] if k < 2 else dv[...], spread[...]).astype(BF)
-            weight_grad(None if k else whole, flat, flipped, k * packed, packs, 6)
+            weight_grad(None if k else whole, flat, flipped, k * packed, packs)
 
     def grad_out():
         loads[1].wait()
         loads[2].wait()
         flat[...] = nt(att[...], spread[...]).astype(BF)
-        weight_grad(rows1, flat, flipped, 3 * packed, packs, 6)
-        copies.append(send_half(packs, sems, (6, 0, 4 * packed)))
-
-    scatter(place, term, bufs, sems, 0, (grad_in, grad_out))
+        weight_grad(rows1, flat, flipped, 3 * packed, packs)
+
+    def grads():
+        grad_in()
+        grad_out()
+        copies.append(send_half(packs, sems, 6, 0, 4 * packed))
+
+    scatter(place, term, bufs, sems, 0, grads)
 
     def finish(rows):
         d_h = scattered(bufs, rows)
@@ -559,7 +657,7 @@
         add_sums(here, 1, sel[rows], d_h * normal)
 
     over_blocks(rows_here, finish)
-    add_halves(packs, copies, total)
+    add_halves(packs, copies, total, 0, 4 * packed)
 
 
 def cell():
@@ -738,13 +836,15 @@
     return pl.CostEstimate(flops=0, bytes_accessed=int(micros * 3.5e6), transcendentals=0)
 
 
-def ring_call(kernel, ident, micros, outs, scratch, args, spaces, scalar=-1):
+def ring_call(kernel, ident, micros, outs, scratch, args, spaces, scalar=-1, loose=99):
     return pl.pallas_call(
         kernel,
         out_shape=outs,
         in_specs=[vmem() if s else anywhere() for s in spaces],
         out_specs=[
-            pl.BlockSpec(memory_space=pltpu.SMEM) if n == scalar else vmem()
+            pl.BlockSpec(memory_space=pltpu.SMEM)
+            if n == scalar
+            else (vmem() if n < loose else anywhere())
             for n in range(len(outs))
         ],
         scratch_shapes=scratch,
@@ -763,14 +863,17 @@
         for n in range(wide // PAD):
             fn(slice(n * PAD, (n + 1) * PAD))
 
-    for item in range(3):
+    def one_item(item, carry):
         at = pl.ds(pl.multiple_of(spans[item], 16), TILE)
         valid = lax.broadcasted_iota(jnp.int32, (TILE, TILE), 1) < spans[4 + item]
 
-        def tile(lanes, at=at, valid=valid):
+        def tile(lanes):
             att[at, lanes] = softmax_rows(q[at, lanes], k[at, lanes], v[at, lanes], valid, scale)
 
         each_head(tile)
+        return carry
+
+    lax.fori_loop(0, 3, one_item, 0)
     first = rows - 48
     start = spans[3]
     at = pl.ds(first, 48)
@@ -815,12 +918,12 @@
         for n in range(wide // PAD):
             fn(slice(n * PAD, (n + 1) * PAD))
 
-    for item in range(3):
+    def one_item(item, carry):
         at = pl.ds(pl.multiple_of(spans[item], 16), TILE)
         keys = lax.broadcasted_iota(jnp.int32, (TILE, TILE), 0) < spans[4 + item]
         queries = lax.broadcasted_iota(jnp.int32, (TILE, TILE), 1) < spans[4 + item]
 
-        def tile(lanes, at=at, keys=keys, queries=queries):
+        def tile(lanes):
             parts = back_tile(
                 q[at, lanes], k[at, lanes], v[at, lanes], grad[at, lanes], keys, queries, scale
             )
@@ -828,6 +931,9 @@
                 dst[at, lanes] = new.astype(BF)
 
         each_head(tile)
+        return carry
+
+    lax.fori_loop(0, 3, one_item, 0)
     first = rows - 48
     start = spans[3]
     at = pl.ds(first, 48)
@@ -981,21 +1087,25 @@
             spans,
             (q, k, v),
         )
-        br1, x1, whole2, gate, up, hidden, br2, y = ring_call(
+        br1, x1, br2, y, whole2, gate, up, hidden = ring_call(
             functools.partial(mlp_kernel, layer, square),
             2 + layer,
             48,
             [
                 sds((rows, width), F32),
                 sds((rows, width), F32),
+                sds((rows, width), F32),
+                sds((rows, width), BF),
                 sds((seq, width), BF),
                 sds((seq, hidden_here), F32),
                 sds((seq, hidden_here), F32),
                 sds((seq, hidden_here), BF),
-                sds((rows, width), F32),
-                sds((rows, width), BF),
             ],
             [
+                pltpu.VMEM((seq, width), BF),
+                pltpu.VMEM((seq, hidden_here), F32),
+                pltpu.VMEM((seq, hidden_here), F32),
+                pltpu.VMEM((seq, hidden_here), BF),
                 pltpu.VMEM((rows, width), BF),
                 pltpu.VMEM((wide, width), BF),
                 pltpu.VMEM((2, width, hidden_here), BF),
@@ -1004,9 +1114,10 @@
             + scatter_scratch(rows, width)
             + scatter_scratch(rows, width)
             + dma_sems(18)
-            + [pltpu.SemaphoreType.DMA((3,)), pltpu.SemaphoreType.DMA((heads,))],
+            + [pltpu.SemaphoreType.DMA((7,)), pltpu.SemaphoreType.DMA((heads,))],
             (att, x, sel, mod, own[1], other[1], own[2], other[2], own[3], other[3]),
             (1, 1, 1, 1) + (0,) * 6,
+            loose=4,
         )
         kept.append((x, whole1, proj, q, k, v, att, br1, x1, whole2, gate, up, hidden, br2, y))
         x = y

time: 608 us -> 597 us (0.982)
  Pallas kernels: 419 us -> 407 us
    pallas_call x10, Pallas kernels: 389 us -> 373 us  [ring_call(): pl.pallas_call(kernel, out_shape=outs, in_specs=[vmem() if s else anywher...]
  transfers between devices with their start and end apart: 12 -> 12, of which waited for: 3 -> 3; matrix products, arithmetic and copies ran while one was open for 5% -> 5% of each run, Pallas kernels for 13% -> 14%
where the time goes in v4:
time: 597 us; the launch traced here: 593 us
  Pallas kernels  407 us (68%)
  waiting for transfers between devices  125 us (21%)
  local copies, waits for them, and re-layouts  22.3 us (4%)
  other arithmetic  17.9 us (3%)
  between operations  14.3 us (2%)
    pallas_call x10, Pallas kernels, ring_call(): pl.pallas_call(kernel, out_shape=outs, in_specs=[vmem() if s else anywher...  373 us
    reduce_scatter x4, waiting for transfers between devices, reduced(): return lax.psum_scatter(total, DP, scatter_dimension=0, tiled=True)[0]  124 us
    pallas_call x4, Pallas kernels, local_call(): pl.pallas_call(kernel, out_shape=outs, in_specs=[pl.BlockSpec(memory_spac...  34.9 us
  transfers between devices with their start and end apart: 12, of which 3 were waited for; matrix products, arithmetic and copies ran while one was open for 5% of the time, Pallas kernels for 14%

profile of v4, /device:TPU:1, one launch (start us, length us, event | category | flops | bytes accessed | tf_op | source)
XLA Modules:
  0.0 592.9 jit_solution(8712772364355710352)
XLA Ops:
  8.3 1.3 fusion.6
  9.7 1.3 reshape.178
  13.7 1.4 bitcast_convert_fusion.lifted
  15.0 15.9 %shard_map.231 = (f32[2,6,8,1152]{3,2,1,0:T(8,128)}, f32[4,16,1152]{2,1,0:T(8,128)}, f32[2,8,128]{2,1,0:T(8,128)}, f32[192,8]{1,0:T(8,128)}, f32[768,256]{1,0:T(8,128)}, /*index=5*/s32[8]{0:T(128)}) custom-call(f32[16,1152]{1,0:T(8,128)} %bitcast_convert_fusion.lifted, bf16[1728,1152]{1,0:T(8,128)(2,1)} %bitcast.90, f32[3,1,576]{2,1,0:T(1,128)} %reshape.191.bias, ...), custom_call_target="tpu_custom_call" | custom-call | bytes 42000000 | tf_op jit(solution)/shard_map/pallas_call | solution.py:840
  31.8 1.8 dynamic-slice_bitcast_fusion.dy
  36.3 23.6 %shard_map.232 = (bf16[768,1152]{1,0:T(8,128)(2,1)}, bf16[2,768,512]{2,1,0:T(8,128)(2,1)}, bf16[768,512]{1,0:T(8,128)(2,1)}, bf16[768,512]{1,0:T(8,128)(2,1)}, bf16[768,512]{1,0:T(8,128)(2,1)}) custom-call(bf16[192,1152]{1,0:T(8,128)(2,1)} %dynamic-slice_bitcast_fusion.1.x, f32[192,8]{1,0:T(8,128)} %get-tuple-element.71.sel, ...), custom_call_target="tpu_custom_call" | custom-call | bytes 70000000 | tf_op jit(solution)/shard_map/pallas_call | solution.py:840
  59.9 6.6 %shard_map.233.att.att_h = bf16[768,512]{1,0:T(8,128)(2,1)} custom-call(s32[8]{0:T(128)} %get-tuple-element.70.spans, bf16[768,512]{1,0:T(8,128)(2,1)} %get-tuple-element.75.q, bf16[768,512]{1,0:T(8,128)(2,1)} %get-tuple-element.76.k, bf16[768,512]{1,0:T(8,128)(2,1)} %get-tuple-element.77.v), custom_call_target="tpu_custom_call" | custom-call | bytes 21000000 | tf_op jit(solution)/shard_map/pallas_call | solution.py:955
  67.3 49.1 %shard_map.234 = (f32[192,1152]{1,0:T(8,128)}, f32[192,1152]{1,0:T(8,128)}, f32[192,1152]{1,0:T(8,128)}, bf16[192,1152]{1,0:T(8,128)(2,1)}, bf16[768,1152]{1,0:T...) custom-call(bf16[768,512]{1,0:T(8,128)(2,1)} %shard_map.233.att.att_h, ...), custom_call_target="tpu_custom_call" | custom-call | bytes 168000000 | tf_op jit(solution)/shard_map/pallas_call | solution.py:840
  116.5 18.9 %shard_map.235 = (bf16[768,1152]{1,0:T(8,128)(2,1)}, bf16[2,768,512]{2,1,0:T(8,128)(2,1)}, bf16[768,512]{1,0:T(8,128)(2,1)}, bf16[768,512]{1,0:T(8,128)(2,1)}, bf16[768,512]{1,0:T(8,128)(2,1)}) custom-call(bf16[192,1152]{1,0:T(8,128)(2,1)} %get-tuple-element.78.x, f32[192,8]{1,0:T(8,128)} %get-tuple-element.71.sel, f32[6,8,1152]{2,1,0:T(8,128)} %get-tuple-element.165.mod, ...), custom_call_target="tpu_custom_call" | custom-call | bytes 70000000 | tf_op jit(solution)/shard_map/pallas_call | solution.py:840
  135.4 6.6 %shard_map.236.att.att_h = bf16[768,512]{1,0:T(8,128)(2,1)} custom-call(s32[8]{0:T(128)} %get-tuple-element.70.spans, bf16[768,512]{1,0:T(8,128)(2,1)} %get-tuple-element.79.q, bf16[768,512]{1,0:T(8,128)(2,1)} %get-tuple-element.80.k, bf16[768,512]{1,0:T(8,128)(2,1)} %get-tuple-element.81.v), custom_call_target="tpu_custom_call" | custom-call | bytes 21000000 | tf_op jit(solution)/shard_map/pallas_call | solution.py:955
  142.0 47.3 %shard_map.237 = (f32[192,1152]{1,0:T(8,128)}, f32[192,1152]{1,0:T(8,128)}, f32[192,1152]{1,0:T(8,128)}, bf16[192,1152]{1,0:T(8,128)(2,1)}, bf16[768,1152]{1,0:T...) custom-call(bf16[768,512]{1,0:T(8,128)(2,1)} %shard_map.236.att.att_h, ...), custom_call_target="tpu_custom_call" | custom-call | bytes 168000000 | tf_op jit(solution)/shard_map/pallas_call | solution.py:840
  189.3 67.4 %shard_map.238 = (bf16[768,1152]{1,0:T(8,128)(2,1)}, bf16[768,512]{1,0:T(8,128)(2,1)}, f32[192,1152]{1,0:T(8,128)}, f32[8,8,576]{2,1,0:T(8,128)}, bf16[4,144,2304]{2,1,0:T(8,128)(2,1)}) custom-call(bf16[192,1152]{1,0:T(8,128)(2,1)} %dynamic-slice_bitcast_fusion.dy, f32[192,1152]{1,0:T(8,128)} %get-tuple-element.83.br2, f32[192,1152]{1,0:T(8,128)} %get-tuple-element.84.br1, ...), custom_call_target="tpu_custom_call" | custom-call | bytes 182000000 | tf_op jit(solution)/shard_map/pallas_call | solution.py:840
  256.7 10.8 %shard_map.239 = (bf16[768,512]{1,0:T(8,128)(2,1)}, bf16[768,512]{1,0:T(8,128)(2,1)}, bf16[768,512]{1,0:T(8,128)(2,1)}) custom-call(s32[8]{0:T(128)} %get-tuple-element.70.spans, bf16[768,512]{1,0:T(8,128)(2,1)} %get-tuple-element.79.q, bf16[768,512]{1,0:T(8,128)(2,1)} %get-tuple-element.80.k, bf16[768,512]{1,0:T(8,128)(2,1)} %get-tuple-element.81.v, ...), custom_call_target="tpu_custom_call" | custom-call | bytes 35000000 | tf_op jit(solution)/shard_map/pallas_call | solution.py:955
  268.3 27.1 %shard_map.240 = (f32[192,1152]{1,0:T(8,128)}, bf16[192,1152]{1,0:T(8,128)(2,1)}, f32[2,12,8,576]{3,2,1,0:T(8,128)}, bf16[4,144,1152]{2,1,0:T(8,128)(2,1)}, f32[2,1,512]{2,1,0:T(1,128)}) custom-call(bf16[768,512]{1,0:T(8,128)(2,1)} %get-tuple-element.91.dq, bf16[768,512]{1,0:T(8,128)(2,1)} %get-tuple-element.92.dk, bf16[768,512]{1,0:T(8,128)(2,1)} %get-tuple-element.93.dv, ...), custom_call_target="tpu_custom_call" | custom-call | bytes 77000000 | tf_op jit(solution)/shard_map/pallas_call | solution.py:840
  295.4 57.3 %shard_map.241 = (bf16[768,1152]{1,0:T(8,128)(2,1)}, bf16[768,512]{1,0:T(8,128)(2,1)}, f32[192,1152]{1,0:T(8,128)}, f32[8,8,576]{2,1,0:T(8,128)}, bf16[4,144,2304]{2,1,0:T(8,128)(2,1)}) custom-call(bf16[192,1152]{1,0:T(8,128)(2,1)} %get-tuple-element.99.dy, f32[192,1152]{1,0:T(8,128)} %get-tuple-element.100.br2, f32[192,1152]{1,0:T(8,128)} %get-tuple-element.101.br1, ...), custom_call_target="tpu_custom_call" | custom-call | bytes 182000000 | tf_op jit(solution)/shard_map/pallas_call | solution.py:840
  352.6 10.9 %shard_map.242 = (bf16[768,512]{1,0:T(8,128)(2,1)}, bf16[768,512]{1,0:T(8,128)(2,1)}, bf16[768,512]{1,0:T(8,128)(2,1)}) custom-call(s32[8]{0:T(128)} %get-tuple-element.70.spans, bf16[768,512]{1,0:T(8,128)(2,1)} %get-tuple-element.75.q, bf16[768,512]{1,0:T(8,128)(2,1)} %get-tuple-element.76.k, bf16[768,512]{1,0:T(8,128)(2,1)} %get-tuple-element.77.v, ...), custom_call_target="tpu_custom_call" | custom-call | bytes 35000000 | tf_op jit(solution)/shard_map/pallas_call | solution.py:955
  364.3 28.1 %shard_map.243 = (f32[192,1152]{1,0:T(8,128)}, bf16[192,1152]{1,0:T(8,128)(2,1)}, f32[2,12,8,576]{3,2,1,0:T(8,128)}, bf16[4,144,1152]{2,1,0:T(8,128)(2,1)}, f32[2,1,512]{2,1,0:T(1,128)}) custom-call(bf16[768,512]{1,0:T(8,128)(2,1)} %get-tuple-element.108.dq, bf16[768,512]{1,0:T(8,128)(2,1)} %get-tuple-element.109.dk, ...), custom_call_target="tpu_custom_call" | custom-call | bytes 77000000 | tf_op jit(solution)/shard_map/pallas_call | solution.py:840
  394.5 1.7 constant_dynamic-slice_fusion
  397.0 1.9 select_bitcast_fusion.2
  399.4 37.8 %shard_map.244 = (f32[288,1728]{1,0:T(8,128)}, f32[3,1,576]{2,1,0:T(1,128)}, f32[2,8,1152]{2,1,0:T(8,128)}, f32[8,512]{1,0:T(8,128)}) custom-call(f32[2,12,8,576]{3,2,1,0:T(8,128)} %get-tuple-element.118.dmod, f32[2,8,512]{2,1,0:T(8,128)} %pad.18.dgain, f32[8,8,288]{2,1,0:T(8,128)} %bitcast.100, bf16[1728,1152]{1,0:T(8,128)(2,1)} %bitcast.91), custom_call_target="tpu_custom_call" | custom-call | bytes 52500000 | tf_op jit(solution)/shard_map/pallas_call | solution.py:840
  437.2 1.5 slice.54
  438.7 1.4 reshape.185
  442.3 1.4 collective-permute-start.4
  443.7 1.3 dynamic_slice.16
  445.6 1.4 fusion.8
  448.1 1.3 maximum_select_fusion
  449.4 17.6 %reduce-scatter.7.cloned.1.call-done = bf16[1,144,1152]{2,1,0:T(8,128)(2,1)} async-done(((bf16[4,144,1152]{2,1,0:T(8,128)(2,1)}), bf16[1,144,1152]{2,1,0:T(8,128)(2,1)}) %reduce-scatter.7.cloned.1.call-update) | async-done | bytes 331792 | tf_op jit(solution)/shard_map/reduce_scatter | solution.py:1002
  469.3 51.5 %reduce-scatter.9.cloned.1.call-done = bf16[1,144,2304]{2,1,0:T(8,128)(2,1)} async-done(((bf16[4,144,2304]{2,1,0:T(8,128)(2,1)}), bf16[1,144,2304]{2,1,0:T(8,128)(2,1)}) %reduce-scatter.9.cloned.1.call-update) | async-done | bytes 663568 | tf_op jit(solution)/shard_map/reduce_scatter | solution.py:1002
  520.8 54.5 %reduce-scatter.11.cloned.1.call-done = bf16[1,144,2304]{2,1,0:T(8,128)(2,1)} async-done(((bf16[4,144,2304]{2,1,0:T(8,128)(2,1)}), bf16[1,144,2304]{2,1,0:T(8,128)(2,1)}) %reduce-scatter.11.cloned.1.call-update) | async-done | bytes 663568 | tf_op jit(solution)/shard_map/reduce_scatter | solution.py:1002
  575.4 2.2 select_bitcast_fusion.1
  582.6 1.3 maximum_bitcast_fusion
  584.8 1.3 copy.35
  (78 shorter events, 24.9 us)
Async XLA Ops:
  7.2 23.8 %copy-start = (bf16[2,192,1152]{2,1,0:T(8,128)(2,1)S(1)}, bf16[2,192,1152]{2,1,0:T(8,128)(2,1)}, u32[]{:S(2)}) copy-start(bf16[2,192,1152]{2,1,0:T(8,128)(2,1)} %param.16) | copy-start | bytes 2654212
  7.2 442.2 %reduce-scatter.5.cloned.1.call-start = ((), (), s32[]{:S(2)}) async-start(), calls=%async_computation.4 | async-start | bytes 1658880 | tf_op jit(solution)/shard_map/reduce_scatter | solution.py:1002
  7.2 59.3 %collective-permute-start.2 = (bf16[2,1152,768]{2,1,0:T(8,128)(2,1)}, bf16[2,1152,768]{2,1,0:T(8,128)(2,1)}, u32[]{:S(2)}, u32[]{:S(2)}) collective-permute-start(bf16[2,1152,768]{2,1,0:T(8,128)(2,1)} %bitcast.75), channel_id=1, source_target_pairs={{0,16},{16,0},{1,17},{17,1},{2,18},{18,2},{3,19},{19,3},{4,20},{20... | collective-permute-start | bytes 10616840 | tf_op jit(solution)/shard_map/ppermute | solution.py:967
  7.3 27.7 %collective-permute-start = (bf16[3,288,1152]{2,1,0:T(8,128)(2,1)}, bf16[3,288,1152]{2,1,0:T(8,128)(2,1)S(1)}, u32[]{:S(2)}, u32[]{:S(2)}) collective-permute-start(bf16[3,288,1152]{2,1,0:T(8,128)(2,1)} %bitcast.80), channel_id=1, source_target_pairs={{0,16},{16,0},{1,17},{17,1},{2,18},{18,2},{3,19},{19,3},{4,20},{20... | collective-permute-start | bytes 5971976 | tf_op jit(solution)/shard_map/ppermute | solution.py:967
  7.8 58.7 %collective-permute-start.3 = (bf16[768,1152]{1,0:T(8,128)(2,1)}, bf16[768,1152]{1,0:T(8,128)(2,1)}, u32[]{:S(2)}, u32[]{:S(2)}) collective-permute-start(bf16[768,1152]{1,0:T(8,128)(2,1)} %bitcast.85), channel_id=1, source_target_pairs={{0,16},{16,0},{1,17},{17,1},{2,18},{18,2},{3,19},{19,3},{4,20},{20... | collective-permute-start | bytes 5308424 | tf_op jit(solution)/shard_map/ppermute | solution.py:967
  7.9 58.6 %collective-permute-start.1 = (bf16[288,1152]{1,0:T(8,128)(2,1)}, bf16[288,1152]{1,0:T(8,128)(2,1)S(1)}, u32[]{:S(2)}, u32[]{:S(2)}) collective-permute-start(bf16[288,1152]{1,0:T(8,128)(2,1)} %bitcast.92), channel_id=1, source_target_pairs={{0,16},{16,0},{1,17},{17,1},{2,18},{18,2},{3,19},{19,3},{4,20},{20... | collective-permute-start | bytes 1990664 | tf_op jit(solution)/shard_map/ppermute | solution.py:967
  31.0 2.6 copy-start.11
  31.0 3.2 copy-start.8
  35.0 1.3 copy-start.2
  66.5 0.8 copy-start.3
  352.6 10.9 %copy-start.10 = (f32[2,12,8,576]{3,2,1,0:T(8,128)S(1)}, f32[2,12,8,576]{3,2,1,0:T(8,128)}, u32[]{:S(2)}) copy-start(f32[2,12,8,576]{3,2,1,0:T(8,128)} %get-tuple-element.114) | copy-start | bytes 1327108
  392.4 74.6 %reduce-scatter.7.cloned.1.call-start = ((), (), s32[]{:S(2)}) async-start(), calls=%async_computation.5 | async-start | bytes 1658880 | tf_op jit(solution)/shard_map/reduce_scatter | solution.py:1002
  393.2 127.7 %reduce-scatter.9.cloned.1.call-start = ((), (), s32[]{:S(2)}) async-start(), calls=%async_computation.6 | async-start | bytes 3317760 | tf_op jit(solution)/shard_map/reduce_scatter | solution.py:1002
  393.9 2.3 copy-start.13
  393.9 2.3 copy-start.12
  393.9 2.3 copy-start.6
  393.9 2.3 copy-start.7
  393.9 181.4 %reduce-scatter.11.cloned.1.call-start = ((), (), s32[]{:S(2)}) async-start(), calls=%async_computation.7 | async-start | bytes 3317760 | tf_op jit(solution)/shard_map/reduce_scatter | solution.py:1002
  394.5 2.4 copy-start.4
  396.4 51.7 %collective-permute-start.5 = (f32[192,1152]{1,0:T(8,128)S(1)}, f32[192,1152]{1,0:T(8,128)S(1)}, u32[]{:S(2)}, u32[]{:S(2)}) collective-permute-start(f32[192,1152]{1,0:T(8,128)S(1)} %get-tuple-element.160), channel_id=1, source_target_pairs={{0,16},{16,0},{1,17},{17,1},{2,18},{18,2},{3,19},{19,3},{4,20},{20... | collective-permute-start | bytes 2654216 | tf_op jit(solution)/shard_map/ppermute | solution.py:967
  399.4 42.8 %copy-start.9 = (bf16[192,1152]{1,0:T(8,128)(2,1)S(1)}, bf16[192,1152]{1,0:T(8,128)(2,1)}, u32[]{:S(2)}) copy-start(bf16[192,1152]{1,0:T(8,128)(2,1)} %get-tuple-element.162) | copy-start | bytes 1327108
  442.3 4.7 collective-permute-start.4
  468.2 110.5 %collective-permute-start.6 = (bf16[144,1152]{1,0:T(8,128)(2,1)S(1)}, bf16[144,1152]{1,0:T(8,128)(2,1)S(1)}, u32[]{:S(2)}, u32[]{:S(2)}) collective-permute-start(bf16[144,1152]{1,0:T(8,128)(2,1)S(1)} %get-tuple-element.164), channel_id=1, source_target_pairs={{0,16},{16,0},{1,17},{17,1},{2,18},{18,2},{3,19},{19,3},{4,20},{20... | collective-permute-start | bytes 995336 | tf_op jit(solution)/shard_map/ppermute | solution.py:967
  577.6 3.7 collective-permute-start.7
  582.6 2.2 copy-start.5
  583.9 2.2 copy-start.1
Sparse Core Ops, SparseCore 0:
  392.5 39.3 reduce-scatter.4
  434.3 32.7 reduce-scatter.6
  469.3 51.4 reduce-scatter.8
  523.0 52.3 reduce-scatter.10

commit v5 on v4

--- a/solution.py
+++ b/solution.py
@@ -55,11 +55,26 @@
     return me, near, 3 - me, (me + 2) % 4, False
 
 
-def nearest_first(place, step):
-    me, low = place[0], ((step + 1) // 2) % 2
-    if place[4]:
-        low = step % 2
-    return (me % 2 + low) % 2 + 2 * ((me // 2 + step // 2) % 2)
+def pieces(place, step, half):
+    me, upper, moved, far = place[0], (step % 3) // 2, (step + 2) // 3, step // 3
+    near = moved - far
+    low = (moved, far) if place[4] else (near, near)
+    found = []
+    for side, high in ((0, far), (1, moved)):
+        chunk = (me % 2 + low[side]) % 2 + 2 * ((me // 2 + high) % 2)
+        row = (2 * chunk + (1 - upper if side else upper)) * half
+        found.append(pl.ds(pl.multiple_of(row, half), half))
+    return found
+
+
+def joined(ref, rows):
+    return jnp.concatenate([ref[rows[0]], ref[rows[1]]], axis=0)
+
+
+def put(ref, rows, values):
+    half = values.shape[0] // 2
+    ref[rows[0]] = values[:half].astype(ref.dtype)
+    ref[rows[1]] = values[half:].astype(ref.dtype)
 
 
 def farthest_first(place, step):
@@ -144,10 +159,10 @@
             b2.start()
             b0.wait_recv()
             a2.start()
-            a1.wait_recv()
 
         @pl.when(step == 2)
         def _():
+            a1.wait_recv()
             b1.wait_recv()
 
         if last is None:
@@ -157,7 +172,7 @@
                 late()
                 final()
 
-        use(nearest_first(place, step))
+        use(pieces(place, step, half))
 
     repeat(body, 4 if last is None else 3)
     if last is not None:
@@ -223,7 +238,7 @@
     def last(final):
         def before():
             final()
-            use(place[3])
+            use(pieces(place, 3, mine.shape[0] // 2))
 
         scatter(place, term, bufs, sems, base + 6, fill, before)
 
@@ -397,8 +412,13 @@
     return inverse * (incoming - normal * jnp.mean(incoming * normal, axis=-1, keepdims=True))
 
 
+def tokens_of(ref):
+    return ref.at[lax.axis_index(S)] if len(ref.shape) == 3 else ref
+
+
 def qkv_kernel(layer, square, x, sel, mod, gain, both, turn, ones, w_own, w_other, whole, proj, q,
                k, v, h, w, ssem, rsem, wsem):
+    x, mod, gain = tokens_of(x), mod.at[layer], gain.at[layer]
     place = ring(square)
     head = w_own.shape[1] * PAD // w.shape[1]
     load = head_weights(w_own, w_other, layer, w, wsem, range(3))
@@ -412,19 +432,22 @@
 
     over_blocks(x.shape[0], prepare)
 
-    def use(chunk):
-        rows = chunk_rows(chunk, x.shape[0])
-        cosine = twice(both[rows, 0:PAD])
-        sine = twice(both[rows, PAD : 2 * PAD])
+    def use(rows):
+        held = joined(whole, rows)
+        table = joined(both, rows)
+        cosine = twice(table[:, 0:PAD])
+        sine = twice(table[:, PAD : 2 * PAD])
         for which, dst in ((0, q), (1, k)):
-            full = nt(whole[rows], w[which])
-            proj[which, rows] = full.astype(BF)
+            full = nt(held, w[which])
+            put(proj.at[which], rows, full)
+            turned = []
             for pair in range(full.shape[1] // (2 * PAD)):
                 lanes = slice(pair * 2 * PAD, (pair + 1) * 2 * PAD)
                 normal, _ = unit(full[:, lanes], ones[...], head)
                 gained = normal * twice(gain[which : which + 1])
-                dst[rows, lanes] = (gained * cosine + two(nn, gained, turn[...]) * sine).astype(BF)
-        v[rows] = nt(whole[rows], w[2]).astype(BF)
+                turned.append(gained * cosine + two(nn, gained, turn[...]) * sine)
+            put(dst, rows, jnp.concatenate(turned, axis=1))
+        put(v, rows, nt(held, w[2]))
 
     gather(place, h, whole, (ssem, rsem), 0, use, lambda: arrive(load))
 
@@ -432,6 +455,7 @@
 def mlp_kernel(layer, square, att, x, sel, mod, wo0, wo1, wg0, wg1, wd0, wd1, br1, x1, br2, y,
                whole_h, gate_h, up_h, hidden_h, whole, gate, up, hidden, h, wo, wg, wd, o1, i1, k1, s1, o2, i2, k2, s2,
                ssem, rsem, wsem, osem):
+    x, mod = tokens_of(x), mod.at[layer]
     place = ring(square)
     rows_here, _ = x.shape
     load_o = head_weights(wo0, wo1, layer, wo, osem, range(1))
@@ -455,12 +479,13 @@
 
     over_blocks(rows_here, between)
 
-    def use(chunk):
-        rows = chunk_rows(chunk, rows_here)
-        gate[rows] = nn(whole[rows], wg[0])
-        up[rows] = nn(whole[rows], wg[1])
-        g = gate[rows]
-        hidden[rows] = (g * jax.nn.sigmoid(g) * up[rows]).astype(BF)
+    def use(rows):
+        held = joined(whole, rows)
+        g = nn(held, wg[0])
+        put(gate, rows, g)
+        u = nn(held, wg[1])
+        put(up, rows, u)
+        put(hidden, rows, g * jax.nn.sigmoid(g) * u)
 
     second = (o2, i2, k2, s2)
     stores = []
@@ -495,6 +520,7 @@
                     wo0, wo1, wg0, wg1, wd0, wd1, whole1, datt, dx1, dmod, total, mine, theirs,
                     got, h, h1, whole2, dgate, dup, gate, up, hidden, saved, flipped, wo, wg, wd, o1, i1, k1,
                     s1, ssem, rsem, wsem, osem):
+    dy, mod = tokens_of(dy), mod.at[layer]
     place = ring(square)
     rows_here, _ = dy.shape
     load_d = layer_weights(wd0, wd1, layer, wd, wsem.at[0])
@@ -522,13 +548,12 @@
     def ready():
         arrive((load_d, load_gate, load_up, load_g, load_hidden))
 
-    def use(chunk):
-        rows = chunk_rows(chunk, rows_here)
-        d_hidden = nt(whole2[rows], wd[...])
-        g = gate[rows]
+    def use(rows):
+        d_hidden = nt(joined(whole2, rows), wd[...])
+        g = joined(gate, rows)
         s = jax.nn.sigmoid(g)
-        dgate[rows] = (d_hidden * up[rows] * s * (1.0 + g * (1.0 - s))).astype(BF)
-        dup[rows] = (d_hidden * g * s).astype(BF)
+        put(dgate, rows, d_hidden * joined(up, rows) * s * (1.0 + g * (1.0 - s)))
+        put(dup, rows, d_hidden * g * s)
 
     bufs = (o1, i1, k1, s1)
     f = hidden.shape[1]
@@ -559,9 +584,8 @@
 
     over_blocks(rows_here, between)
 
-    def use_out(chunk):
-        rows = chunk_rows(chunk, rows_here)
-        datt[rows] = nt(whole1[rows], wo[...]).astype(BF)
+    def use_out(rows):
+        put(datt, rows, nt(joined(whole1, rows), wo[...]))
 
     def sums():
         def one(rows):
@@ -590,6 +614,7 @@
                     mod, part, prev, w_own, w_other, whole_h, att_h, rows1_h, du, du_b, dmod, total,
                     dgain, w, whole, att, rows1, flipped, dproj, flat, mine, theirs, got, o1, i1,
                     k1, s1, ssem, rsem, wsem, hsem):
+    x, mod, gain = tokens_of(x), mod.at[layer], gain.at[layer]
     place = ring(square)
     rows_here, _ = x.shape
     packed = spread.shape[0]
@@ -695,10 +720,18 @@
     return copy
 
 
-def head_kernel(dp, lifted, ada_h, bias, gain, items, pos, tables, mod, lifted_all, gains, sel,
-                both, spans, ada, parts, got, wide, tall, ssem, rsem, wsem):
+def head_kernel(dp, cond, ada_h, bias, gain_own, items, pos, tables, mod, lifted_all, gains, sel,
+                both, spans, ada, parts, got, wide, tall, lifted, gain, ssem, rsem, wsem):
     load = pltpu.make_async_copy(ada_h, ada, wsem)
     load.start()
+    lifted[...] = jnp.zeros_like(lifted)
+    raw = cond[...].astype(F32)
+    raw = (raw * jax.nn.sigmoid(raw)).astype(BF).astype(F32)
+    lifted[0:3] = raw[0:3]
+    lifted[8:11] = raw[3:6]
+    gain[...] = jnp.zeros_like(gain)
+    gain[0:2, 0 : gain_own.shape[1]] = gain_own[...].astype(F32)
+    biases = bias[...].astype(F32)
     greet_all(dp)
     sems = (ssem, rsem)
     here, shard, section = cell(), lax.axis_index(DP), lax.axis_index(S)
@@ -714,7 +747,8 @@
     for micro in range(2):
         for j in range(3):
             rows = lifted[pl.ds(micro * 8, 8)].astype(BF)
-            parts[micro, j] = nt(rows, ada[pl.ds(j * half, half)]) + bias[j]
+            here_bias = biases[:, j * half : (j + 1) * half]
+            parts[micro, j] = nt(rows, ada[pl.ds(j * half, half)]) + here_bias
     for k in range(1, 8):
         peer = (here + k) % 8
         copies.append(push(parts.at[peer // 4], got.at[here], sems, k - 1, cell_id(peer)))
@@ -754,8 +788,8 @@
         copy.wait_send()
 
 
-def tail_kernel(dp, dmod, dgain, lifted_part, ada_h, ada_grad, bias_grad, dl_sum, gain_sum, ada,
-                got, got_gain, total, total_gain, every, every_gain, lifts, ssem, rsem, wsem):
+def tail_kernel(dp, dmod, dgain, lifted_part, cond, ada_h, ada_grad, bias_grad, cond_grad, gain_grad,
+                ada, bias_row, got, got_gain, total, total_gain, every, every_gain, lifts, ssem, rsem, wsem):
     load = pltpu.make_async_copy(ada_h, ada, wsem)
     load.start()
     greet_all(dp)
@@ -807,7 +841,11 @@
     gain = every_gain[0]
     for k in range(1, dp):
         gain = gain + every_gain[k]
-    gain_sum[...] = gain
+    heads = gain.shape[1] // PAD
+    summed = gain[:, 0:PAD]
+    for h in range(1, heads):
+        summed = summed + gain[:, h * PAD : (h + 1) * PAD]
+    gain_grad[...] = summed[0:2, 0 : gain_grad.shape[1]]
     for j in range(3):
         bias = jnp.zeros((1, half), F32)
         grad = jnp.zeros((lifted_part.shape[2], half), F32)
@@ -819,7 +857,7 @@
                 low = (block - high.astype(F32)).astype(BF)
                 rows = lifted_part[2 * k + micro].astype(BF)
                 grad = grad + tn(rows, high) + tn(rows, low)
-        bias_grad[j] = bias
+        bias_row[:, pl.ds(j * half, half)] = bias
         ada_grad[:, pl.ds(j * half, half)] = grad
     for copy in lift_copies:
         copy.wait_recv()
@@ -827,7 +865,18 @@
     lift = lifts[0]
     for k in range(1, 8):
         lift = lift + lifts[k]
-    dl_sum[...] = lift
+    raw = cond[...].astype(F32)
+    s = jax.nn.sigmoid(raw)
+    factor = s * (1.0 + raw * (1.0 - s))
+    cond_grad[0:3] = lift[0, 0:3] * factor[0:3]
+    cond_grad[3:6] = lift[1, 0:3] * factor[3:6]
+    part = bias_grad.shape[1]
+    row = bias_row[...]
+    total_bias = jnp.zeros((1, part), F32)
+    for k in range(dp):
+        chosen = (shard == k).astype(F32)
+        total_bias = total_bias + row[:, k * part : (k + 1) * part] * chosen
+    bias_grad[...] = total_bias
     for copy in sends:
         copy.wait_send()
 
@@ -1016,7 +1065,6 @@
     rows, width = tokens.shape[1:]
     seq = patch_item.shape[1]
     items = cond.shape[0]
-    per_micro = items // 2
     head = qk_gain.shape[-1]
     packed = w_qkv.shape[-1]
     heads = packed // head
@@ -1024,14 +1072,8 @@
     own = (jnp.swapaxes(w_qkv[0], 1, 2), w_out[0], w_gate_up[0], w_down[0])
     other = tuple(swap(w) for w in own)
 
-    cond_wide = cond.astype(F32)
-    cond_sigmoid = jax.nn.sigmoid(cond_wide)
-    lifted = (cond_wide * cond_sigmoid).astype(BF).astype(F32).reshape(2, per_micro, width)
-    lifted = jnp.pad(lifted, ((0, 0), (0, 8 - per_micro), (0, 0))).reshape(16, width)
     ada = ada_weight[0].T
     half = width // 2
-    bias = ada_bias.astype(F32).reshape(3, 1, half)
-    gain = jnp.pad(qk_gain[0].astype(F32), ((0, 6), (0, PAD - head)))
     trig, (turn, ones, spread) = head_tables(packed, head)
     wide = heads * PAD
     mods, lifted_all, gains, sel, both, spans = ring_call(
@@ -1052,10 +1094,12 @@
             pltpu.VMEM((8, 3, 8, half), F32),
             pltpu.VMEM((8, seq), F32),
             pltpu.VMEM((seq, 8), F32),
+            pltpu.VMEM((16, width), F32),
+            pltpu.VMEM((8, PAD), F32),
         ]
         + dma_sems(7 + dp)
         + [pltpu.SemaphoreType.DMA],
-        (lifted, ada, bias, gain, patch_item, patch_pos, trig),
+        (cond, ada, ada_bias, qk_gain[0], patch_item, patch_pos, trig),
         (1, 0, 1, 1, 1, 1, 1),
         scalar=5,
     )
@@ -1064,10 +1108,10 @@
     lifted_part = lax.dynamic_slice_in_dim(lifted_all, shard * part, part, 2)
     lifted_part = lifted_part.reshape(2 * dp, 8, part)
 
-    x = lax.dynamic_index_in_dim(tokens, section, 0, keepdims=False)
+    x = tokens
     kept = []
     for layer in range(2):
-        mod = mods[layer]
+        mod = mods
         whole1, proj, q, k, v = ring_call(
             functools.partial(qkv_kernel, layer, square),
             layer,
@@ -1076,7 +1120,7 @@
             [pltpu.VMEM((rows, width), BF), pltpu.VMEM((3, wide, width), BF)]
             + dma_sems(6)
             + [pltpu.SemaphoreType.DMA((3 * heads,))],
-            (x, sel, mod, gains[layer], both, turn, ones, own[0], other[0]),
+            (x, sel, mod, gains, both, turn, ones, own[0], other[0]),
             (1,) * 7 + (0, 0),
         )
         (att,) = local_call(
@@ -1122,14 +1166,14 @@
         kept.append((x, whole1, proj, q, k, v, att, br1, x1, whole2, gate, up, hidden, br2, y))
         x = y
 
-    dy = lax.dynamic_index_in_dim(cotangent, section, 0, keepdims=False)
+    dy = cotangent
     packs = [None, None]
     prev = jnp.zeros((12, 8, half), F32)
     d_gains = [None, None]
     d_inputs = [None, None]
     for layer in (1, 0):
         x, whole1, proj, q, k, v, att, br1, x1, whole2, gate, up, hidden, br2, y = kept[layer]
-        mod = mods[layer]
+        mod = mods
         rows1, datt, dx1, dmod_a, total_mlp = ring_call(
             functools.partial(mlp_back_kernel, layer, square),
             4 + layer,
@@ -1197,7 +1241,7 @@
             + scatter_scratch(rows, width)
             + dma_sems(7)
             + [pltpu.SemaphoreType.DMA((3,)), pltpu.SemaphoreType.DMA((3 * heads,))],
-            (dq, dk, dv, proj, gains[layer], both, turn, ones, spread, x, dx1, sel, mod, dmod_a,
+            (dq, dk, dv, proj, gains, both, turn, ones, spread, x, dx1, sel, mod, dmod_a,
              prev, own[0], other[0], whole1, att, rows1),
             (1,) * 15 + (0,) * 5,
         )
@@ -1209,18 +1253,20 @@
         dy = du_b
 
     gain_parts = jnp.pad(jnp.stack(d_gains).reshape(2, 2, wide), ((0, 0), (0, 6), (0, 0)))
-    g_ada_w, bias_grad, dl_sum, gain_sum = ring_call(
+    bias_part = ada_bias.shape[1] // dp
+    g_ada_w, g_ada_b, cond_grad, gain_total = ring_call(
         functools.partial(tail_kernel, dp),
         9,
         15,
         [
             sds((part, 3 * half), F32),
-            sds((3, 1, half), F32),
-            sds((2, 8, width), F32),
-            sds((8, wide), F32),
+            sds((1, bias_part), F32),
+            sds((items, width), F32),
+            sds((2, head), F32),
         ],
         [
             pltpu.VMEM((3 * half, width), BF),
+            pltpu.VMEM((1, 3 * half), F32),
             pltpu.VMEM((8, 3, 8, half), F32),
             pltpu.VMEM((8, 8, wide), F32),
             pltpu.VMEM((2, 3, 8, half), F32),
@@ -1231,14 +1277,9 @@
         ]
         + dma_sems(13 + 2 * (dp - 1) + 8)
         + [pltpu.SemaphoreType.DMA],
-        (d_mod, gain_parts, lifted_part, ada),
-        (1, 1, 1, 0),
+        (d_mod, gain_parts, lifted_part, cond, ada),
+        (1, 1, 1, 1, 0),
     )
-    bias_part = ada_bias.shape[1] // dp
-    g_ada_b = lax.dynamic_slice_in_dim(bias_grad.reshape(-1), shard * bias_part, bias_part)
-    cond_grad = dl_sum[:, :per_micro].reshape(items, width) * cond_sigmoid
-    cond_grad = cond_grad * (1.0 + cond_wide * (1.0 - cond_sigmoid))
-    gain_total = gain_sum[:2].reshape(1, 2, heads, PAD)[..., :head].sum(axis=2)
 
     mlp = own_layer(section, (packs[0][0], packs[1][0]))
     attn = own_layer(section, (packs[0][1], packs[1][1]))
@@ -1263,9 +1304,9 @@
         g_out,
         g_gate_up,
         g_down,
-        gain_total,
+        gain_total[None],
         g_ada_w[None],
-        g_ada_b[None],
+        g_ada_b,
     )
 
 

time: 597 us -> 586 us (0.982)
  local copies, waits for them, and re-layouts: 22.3 us -> 11.7 us
  waiting for transfers between devices: 125 us -> 134 us
  other arithmetic: 17.9 us -> 10.5 us
    reduce_scatter x4, waiting for transfers between devices: 124 us -> 133 us  [reduced(): return lax.psum_scatter(total, DP, scatter_dimension=0, tiled=True)[0]]
  transfers between devices with their start and end apart: 12 -> 12, of which waited for: 3 -> 3; matrix products, arithmetic and copies ran while one was open for 5% -> 2% of each run, Pallas kernels for 14% -> 14%
where the time goes in v5:
time: 586 us; the launch traced here: 583 us
  Pallas kernels  408 us (70%)
  waiting for transfers between devices  134 us (23%)
  between operations  14.3 us (2%)
  local copies, waits for them, and re-layouts  11.7 us (2%)
  other arithmetic  10.5 us (2%)
    pallas_call x10, Pallas kernels, ring_call(): pl.pallas_call(kernel, out_shape=outs, in_specs=[vmem() if s else anywher...  373 us
    reduce_scatter x4, waiting for transfers between devices, reduced(): return lax.psum_scatter(total, DP, scatter_dimension=0, tiled=True)[0]  133 us
    pallas_call x4, Pallas kernels, local_call(): pl.pallas_call(kernel, out_shape=outs, in_specs=[pl.BlockSpec(memory_spac...  34.9 us
  transfers between devices with their start and end apart: 12, of which 3 were waited for; matrix products, arithmetic and copies ran while one was open for 2% of the time, Pallas kernels for 14%

profile of v5, /device:TPU:1, one launch (start us, length us, event | category | flops | bytes accessed | tf_op | source)
XLA Modules:
  0.0 583.2 jit_solution(12195467186036433280)
XLA Ops:
  8.3 16.1 %shard_map.231 = (f32[2,6,8,1152]{3,2,1,0:T(8,128)}, f32[4,16,1152]{2,1,0:T(8,128)}, f32[2,8,128]{2,1,0:T(8,128)}, f32[192,8]{1,0:T(8,128)}, f32[768,256]{1,0:T(8,128)}, /*index=5*/s32[8]{0:T(128)}) custom-call(bf16[6,1152]{1,0:T(8,128)(2,1)} %cond.3, bf16[1728,1152]{1,0:T(8,128)(2,1)} %bitcast.74, bf16[1,1728]{1,0:T(2,128)(2,1)} %bias.1, ...), custom_call_target="tpu_custom_call" | custom-call | bytes 42000000 | tf_op jit(solution)/shard_map/pallas_call | solution.py:889
  24.4 23.8 %shard_map.232 = (bf16[768,1152]{1,0:T(8,128)(2,1)}, bf16[2,768,512]{2,1,0:T(8,128)(2,1)}, bf16[768,512]{1,0:T(8,128)(2,1)}, bf16[768,512]{1,0:T(8,128)(2,1)}, bf16[768,512]{1,0:T(8,128)(2,1)}) custom-call(bf16[2,192,1152]{2,1,0:T(8,128)(2,1)} %x.7, f32[192,8]{1,0:T(8,128)} %get-tuple-element.71.sel, f32[2,6,8,1152]{3,2,1,0:T(8,128)} %get-tuple-element.72.mod, ...), custom_call_target="tpu_custom_call" | custom-call | bytes 70000000 | tf_op jit(solution)/shard_map/pallas_call | solution.py:889
  48.2 6.6 %shard_map.233.att.att_h = bf16[768,512]{1,0:T(8,128)(2,1)} custom-call(s32[8]{0:T(128)} %get-tuple-element.70.spans, bf16[768,512]{1,0:T(8,128)(2,1)} %get-tuple-element.75.q, bf16[768,512]{1,0:T(8,128)(2,1)} %get-tuple-element.76.k, bf16[768,512]{1,0:T(8,128)(2,1)} %get-tuple-element.77.v), custom_call_target="tpu_custom_call" | custom-call | bytes 21000000 | tf_op jit(solution)/shard_map/pallas_call | solution.py:1004
  54.8 1.7 copy-done
  56.6 50.6 %shard_map.234 = (f32[192,1152]{1,0:T(8,128)}, f32[192,1152]{1,0:T(8,128)}, f32[192,1152]{1,0:T(8,128)}, bf16[192,1152]{1,0:T(8,128)(2,1)}, bf16[768,1152]{1,0:T...) custom-call(bf16[768,512]{1,0:T(8,128)(2,1)} %shard_map.233.att.att_h, ...), custom_call_target="tpu_custom_call" | custom-call | bytes 168000000 | tf_op jit(solution)/shard_map/pallas_call | solution.py:889
  107.2 19.8 %shard_map.235 = (bf16[768,1152]{1,0:T(8,128)(2,1)}, bf16[2,768,512]{2,1,0:T(8,128)(2,1)}, bf16[768,512]{1,0:T(8,128)(2,1)}, bf16[768,512]{1,0:T(8,128)(2,1)}, bf16[768,512]{1,0:T(8,128)(2,1)}) custom-call(bf16[192,1152]{1,0:T(8,128)(2,1)} %get-tuple-element.78.x, f32[192,8]{1,0:T(8,128)} %get-tuple-element.71.sel, f32[2,6,8,1152]{3,2,1,0:T(8,128)} %get-tuple-element.72.mod, ...), custom_call_target="tpu_custom_call" | custom-call | bytes 70000000 | tf_op jit(solution)/shard_map/pallas_call | solution.py:889
  127.0 6.6 %shard_map.236.att.att_h = bf16[768,512]{1,0:T(8,128)(2,1)} custom-call(s32[8]{0:T(128)} %get-tuple-element.70.spans, bf16[768,512]{1,0:T(8,128)(2,1)} %get-tuple-element.79.q, bf16[768,512]{1,0:T(8,128)(2,1)} %get-tuple-element.80.k, bf16[768,512]{1,0:T(8,128)(2,1)} %get-tuple-element.81.v), custom_call_target="tpu_custom_call" | custom-call | bytes 21000000 | tf_op jit(solution)/shard_map/pallas_call | solution.py:1004
  133.6 48.5 %shard_map.237 = (f32[192,1152]{1,0:T(8,128)}, f32[192,1152]{1,0:T(8,128)}, f32[192,1152]{1,0:T(8,128)}, bf16[192,1152]{1,0:T(8,128)(2,1)}, bf16[768,1152]{1,0:T...) custom-call(bf16[768,512]{1,0:T(8,128)(2,1)} %shard_map.236.att.att_h, ...), custom_call_target="tpu_custom_call" | custom-call | bytes 168000000 | tf_op jit(solution)/shard_map/pallas_call | solution.py:889
  182.1 64.3 %shard_map.238 = (bf16[768,1152]{1,0:T(8,128)(2,1)}, bf16[768,512]{1,0:T(8,128)(2,1)}, f32[192,1152]{1,0:T(8,128)}, f32[8,8,576]{2,1,0:T(8,128)}, bf16[4,144,2304]{2,1,0:T(8,128)(2,1)}) custom-call(bf16[2,192,1152]{2,1,0:T(8,128)(2,1)} %dy.1, f32[192,1152]{1,0:T(8,128)} %get-tuple-element.83.br2, f32[192,1152]{1,0:T(8,128)} %get-tuple-element.84.br1, ...), custom_call_target="tpu_custom_call" | custom-call | bytes 182000000 | tf_op jit(solution)/shard_map/pallas_call | solution.py:889
  246.4 10.8 %shard_map.239 = (bf16[768,512]{1,0:T(8,128)(2,1)}, bf16[768,512]{1,0:T(8,128)(2,1)}, bf16[768,512]{1,0:T(8,128)(2,1)}) custom-call(s32[8]{0:T(128)} %get-tuple-element.70.spans, bf16[768,512]{1,0:T(8,128)(2,1)} %get-tuple-element.79.q, bf16[768,512]{1,0:T(8,128)(2,1)} %get-tuple-element.80.k, bf16[768,512]{1,0:T(8,128)(2,1)} %get-tuple-element.81.v, ...), custom_call_target="tpu_custom_call" | custom-call | bytes 35000000 | tf_op jit(solution)/shard_map/pallas_call | solution.py:1004
  257.9 27.2 %shard_map.240 = (f32[192,1152]{1,0:T(8,128)}, bf16[192,1152]{1,0:T(8,128)(2,1)}, f32[2,12,8,576]{3,2,1,0:T(8,128)}, bf16[4,144,1152]{2,1,0:T(8,128)(2,1)}, f32[2,1,512]{2,1,0:T(1,128)}) custom-call(bf16[768,512]{1,0:T(8,128)(2,1)} %get-tuple-element.91.dq, bf16[768,512]{1,0:T(8,128)(2,1)} %get-tuple-element.92.dk, bf16[768,512]{1,0:T(8,128)(2,1)} %get-tuple-element.93.dv, ...), custom_call_target="tpu_custom_call" | custom-call | bytes 77000000 | tf_op jit(solution)/shard_map/pallas_call | solution.py:889
  285.2 58.0 %shard_map.241 = (bf16[768,1152]{1,0:T(8,128)(2,1)}, bf16[768,512]{1,0:T(8,128)(2,1)}, f32[192,1152]{1,0:T(8,128)}, f32[8,8,576]{2,1,0:T(8,128)}, bf16[4,144,2304]{2,1,0:T(8,128)(2,1)}) custom-call(bf16[192,1152]{1,0:T(8,128)(2,1)} %get-tuple-element.99.dy, f32[192,1152]{1,0:T(8,128)} %get-tuple-element.100.br2, f32[192,1152]{1,0:T(8,128)} %get-tuple-element.101.br1, ...), custom_call_target="tpu_custom_call" | custom-call | bytes 182000000 | tf_op jit(solution)/shard_map/pallas_call | solution.py:889
  343.1 10.9 %shard_map.242 = (bf16[768,512]{1,0:T(8,128)(2,1)}, bf16[768,512]{1,0:T(8,128)(2,1)}, bf16[768,512]{1,0:T(8,128)(2,1)}) custom-call(s32[8]{0:T(128)} %get-tuple-element.70.spans, bf16[768,512]{1,0:T(8,128)(2,1)} %get-tuple-element.75.q, bf16[768,512]{1,0:T(8,128)(2,1)} %get-tuple-element.76.k, bf16[768,512]{1,0:T(8,128)(2,1)} %get-tuple-element.77.v, ...), custom_call_target="tpu_custom_call" | custom-call | bytes 35000000 | tf_op jit(solution)/shard_map/pallas_call | solution.py:1004
  354.7 26.9 %shard_map.243 = (f32[192,1152]{1,0:T(8,128)}, bf16[192,1152]{1,0:T(8,128)(2,1)}, f32[2,12,8,576]{3,2,1,0:T(8,128)}, bf16[4,144,1152]{2,1,0:T(8,128)(2,1)}, f32[2,1,512]{2,1,0:T(1,128)}) custom-call(bf16[768,512]{1,0:T(8,128)(2,1)} %get-tuple-element.108.dq, bf16[768,512]{1,0:T(8,128)(2,1)} %get-tuple-element.109.dk, ...), custom_call_target="tpu_custom_call" | custom-call | bytes 77000000 | tf_op jit(solution)/shard_map/pallas_call | solution.py:889
  384.6 0.8 collective-permute-start.5
  385.4 1.9 select_bitcast_fusion.2
  387.5 1.6 constant_dynamic-slice_fusion
  389.8 37.6 %shard_map.244 = (f32[288,1728]{1,0:T(8,128)}, f32[1,432]{1,0:T(1,128)}, f32[6,1152]{1,0:T(8,128)}, f32[2,72]{1,0:T(2,128)}) custom-call(f32[2,12,8,576]{3,2,1,0:T(8,128)} %get-tuple-element.118.dmod, f32[2,8,512]{2,1,0:T(8,128)} %pad.4.dgain, f32[8,8,288]{2,1,0:T(8,128)} %bitcast.84, bf16[6,1152]{1,0:T(8,128)(2,1)} %cond.3, bf16[1728,1152]{1,0:T(8,128)(2,1)} %bitcast.75), custom_call_target="tpu_custom_call" | custom-call | bytes 52500000 | tf_op jit(solution)/shard_map/pallas_call | solution.py:889
  427.4 1.1 maximum_select_fusion.2
  428.5 1.3 maximum_select_fusion
  429.8 26.6 %reduce-scatter.7.cloned.1.call-done = bf16[1,144,1152]{2,1,0:T(8,128)(2,1)} async-done(((bf16[4,144,1152]{2,1,0:T(8,128)(2,1)}), bf16[1,144,1152]{2,1,0:T(8,128)(2,1)}) %reduce-scatter.7.cloned.1.call-update) | async-done | bytes 331792 | tf_op jit(solution)/shard_map/reduce_scatter | solution.py:1051
  456.4 1.1 select_bitcast_fusion.4
  457.5 1.1 collective-permute-start.6
  458.7 51.5 %reduce-scatter.9.cloned.1.call-done = bf16[1,144,2304]{2,1,0:T(8,128)(2,1)} async-done(((bf16[4,144,2304]{2,1,0:T(8,128)(2,1)}), bf16[1,144,2304]{2,1,0:T(8,128)(2,1)}) %reduce-scatter.9.cloned.1.call-update) | async-done | bytes 663568 | tf_op jit(solution)/shard_map/reduce_scatter | solution.py:1051
  510.2 54.5 %reduce-scatter.11.cloned.1.call-done = bf16[1,144,2304]{2,1,0:T(8,128)(2,1)} async-done(((bf16[4,144,2304]{2,1,0:T(8,128)(2,1)}), bf16[1,144,2304]{2,1,0:T(8,128)(2,1)}) %reduce-scatter.11.cloned.1.call-update) | async-done | bytes 663568 | tf_op jit(solution)/shard_map/reduce_scatter | solution.py:1051
  564.7 2.2 select_bitcast_fusion.1
  567.0 1.1 collective-permute-start.7
  568.6 1.0 copy.26
  569.5 1.1 maximum_bitcast_fusion.1
  570.9 1.1 slice_bitcast_fusion
  572.0 1.3 maximum_bitcast_fusion
  574.5 1.3 copy.39
  (56 shorter events, 8.7 us)
Async XLA Ops:
  7.2 422.6 %reduce-scatter.5.cloned.1.call-start = ((), (), s32[]{:S(2)}) async-start(), calls=%async_computation.4 | async-start | bytes 1658880 | tf_op jit(solution)/shard_map/reduce_scatter | solution.py:1051
  7.2 47.6 %collective-permute-start.2 = (bf16[2,1152,768]{2,1,0:T(8,128)(2,1)}, bf16[2,1152,768]{2,1,0:T(8,128)(2,1)S(1)}, u32[]{:S(2)}, u32[]{:S(2)}) collective-permute-start(bf16[2,1152,768]{2,1,0:T(8,128)(2,1)} %bitcast.59), channel_id=1, source_target_pairs={{0,16},{16,0},{1,17},{17,1},{2,18},{18,2},{3,19},{19,3},{4,20},{20... | collective-permute-start | bytes 10616840 | tf_op jit(solution)/shard_map/ppermute | solution.py:1016
  7.3 17.1 %collective-permute-start = (bf16[3,288,1152]{2,1,0:T(8,128)(2,1)}, bf16[3,288,1152]{2,1,0:T(8,128)(2,1)}, u32[]{:S(2)}, u32[]{:S(2)}) collective-permute-start(bf16[3,288,1152]{2,1,0:T(8,128)(2,1)} %bitcast.64), channel_id=1, source_target_pairs={{0,16},{16,0},{1,17},{17,1},{2,18},{18,2},{3,19},{19,3},{4,20},{20... | collective-permute-start | bytes 5971976 | tf_op jit(solution)/shard_map/ppermute | solution.py:1016
  7.8 47.0 %collective-permute-start.3 = (bf16[768,1152]{1,0:T(8,128)(2,1)}, bf16[768,1152]{1,0:T(8,128)(2,1)}, u32[]{:S(2)}, u32[]{:S(2)}) collective-permute-start(bf16[768,1152]{1,0:T(8,128)(2,1)} %bitcast.69), channel_id=1, source_target_pairs={{0,16},{16,0},{1,17},{17,1},{2,18},{18,2},{3,19},{19,3},{4,20},{20... | collective-permute-start | bytes 5308424 | tf_op jit(solution)/shard_map/ppermute | solution.py:1016
  7.9 46.9 %collective-permute-start.1 = (bf16[288,1152]{1,0:T(8,128)(2,1)}, bf16[288,1152]{1,0:T(8,128)(2,1)}, u32[]{:S(2)}, u32[]{:S(2)}) collective-permute-start(bf16[288,1152]{1,0:T(8,128)(2,1)} %bitcast.76), channel_id=1, source_target_pairs={{0,16},{16,0},{1,17},{17,1},{2,18},{18,2},{3,19},{19,3},{4,20},{20... | collective-permute-start | bytes 1990664 | tf_op jit(solution)/shard_map/ppermute | solution.py:1016
  54.8 1.7 copy-start
  343.1 10.9 %copy-start.5 = (f32[2,12,8,576]{3,2,1,0:T(8,128)S(1)}, f32[2,12,8,576]{3,2,1,0:T(8,128)}, u32[]{:S(2)}) copy-start(f32[2,12,8,576]{3,2,1,0:T(8,128)} %get-tuple-element.114) | copy-start | bytes 1327108
  381.7 74.7 %reduce-scatter.7.cloned.1.call-start = ((), (), s32[]{:S(2)}) async-start(), calls=%async_computation.5 | async-start | bytes 1658880 | tf_op jit(solution)/shard_map/reduce_scatter | solution.py:1051
  382.5 127.7 %reduce-scatter.9.cloned.1.call-start = ((), (), s32[]{:S(2)}) async-start(), calls=%async_computation.6 | async-start | bytes 3317760 | tf_op jit(solution)/shard_map/reduce_scatter | solution.py:1051
  383.2 1.0 copy-start.3
  383.2 1.3 copy-start.4
  383.2 181.5 %reduce-scatter.11.cloned.1.call-start = ((), (), s32[]{:S(2)}) async-start(), calls=%async_computation.7 | async-start | bytes 3317760 | tf_op jit(solution)/shard_map/reduce_scatter | solution.py:1051
  383.8 1.6 copy-start.1
  384.6 4.5 copy-start.8
  384.6 4.5 copy-start.7
  384.6 43.8 %collective-permute-start.5 = (f32[192,1152]{1,0:T(8,128)S(1)}, f32[192,1152]{1,0:T(8,128)S(1)}, u32[]{:S(2)}, u32[]{:S(2)}) collective-permute-start(f32[192,1152]{1,0:T(8,128)S(1)} %get-tuple-element.150), channel_id=1, source_target_pairs={{0,16},{16,0},{1,17},{17,1},{2,18},{18,2},{3,19},{19,3},{4,20},{20... | collective-permute-start | bytes 2654216 | tf_op jit(solution)/shard_map/ppermute | solution.py:1016
  387.3 40.1 %collective-permute-start.4 = (bf16[192,1152]{1,0:T(8,128)(2,1)}, bf16[192,1152]{1,0:T(8,128)(2,1)S(1)}, u32[]{:S(2)}, u32[]{:S(2)}) collective-permute-start(bf16[192,1152]{1,0:T(8,128)(2,1)} %get-tuple-element.152), channel_id=1, source_target_pairs={{0,16},{16,0},{1,17},{17,1},{2,18},{18,2},{3,19},{19,3},{4,20},{20... | collective-permute-start | bytes 1327112 | tf_op jit(solution)/shard_map/ppermute | solution.py:1016
  457.5 110.5 %collective-permute-start.6 = (bf16[144,1152]{1,0:T(8,128)(2,1)S(1)}, bf16[144,1152]{1,0:T(8,128)(2,1)S(1)}, u32[]{:S(2)}, u32[]{:S(2)}) collective-permute-start(bf16[144,1152]{1,0:T(8,128)(2,1)S(1)} %get-tuple-element.154), channel_id=1, source_target_pairs={{0,16},{16,0},{1,17},{17,1},{2,18},{18,2},{3,19},{19,3},{4,20},{20... | collective-permute-start | bytes 995336 | tf_op jit(solution)/shard_map/ppermute | solution.py:1016
  567.0 3.7 collective-permute-start.7
  572.0 1.3 copy-start.6
  572.0 1.9 copy-start.10
  572.0 2.5 copy-start.2
  574.5 1.3 copy-start.9
Sparse Core Ops, SparseCore 0:
  381.8 39.2 reduce-scatter.4
  423.5 32.8 reduce-scatter.6
  458.7 51.4 reduce-scatter.8
  512.3 52.3 reduce-scatter.10

commit v6 on v5

--- a/solution.py
+++ b/solution.py
@@ -612,14 +612,14 @@
 
 def qkv_back_kernel(layer, square, dq, dk, dv, proj, gain, both, turn, ones, spread, x, dx1, sel,
                     mod, part, prev, w_own, w_other, whole_h, att_h, rows1_h, du, du_b, dmod, total,
-                    dgain, w, whole, att, rows1, flipped, dproj, flat, mine, theirs, got, o1, i1,
-                    k1, s1, ssem, rsem, wsem, hsem):
+                    dgain, w, whole, att, rows1, flipped, dpack, flat, mine, theirs, got, o1, i1,
+                    k1, s1, ssem, rsem, wsem):
     x, mod, gain = tokens_of(x), mod.at[layer], gain.at[layer]
     place = ring(square)
     rows_here, _ = x.shape
     packed = spread.shape[0]
     head = packed * PAD // spread.shape[1]
-    load = head_weights(w_own, w_other, layer, w, hsem, range(3))
+    load = layer_weights(w_own, w_other, layer, w, wsem.at[3])
     loads = []
     for n, (src, dst) in enumerate(((whole_h, whole), (att_h, att), (rows1_h, rows1))):
         loads.append(pltpu.make_async_copy(src, dst, wsem.at[n]))
@@ -630,7 +630,7 @@
     here[pl.ds(0, 4)] = jnp.zeros_like(prev[pl.ds(0, 4)])
     here[pl.ds(4, 8)] = part[...]
     dgain[...] = jnp.zeros_like(dgain)
-    arrive(load)
+    load.wait()
     bufs = (o1, i1, k1, s1)
     sems = (ssem, rsem)
     packs = (mine, theirs, got)
@@ -641,6 +641,7 @@
         cosine = twice(both[rows, 0:PAD])
         sine = twice(both[rows, PAD : 2 * PAD])
         for which, src in ((0, dq), (1, dk)):
+            parts = []
             for pair in range(src.shape[1] // (2 * PAD)):
                 lanes = slice(pair * 2 * PAD, (pair + 1) * 2 * PAD)
                 turned = src[rows, lanes]
@@ -649,24 +650,22 @@
                 dgain[which, :, lanes] += jnp.sum(back * normal, axis=0, keepdims=True)
                 gained = back * twice(gain[which : which + 1])
                 mean = two(nn, gained * normal, ones[...]) * (1.0 / head)
-                dproj[which, rows, lanes] = (inverse * (gained - normal * mean)).astype(BF)
-        return nn(dproj[0, rows], w[0]) + nn(dproj[1, rows], w[1]) + nn(dv[rows], w[2])
-
-    def grad_in():
+                parts.append((inverse * (gained - normal * mean)).astype(BF))
+            full = jnp.concatenate(parts, axis=1)
+            dpack[rows, which * packed : (which + 1) * packed] = nt(full, spread[...]).astype(BF)
+        dpack[rows, 2 * packed : 3 * packed] = nt(dv[rows], spread[...]).astype(BF)
+        return nn(dpack[rows], w[...])
+
+    def grads():
         loads[0].wait()
-        for k in range(3):
-            flat[...] = nt(dproj[k] if k < 2 else dv[...], spread[...]).astype(BF)
-            weight_grad(None if k else whole, flat, flipped, k * packed, packs)
-
-    def grad_out():
+        flipped[...] = whole[...].T
+        for col in range(0, 3 * packed, TILE):
+            size = min(TILE, 3 * packed - col)
+            weight_grad(None, dpack.at[:, col : col + size], flipped, col, packs)
         loads[1].wait()
         loads[2].wait()
         flat[...] = nt(att[...], spread[...]).astype(BF)
         weight_grad(rows1, flat, flipped, 3 * packed, packs)
-
-    def grads():
-        grad_in()
-        grad_out()
         copies.append(send_half(packs, sems, 6, 0, 4 * packed))
 
     scatter(place, term, bufs, sems, 0, grads)
@@ -912,17 +911,14 @@
         for n in range(wide // PAD):
             fn(slice(n * PAD, (n + 1) * PAD))
 
-    def one_item(item, carry):
+    for item in range(3):
         at = pl.ds(pl.multiple_of(spans[item], 16), TILE)
         valid = lax.broadcasted_iota(jnp.int32, (TILE, TILE), 1) < spans[4 + item]
 
-        def tile(lanes):
+        def tile(lanes, at=at, valid=valid):
             att[at, lanes] = softmax_rows(q[at, lanes], k[at, lanes], v[at, lanes], valid, scale)
 
         each_head(tile)
-        return carry
-
-    lax.fori_loop(0, 3, one_item, 0)
     first = rows - 48
     start = spans[3]
     at = pl.ds(first, 48)
@@ -967,12 +963,12 @@
         for n in range(wide // PAD):
             fn(slice(n * PAD, (n + 1) * PAD))
 
-    def one_item(item, carry):
+    for item in range(3):
         at = pl.ds(pl.multiple_of(spans[item], 16), TILE)
         keys = lax.broadcasted_iota(jnp.int32, (TILE, TILE), 0) < spans[4 + item]
         queries = lax.broadcasted_iota(jnp.int32, (TILE, TILE), 1) < spans[4 + item]
 
-        def tile(lanes):
+        def tile(lanes, at=at, keys=keys, queries=queries):
             parts = back_tile(
                 q[at, lanes], k[at, lanes], v[at, lanes], grad[at, lanes], keys, queries, scale
             )
@@ -980,9 +976,6 @@
                 dst[at, lanes] = new.astype(BF)
 
         each_head(tile)
-        return carry
-
-    lax.fori_loop(0, 3, one_item, 0)
     first = rows - 48
     start = spans[3]
     at = pl.ds(first, 48)
@@ -1071,6 +1064,7 @@
     hidden_here = w_down.shape[1]
     own = (jnp.swapaxes(w_qkv[0], 1, 2), w_out[0], w_gate_up[0], w_down[0])
     other = tuple(swap(w) for w in own)
+    flat_qkv = (own[0].reshape(3 * packed, width), other[0].reshape(3 * packed, width))
 
     ada = ada_weight[0].T
     half = width // 2
@@ -1229,20 +1223,20 @@
                 sds((2, 1, wide), F32),
             ],
             [
-                pltpu.VMEM((3, wide, width), BF),
+                pltpu.VMEM((3 * packed, width), BF),
                 pltpu.VMEM((seq, width), BF),
                 pltpu.VMEM((seq, wide), BF),
                 pltpu.VMEM((seq, width), BF),
                 pltpu.VMEM((width, seq), BF),
-                pltpu.VMEM((2, seq, wide), BF),
+                pltpu.VMEM((seq, 3 * packed), BF),
                 pltpu.VMEM((seq, packed), BF),
             ]
             + [pltpu.VMEM((dp, part // 2, 4 * packed), BF)] * 3
             + scatter_scratch(rows, width)
             + dma_sems(7)
-            + [pltpu.SemaphoreType.DMA((3,)), pltpu.SemaphoreType.DMA((3 * heads,))],
+            + [pltpu.SemaphoreType.DMA((4,))],
             (dq, dk, dv, proj, gains, both, turn, ones, spread, x, dx1, sel, mod, dmod_a,
-             prev, own[0], other[0], whole1, att, rows1),
+             prev, *flat_qkv, whole1, att, rows1),
             (1,) * 15 + (0,) * 5,
         )
         prev = d_mod[1]

time: 586 us -> 580 us (0.990)
  no operation moved by 1% of the time
where the time goes in v6:
time: 580 us; the launch traced here: 577 us
  Pallas kernels  403 us (69%)
  waiting for transfers between devices  134 us (23%)
  between operations  14.3 us (2%)
  local copies, waits for them, and re-layouts  11.7 us (2%)
  other arithmetic  10.5 us (2%)
    pallas_call x10, Pallas kernels, ring_call(): pl.pallas_call(kernel, out_shape=outs, in_specs=[vmem() if s else anywher...  373 us
    reduce_scatter x4, waiting for transfers between devices, reduced(): return lax.psum_scatter(total, DP, scatter_dimension=0, tiled=True)[0]  132 us
    pallas_call x4, Pallas kernels, local_call(): pl.pallas_call(kernel, out_shape=outs, in_specs=[pl.BlockSpec(memory_spac...  30 us
  transfers between devices with their start and end apart: 12, of which 3 were waited for; matrix products, arithmetic and copies ran while one was open for 2% of the time, Pallas kernels for 14%

profile of v6, /device:TPU:1, one launch (start us, length us, event | category | flops | bytes accessed | tf_op | source)
XLA Modules:
  0.0 577.3 jit_solution(2499287116516334242)
XLA Ops:
  8.3 16.1 %shard_map.231 = (f32[2,6,8,1152]{3,2,1,0:T(8,128)}, f32[4,16,1152]{2,1,0:T(8,128)}, f32[2,8,128]{2,1,0:T(8,128)}, f32[192,8]{1,0:T(8,128)}, f32[768,256]{1,0:T(8,128)}, /*index=5*/s32[8]{0:T(128)}) custom-call(bf16[6,1152]{1,0:T(8,128)(2,1)} %cond.3, bf16[1728,1152]{1,0:T(8,128)(2,1)} %bitcast.77, bf16[1,1728]{1,0:T(2,128)(2,1)} %bias.1, ...), custom_call_target="tpu_custom_call" | custom-call | bytes 42000000 | tf_op jit(solution)/shard_map/pallas_call | solution.py:888
  24.4 23.8 %shard_map.232 = (bf16[768,1152]{1,0:T(8,128)(2,1)}, bf16[2,768,512]{2,1,0:T(8,128)(2,1)}, bf16[768,512]{1,0:T(8,128)(2,1)}, bf16[768,512]{1,0:T(8,128)(2,1)}, bf16[768,512]{1,0:T(8,128)(2,1)}) custom-call(bf16[2,192,1152]{2,1,0:T(8,128)(2,1)} %x.7, f32[192,8]{1,0:T(8,128)} %get-tuple-element.71.sel, f32[2,6,8,1152]{3,2,1,0:T(8,128)} %get-tuple-element.72.mod, ...), custom_call_target="tpu_custom_call" | custom-call | bytes 70000000 | tf_op jit(solution)/shard_map/pallas_call | solution.py:888
  48.2 5.1 shard_map.233.att.att_h
  53.4 1.7 copy-done
  55.1 50.6 %shard_map.234 = (f32[192,1152]{1,0:T(8,128)}, f32[192,1152]{1,0:T(8,128)}, f32[192,1152]{1,0:T(8,128)}, bf16[192,1152]{1,0:T(8,128)(2,1)}, bf16[768,1152]{1,0:T...) custom-call(bf16[768,512]{1,0:T(8,128)(2,1)} %shard_map.233.att.att_h, ...), custom_call_target="tpu_custom_call" | custom-call | bytes 168000000 | tf_op jit(solution)/shard_map/pallas_call | solution.py:888
  105.7 19.8 %shard_map.235 = (bf16[768,1152]{1,0:T(8,128)(2,1)}, bf16[2,768,512]{2,1,0:T(8,128)(2,1)}, bf16[768,512]{1,0:T(8,128)(2,1)}, bf16[768,512]{1,0:T(8,128)(2,1)}, bf16[768,512]{1,0:T(8,128)(2,1)}) custom-call(bf16[192,1152]{1,0:T(8,128)(2,1)} %get-tuple-element.78.x, f32[192,8]{1,0:T(8,128)} %get-tuple-element.71.sel, f32[2,6,8,1152]{3,2,1,0:T(8,128)} %get-tuple-element.72.mod, ...), custom_call_target="tpu_custom_call" | custom-call | bytes 70000000 | tf_op jit(solution)/shard_map/pallas_call | solution.py:888
  125.5 5.1 shard_map.236.att.att_h
  130.6 48.5 %shard_map.237 = (f32[192,1152]{1,0:T(8,128)}, f32[192,1152]{1,0:T(8,128)}, f32[192,1152]{1,0:T(8,128)}, bf16[192,1152]{1,0:T(8,128)(2,1)}, bf16[768,1152]{1,0:T...) custom-call(bf16[768,512]{1,0:T(8,128)(2,1)} %shard_map.236.att.att_h, ...), custom_call_target="tpu_custom_call" | custom-call | bytes 168000000 | tf_op jit(solution)/shard_map/pallas_call | solution.py:888
  179.2 64.7 %shard_map.238 = (bf16[768,1152]{1,0:T(8,128)(2,1)}, bf16[768,512]{1,0:T(8,128)(2,1)}, f32[192,1152]{1,0:T(8,128)}, f32[8,8,576]{2,1,0:T(8,128)}, bf16[4,144,2304]{2,1,0:T(8,128)(2,1)}) custom-call(bf16[2,192,1152]{2,1,0:T(8,128)(2,1)} %dy.1, f32[192,1152]{1,0:T(8,128)} %get-tuple-element.83.br2, f32[192,1152]{1,0:T(8,128)} %get-tuple-element.84.br1, ...), custom_call_target="tpu_custom_call" | custom-call | bytes 182000000 | tf_op jit(solution)/shard_map/pallas_call | solution.py:888
  243.9 9.9 %shard_map.239 = (bf16[768,512]{1,0:T(8,128)(2,1)}, bf16[768,512]{1,0:T(8,128)(2,1)}, bf16[768,512]{1,0:T(8,128)(2,1)}) custom-call(s32[8]{0:T(128)} %get-tuple-element.70.spans, bf16[768,512]{1,0:T(8,128)(2,1)} %get-tuple-element.79.q, bf16[768,512]{1,0:T(8,128)(2,1)} %get-tuple-element.80.k, bf16[768,512]{1,0:T(8,128)(2,1)} %get-tuple-element.81.v, ...), custom_call_target="tpu_custom_call" | custom-call | bytes 35000000 | tf_op jit(solution)/shard_map/pallas_call | solution.py:997
  254.4 26.5 %shard_map.240 = (f32[192,1152]{1,0:T(8,128)}, bf16[192,1152]{1,0:T(8,128)(2,1)}, f32[2,12,8,576]{3,2,1,0:T(8,128)}, bf16[4,144,1152]{2,1,0:T(8,128)(2,1)}, f32[2,1,512]{2,1,0:T(1,128)}) custom-call(bf16[768,512]{1,0:T(8,128)(2,1)} %get-tuple-element.91.dq, bf16[768,512]{1,0:T(8,128)(2,1)} %get-tuple-element.92.dk, bf16[768,512]{1,0:T(8,128)(2,1)} %get-tuple-element.93.dv, ...), custom_call_target="tpu_custom_call" | custom-call | bytes 77000000 | tf_op jit(solution)/shard_map/pallas_call | solution.py:888
  280.9 57.9 %shard_map.241 = (bf16[768,1152]{1,0:T(8,128)(2,1)}, bf16[768,512]{1,0:T(8,128)(2,1)}, f32[192,1152]{1,0:T(8,128)}, f32[8,8,576]{2,1,0:T(8,128)}, bf16[4,144,2304]{2,1,0:T(8,128)(2,1)}) custom-call(bf16[192,1152]{1,0:T(8,128)(2,1)} %get-tuple-element.99.dy, f32[192,1152]{1,0:T(8,128)} %get-tuple-element.100.br2, f32[192,1152]{1,0:T(8,128)} %get-tuple-element.101.br1, ...), custom_call_target="tpu_custom_call" | custom-call | bytes 182000000 | tf_op jit(solution)/shard_map/pallas_call | solution.py:888
  338.8 9.9 %shard_map.242 = (bf16[768,512]{1,0:T(8,128)(2,1)}, bf16[768,512]{1,0:T(8,128)(2,1)}, bf16[768,512]{1,0:T(8,128)(2,1)}) custom-call(s32[8]{0:T(128)} %get-tuple-element.70.spans, bf16[768,512]{1,0:T(8,128)(2,1)} %get-tuple-element.75.q, bf16[768,512]{1,0:T(8,128)(2,1)} %get-tuple-element.76.k, bf16[768,512]{1,0:T(8,128)(2,1)} %get-tuple-element.77.v, ...), custom_call_target="tpu_custom_call" | custom-call | bytes 35000000 | tf_op jit(solution)/shard_map/pallas_call | solution.py:997
  348.7 0.7 slice_bitcast_fusion.7.prev
  349.4 27.1 %shard_map.243 = (f32[192,1152]{1,0:T(8,128)}, bf16[192,1152]{1,0:T(8,128)(2,1)}, f32[2,12,8,576]{3,2,1,0:T(8,128)}, bf16[4,144,1152]{2,1,0:T(8,128)(2,1)}, f32[2,1,512]{2,1,0:T(1,128)}) custom-call(bf16[768,512]{1,0:T(8,128)(2,1)} %get-tuple-element.108.dq, bf16[768,512]{1,0:T(8,128)(2,1)} %get-tuple-element.109.dk, ...), custom_call_target="tpu_custom_call" | custom-call | bytes 77000000 | tf_op jit(solution)/shard_map/pallas_call | solution.py:888
  380.0 1.9 select_bitcast_fusion.2
  382.0 1.6 constant_dynamic-slice_fusion
  384.4 38.1 %shard_map.244 = (f32[288,1728]{1,0:T(8,128)}, f32[1,432]{1,0:T(1,128)}, f32[6,1152]{1,0:T(8,128)}, f32[2,72]{1,0:T(2,128)}) custom-call(f32[2,12,8,576]{3,2,1,0:T(8,128)} %get-tuple-element.118.dmod, f32[2,8,512]{2,1,0:T(8,128)} %pad.4.dgain, f32[8,8,288]{2,1,0:T(8,128)} %bitcast.87, bf16[6,1152]{1,0:T(8,128)(2,1)} %cond.3, bf16[1728,1152]{1,0:T(8,128)(2,1)} %bitcast.78), custom_call_target="tpu_custom_call" | custom-call | bytes 52500000 | tf_op jit(solution)/shard_map/pallas_call | solution.py:888
  422.5 1.1 maximum_select_fusion.2
  423.6 1.3 maximum_select_fusion
  424.9 25.6 %reduce-scatter.7.cloned.1.call-done = bf16[1,144,1152]{2,1,0:T(8,128)(2,1)} async-done(((bf16[4,144,1152]{2,1,0:T(8,128)(2,1)}), bf16[1,144,1152]{2,1,0:T(8,128)(2,1)}) %reduce-scatter.7.cloned.1.call-update) | async-done | bytes 331792 | tf_op jit(solution)/shard_map/reduce_scatter | solution.py:1044
  450.5 1.1 select_bitcast_fusion.4
  451.7 1.1 collective-permute-start.6
  452.8 51.5 %reduce-scatter.9.cloned.1.call-done = bf16[1,144,2304]{2,1,0:T(8,128)(2,1)} async-done(((bf16[4,144,2304]{2,1,0:T(8,128)(2,1)}), bf16[1,144,2304]{2,1,0:T(8,128)(2,1)}) %reduce-scatter.9.cloned.1.call-update) | async-done | bytes 663568 | tf_op jit(solution)/shard_map/reduce_scatter | solution.py:1044
  504.3 54.5 %reduce-scatter.11.cloned.1.call-done = bf16[1,144,2304]{2,1,0:T(8,128)(2,1)} async-done(((bf16[4,144,2304]{2,1,0:T(8,128)(2,1)}), bf16[1,144,2304]{2,1,0:T(8,128)(2,1)}) %reduce-scatter.11.cloned.1.call-update) | async-done | bytes 663568 | tf_op jit(solution)/shard_map/reduce_scatter | solution.py:1044
  558.9 2.2 select_bitcast_fusion.1
  561.1 1.1 collective-permute-start.7
  562.7 1.0 copy.26
  563.7 1.1 maximum_bitcast_fusion.1
  565.0 1.1 slice_bitcast_fusion
  566.1 1.3 maximum_bitcast_fusion
  568.6 1.3 copy.39
  (56 shorter events, 8.5 us)
Async XLA Ops:
  7.2 417.7 %reduce-scatter.5.cloned.1.call-start = ((), (), s32[]{:S(2)}) async-start(), calls=%async_computation.4 | async-start | bytes 1658880 | tf_op jit(solution)/shard_map/reduce_scatter | solution.py:1044
  7.2 46.1 %collective-permute-start.2 = (bf16[2,1152,768]{2,1,0:T(8,128)(2,1)}, bf16[2,1152,768]{2,1,0:T(8,128)(2,1)S(1)}, u32[]{:S(2)}, u32[]{:S(2)}) collective-permute-start(bf16[2,1152,768]{2,1,0:T(8,128)(2,1)} %bitcast.62), channel_id=1, source_target_pairs={{0,16},{16,0},{1,17},{17,1},{2,18},{18,2},{3,19},{19,3},{4,20},{20... | collective-permute-start | bytes 10616840 | tf_op jit(solution)/shard_map/ppermute | solution.py:1009
  7.3 17.1 %collective-permute-start = (bf16[3,288,1152]{2,1,0:T(8,128)(2,1)}, bf16[3,288,1152]{2,1,0:T(8,128)(2,1)}, u32[]{:S(2)}, u32[]{:S(2)}) collective-permute-start(bf16[3,288,1152]{2,1,0:T(8,128)(2,1)} %bitcast.67), channel_id=1, source_target_pairs={{0,16},{16,0},{1,17},{17,1},{2,18},{18,2},{3,19},{19,3},{4,20},{20... | collective-permute-start | bytes 5971976 | tf_op jit(solution)/shard_map/ppermute | solution.py:1009
  7.8 45.6 %collective-permute-start.3 = (bf16[768,1152]{1,0:T(8,128)(2,1)}, bf16[768,1152]{1,0:T(8,128)(2,1)}, u32[]{:S(2)}, u32[]{:S(2)}) collective-permute-start(bf16[768,1152]{1,0:T(8,128)(2,1)} %bitcast.72), channel_id=1, source_target_pairs={{0,16},{16,0},{1,17},{17,1},{2,18},{18,2},{3,19},{19,3},{4,20},{20... | collective-permute-start | bytes 5308424 | tf_op jit(solution)/shard_map/ppermute | solution.py:1009
  7.9 45.5 %collective-permute-start.1 = (bf16[288,1152]{1,0:T(8,128)(2,1)}, bf16[288,1152]{1,0:T(8,128)(2,1)}, u32[]{:S(2)}, u32[]{:S(2)}) collective-permute-start(bf16[288,1152]{1,0:T(8,128)(2,1)} %bitcast.79), channel_id=1, source_target_pairs={{0,16},{16,0},{1,17},{17,1},{2,18},{18,2},{3,19},{19,3},{4,20},{20... | collective-permute-start | bytes 1990664 | tf_op jit(solution)/shard_map/ppermute | solution.py:1009
  53.4 1.7 copy-start
  338.8 9.9 %copy-start.5 = (f32[2,12,8,576]{3,2,1,0:T(8,128)S(1)}, f32[2,12,8,576]{3,2,1,0:T(8,128)}, u32[]{:S(2)}) copy-start(f32[2,12,8,576]{3,2,1,0:T(8,128)} %get-tuple-element.114) | copy-start | bytes 1327108
  376.6 73.9 %reduce-scatter.7.cloned.1.call-start = ((), (), s32[]{:S(2)}) async-start(), calls=%async_computation.5 | async-start | bytes 1658880 | tf_op jit(solution)/shard_map/reduce_scatter | solution.py:1044
  377.3 127.0 %reduce-scatter.9.cloned.1.call-start = ((), (), s32[]{:S(2)}) async-start(), calls=%async_computation.6 | async-start | bytes 3317760 | tf_op jit(solution)/shard_map/reduce_scatter | solution.py:1044
  378.1 1.0 copy-start.3
  378.1 1.3 copy-start.4
  378.1 180.8 %reduce-scatter.11.cloned.1.call-start = ((), (), s32[]{:S(2)}) async-start(), calls=%async_computation.7 | async-start | bytes 3317760 | tf_op jit(solution)/shard_map/reduce_scatter | solution.py:1044
  378.7 1.3 copy-start.1
  379.5 4.2 copy-start.8
  379.5 4.2 copy-start.7
  379.5 44.1 %collective-permute-start.5 = (f32[192,1152]{1,0:T(8,128)S(1)}, f32[192,1152]{1,0:T(8,128)S(1)}, u32[]{:S(2)}, u32[]{:S(2)}) collective-permute-start(f32[192,1152]{1,0:T(8,128)S(1)} %get-tuple-element.150), channel_id=1, source_target_pairs={{0,16},{16,0},{1,17},{17,1},{2,18},{18,2},{3,19},{19,3},{4,20},{20... | collective-permute-start | bytes 2654216 | tf_op jit(solution)/shard_map/ppermute | solution.py:1009
  381.9 40.7 %collective-permute-start.4 = (bf16[192,1152]{1,0:T(8,128)(2,1)}, bf16[192,1152]{1,0:T(8,128)(2,1)S(1)}, u32[]{:S(2)}, u32[]{:S(2)}) collective-permute-start(bf16[192,1152]{1,0:T(8,128)(2,1)} %get-tuple-element.152), channel_id=1, source_target_pairs={{0,16},{16,0},{1,17},{17,1},{2,18},{18,2},{3,19},{19,3},{4,20},{20... | collective-permute-start | bytes 1327112 | tf_op jit(solution)/shard_map/ppermute | solution.py:1009
  451.7 110.5 %collective-permute-start.6 = (bf16[144,1152]{1,0:T(8,128)(2,1)S(1)}, bf16[144,1152]{1,0:T(8,128)(2,1)S(1)}, u32[]{:S(2)}, u32[]{:S(2)}) collective-permute-start(bf16[144,1152]{1,0:T(8,128)(2,1)S(1)} %get-tuple-element.154), channel_id=1, source_target_pairs={{0,16},{16,0},{1,17},{17,1},{2,18},{18,2},{3,19},{19,3},{4,20},{20... | collective-permute-start | bytes 995336 | tf_op jit(solution)/shard_map/ppermute | solution.py:1009
  561.1 3.7 collective-permute-start.7
  566.1 1.3 copy-start.6
  566.1 1.9 copy-start.10
  566.1 2.5 copy-start.2
  568.6 1.3 copy-start.9
Sparse Core Ops, SparseCore 0:
  376.7 37.6 reduce-scatter.4
  416.7 33.7 reduce-scatter.6
  452.9 51.4 reduce-scatter.8
  506.5 52.3 reduce-scatter.10

commit v7 on v6

--- a/solution.py
+++ b/solution.py
@@ -418,12 +418,18 @@
 
 def qkv_kernel(layer, square, x, sel, mod, gain, both, turn, ones, w_own, w_other, whole, proj, q,
                k, v, h, w, ssem, rsem, wsem):
-    x, mod, gain = tokens_of(x), mod.at[layer], gain.at[layer]
     place = ring(square)
-    head = w_own.shape[1] * PAD // w.shape[1]
     load = head_weights(w_own, w_other, layer, w, wsem, range(3))
     greet(place)
-
+    head = w_own.shape[1] * PAD // w.shape[1]
+    qkv_part(
+        place, head, tokens_of(x), sel, mod.at[layer], gain.at[layer], both, turn, ones, load,
+        whole, proj, q, k, v, h, w, (ssem, rsem), 0
+    )
+
+
+def qkv_part(place, head, x, sel, mod, gain, both, turn, ones, load, whole, proj, q, k, v, h, w,
+             sems, base):
     def prepare(rows):
         normal, _ = normed(x[rows].astype(F32))
         shift = mod_rows(sel[rows], mod, 0)
@@ -449,7 +455,25 @@
             put(dst, rows, jnp.concatenate(turned, axis=1))
         put(v, rows, nt(held, w[2]))
 
-    gather(place, h, whole, (ssem, rsem), 0, use, lambda: arrive(load))
+    gather(place, h, whole, sems, base, use, lambda: arrive(load))
+
+
+def mlp_qkv_kernel(layer, square, att, x, sel, mod, wo0, wo1, wg0, wg1, wd0, wd1, gain, both, turn,
+                   ones, w_own, w_other, br1, x1, br2, y, whole_q, proj, q, k, v, whole_h, gate_h,
+                   up_h, hidden_h, whole, gate, up, hidden, h, wo, wg, wd, o1, i1, k1, s1, o2, i2,
+                   k2, s2, ssem, rsem, wsem, osem, w, hsem):
+    place = ring(square)
+    load = head_weights(w_own, w_other, layer + 1, w, hsem, range(3))
+    mlp_kernel(
+        layer, square, att, x, sel, mod, wo0, wo1, wg0, wg1, wd0, wd1, br1, x1, br2, y, whole_h,
+        gate_h, up_h, hidden_h, whole, gate, up, hidden, h, wo, wg, wd, o1, i1, k1, s1, o2, i2, k2,
+        s2, ssem, rsem, wsem, osem
+    )
+    head = w_own.shape[1] * PAD // w.shape[1]
+    qkv_part(
+        place, head, y, sel, mod.at[layer + 1], gain.at[layer + 1], both, turn, ones, load, whole_q,
+        proj, q, k, v, h, w, (ssem, rsem), 18
+    )
 
 
 def mlp_kernel(layer, square, att, x, sel, mod, wo0, wo1, wg0, wg1, wd0, wd1, br1, x1, br2, y,
@@ -808,8 +832,10 @@
     for copy in arrivals:
         copy.wait_recv()
     sends += arrivals
+    total[...] = jnp.zeros_like(total)
     for micro in range(2):
-        total[micro] = (got[4 * micro] + got[4 * micro + 1]) + (got[4 * micro + 2] + got[4 * micro + 3])
+        summed = (got[4 * micro] + got[4 * micro + 1]) + (got[4 * micro + 2] + got[4 * micro + 3])
+        total[:, 3 * micro : 3 * micro + 3] = summed[:, 0:3]
     gain = got_gain[0]
     for k in range(1, 8):
         gain = gain + got_gain[k]
@@ -822,12 +848,11 @@
     every[shard] = total[...]
     every_gain[shard] = total_gain[...]
     load.wait()
-    half = total.shape[3]
-    for micro in range(2):
-        lift = two(nn, total[micro, 0], ada[pl.ds(0, half)])
-        for j in range(1, 3):
-            lift = lift + two(nn, total[micro, j], ada[pl.ds(j * half, half)])
-        lifts[here, micro] = lift
+    half = total.shape[2]
+    lift = two(nn, total[0], ada[pl.ds(0, half)])
+    for j in range(1, 3):
+        lift = lift + two(nn, total[j], ada[pl.ds(j * half, half)])
+    lifts[here] = lift
     base = 13 + 2 * (dp - 1)
     lift_copies = []
     for k in range(1, 8):
@@ -849,13 +874,13 @@
         bias = jnp.zeros((1, half), F32)
         grad = jnp.zeros((lifted_part.shape[2], half), F32)
         for k in range(dp):
-            for micro in range(2):
-                block = every[k, micro, j]
-                bias = bias + jnp.sum(block, axis=0, keepdims=True)
-                high = block.astype(BF)
-                low = (block - high.astype(F32)).astype(BF)
-                rows = lifted_part[2 * k + micro].astype(BF)
-                grad = grad + tn(rows, high) + tn(rows, low)
+            block = every[k, j, 0:6]
+            bias = bias + jnp.sum(block, axis=0, keepdims=True)
+            high = block.astype(BF)
+            low = (block - high.astype(F32)).astype(BF)
+            rows = jnp.concatenate([lifted_part[2 * k, 0:3], lifted_part[2 * k + 1, 0:3]], axis=0)
+            rows = rows.astype(BF)
+            grad = grad + tn(rows, high) + tn(rows, low)
         bias_row[:, pl.ds(j * half, half)] = bias
         ada_grad[:, pl.ds(j * half, half)] = grad
     for copy in lift_copies:
@@ -867,8 +892,7 @@
     raw = cond[...].astype(F32)
     s = jax.nn.sigmoid(raw)
     factor = s * (1.0 + raw * (1.0 - s))
-    cond_grad[0:3] = lift[0, 0:3] * factor[0:3]
-    cond_grad[3:6] = lift[1, 0:3] * factor[3:6]
+    cond_grad[...] = lift[0:6] * factor
     part = bias_grad.shape[1]
     row = bias_row[...]
     total_bias = jnp.zeros((1, part), F32)
@@ -1104,19 +1128,19 @@
 
     x = tokens
     kept = []
+    held = ring_call(
+        functools.partial(qkv_kernel, 0, square),
+        0,
+        20,
+        [sds((seq, width), BF), sds((2, seq, wide), BF)] + [sds((seq, wide), BF)] * 3,
+        [pltpu.VMEM((rows, width), BF), pltpu.VMEM((3, wide, width), BF)]
+        + dma_sems(6)
+        + [pltpu.SemaphoreType.DMA((3 * heads,))],
+        (x, sel, mods, gains, both, turn, ones, own[0], other[0]),
+        (1,) * 7 + (0, 0),
+    )
     for layer in range(2):
-        mod = mods
-        whole1, proj, q, k, v = ring_call(
-            functools.partial(qkv_kernel, layer, square),
-            layer,
-            20,
-            [sds((seq, width), BF), sds((2, seq, wide), BF)] + [sds((seq, wide), BF)] * 3,
-            [pltpu.VMEM((rows, width), BF), pltpu.VMEM((3, wide, width), BF)]
-            + dma_sems(6)
-            + [pltpu.SemaphoreType.DMA((3 * heads,))],
-            (x, sel, mod, gains, both, turn, ones, own[0], other[0]),
-            (1,) * 7 + (0, 0),
-        )
+        whole1, proj, q, k, v = held
         (att,) = local_call(
             functools.partial(attention_kernel, head),
             6,
@@ -1125,25 +1149,16 @@
             spans,
             (q, k, v),
         )
-        br1, x1, br2, y, whole2, gate, up, hidden = ring_call(
-            functools.partial(mlp_kernel, layer, square),
-            2 + layer,
-            48,
-            [
-                sds((rows, width), F32),
-                sds((rows, width), F32),
-                sds((rows, width), F32),
-                sds((rows, width), BF),
-                sds((seq, width), BF),
-                sds((seq, hidden_here), F32),
-                sds((seq, hidden_here), F32),
-                sds((seq, hidden_here), BF),
-            ],
-            [
-                pltpu.VMEM((seq, width), BF),
-                pltpu.VMEM((seq, hidden_here), F32),
-                pltpu.VMEM((seq, hidden_here), F32),
-                pltpu.VMEM((seq, hidden_here), BF),
+        small = [sds((rows, width), F32)] * 3 + [sds((rows, width), BF)]
+        large = [
+            sds((seq, width), BF),
+            sds((seq, hidden_here), F32),
+            sds((seq, hidden_here), F32),
+            sds((seq, hidden_here), BF),
+        ]
+        scratch = (
+            [pltpu.VMEM(t.shape, t.dtype) for t in large]
+            + [
                 pltpu.VMEM((rows, width), BF),
                 pltpu.VMEM((wide, width), BF),
                 pltpu.VMEM((2, width, hidden_here), BF),
@@ -1151,12 +1166,39 @@
             ]
             + scatter_scratch(rows, width)
             + scatter_scratch(rows, width)
-            + dma_sems(18)
-            + [pltpu.SemaphoreType.DMA((7,)), pltpu.SemaphoreType.DMA((heads,))],
-            (att, x, sel, mod, own[1], other[1], own[2], other[2], own[3], other[3]),
-            (1, 1, 1, 1) + (0,) * 6,
-            loose=4,
+            + dma_sems(18 if layer else 24)
+            + [pltpu.SemaphoreType.DMA((7,)), pltpu.SemaphoreType.DMA((heads,))]
         )
+        weights = (own[1], other[1], own[2], other[2], own[3], other[3])
+        if layer:
+            outs = ring_call(
+                functools.partial(mlp_kernel, layer, square),
+                3,
+                48,
+                small + large,
+                scratch,
+                (att, x, sel, mods) + weights,
+                (1,) * 4 + (0,) * 6,
+                loose=4,
+            )
+        else:
+            outs = ring_call(
+                functools.partial(mlp_qkv_kernel, layer, square),
+                2,
+                70,
+                small
+                + [sds((seq, width), BF), sds((2, seq, wide), BF)]
+                + [sds((seq, wide), BF)] * 3
+                + large,
+                scratch
+                + [pltpu.VMEM((3, wide, width), BF), pltpu.SemaphoreType.DMA((3 * heads,))],
+                (att, x, sel, mods) + weights + (gains, both, turn, ones, own[0], other[0]),
+                (1,) * 4 + (0,) * 6 + (1,) * 4 + (0, 0),
+                loose=9,
+            )
+            held = outs[4:9]
+        br1, x1, br2, y = outs[:4]
+        whole2, gate, up, hidden = outs[-4:]
         kept.append((x, whole1, proj, q, k, v, att, br1, x1, whole2, gate, up, hidden, br2, y))
         x = y
 
@@ -1263,11 +1305,11 @@
             pltpu.VMEM((1, 3 * half), F32),
             pltpu.VMEM((8, 3, 8, half), F32),
             pltpu.VMEM((8, 8, wide), F32),
-            pltpu.VMEM((2, 3, 8, half), F32),
+            pltpu.VMEM((3, 8, half), F32),
             pltpu.VMEM((8, wide), F32),
-            pltpu.VMEM((dp, 2, 3, 8, half), F32),
+            pltpu.VMEM((dp, 3, 8, half), F32),
             pltpu.VMEM((dp, 8, wide), F32),
-            pltpu.VMEM((8, 2, 8, width), F32),
+            pltpu.VMEM((8, 8, width), F32),
         ]
         + dma_sems(13 + 2 * (dp - 1) + 8)
         + [pltpu.SemaphoreType.DMA],
@@ -1275,11 +1317,13 @@
         (1, 1, 1, 1, 0),
     )
 
-    mlp = own_layer(section, (packs[0][0], packs[1][0]))
-    attn = own_layer(section, (packs[0][1], packs[1][1]))
     f = hidden_here
+    ready = lax.optimization_barrier((packs[0][0], packs[1][0], cond_grad))
+    cond_grad = ready[2]
+    mlp = own_layer(section, ready[:2])
     g_gate_up = jnp.stack([mlp[:, :f], mlp[:, f : 2 * f]])[None]
     g_down = mlp[:, 2 * f :].T[None]
+    attn = own_layer(section, (packs[0][1], packs[1][1]))
     g_qkv = jnp.stack([attn[:, k * packed : (k + 1) * packed] for k in range(3)])[None]
     g_out = attn[:, 3 * packed :].T[None]
 

time: 580 us -> 579 us (level)
  Pallas kernels: 403 us -> 396 us
    pallas_call x10 -> x9, Pallas kernels: 373 us -> 366 us  [ring_call(): pl.pallas_call(kernel, out_shape=outs, in_specs=[vmem() if s else anywher...]
    reduce_scatter x4, waiting for transfers between devices: 132 us -> 138 us  [reduced(): return lax.psum_scatter(total, DP, scatter_dimension=0, tiled=True)[0]]
  transfers between devices with their start and end apart: 12 -> 12, of which waited for: 3 -> 3; matrix products, arithmetic and copies ran while one was open for 2% -> 2% of each run, Pallas kernels for 14% -> 13%
where the time goes in v7:
time: 579 us; the launch traced here: 576 us
  Pallas kernels  396 us (68%)
  waiting for transfers between devices  139 us (24%)
  between operations  14.3 us (2%)
  local copies, waits for them, and re-layouts  11.7 us (2%)
  other arithmetic  10.5 us (2%)
    pallas_call x9, Pallas kernels, ring_call(): pl.pallas_call(kernel, out_shape=outs, in_specs=[vmem() if s else anywher...  366 us
    reduce_scatter x4, waiting for transfers between devices, reduced(): return lax.psum_scatter(total, DP, scatter_dimension=0, tiled=True)[0]  138 us
    pallas_call x4, Pallas kernels, local_call(): pl.pallas_call(kernel, out_shape=outs, in_specs=[pl.BlockSpec(memory_spac...  30 us
  transfers between devices with their start and end apart: 12, of which 3 were waited for; matrix products, arithmetic and copies ran while one was open for 2% of the time, Pallas kernels for 13%

profile of v7, /device:TPU:1, one launch (start us, length us, event | category | flops | bytes accessed | tf_op | source)
XLA Modules:
  0.0 575.9 jit_solution(18374506534055133081)
XLA Ops:
  8.3 16.1 %shard_map.231 = (f32[2,6,8,1152]{3,2,1,0:T(8,128)}, f32[4,16,1152]{2,1,0:T(8,128)}, f32[2,8,128]{2,1,0:T(8,128)}, f32[192,8]{1,0:T(8,128)}, f32[768,256]{1,0:T(8,128)}, /*index=5*/s32[8]{0:T(128)}) custom-call(bf16[6,1152]{1,0:T(8,128)(2,1)} %cond.3, bf16[1728,1152]{1,0:T(8,128)(2,1)} %bitcast.75, bf16[1,1728]{1,0:T(2,128)(2,1)} %bias.1, ...), custom_call_target="tpu_custom_call" | custom-call | bytes 42000000 | tf_op jit(solution)/shard_map/pallas_call | solution.py:912
  24.4 23.8 %shard_map.232 = (bf16[768,1152]{1,0:T(8,128)(2,1)}, bf16[2,768,512]{2,1,0:T(8,128)(2,1)}, bf16[768,512]{1,0:T(8,128)(2,1)}, bf16[768,512]{1,0:T(8,128)(2,1)}, bf16[768,512]{1,0:T(8,128)(2,1)}) custom-call(bf16[2,192,1152]{2,1,0:T(8,128)(2,1)} %x.7, f32[192,8]{1,0:T(8,128)} %get-tuple-element.74.sel, f32[2,6,8,1152]{3,2,1,0:T(8,128)} %get-tuple-element.75.mod, ...), custom_call_target="tpu_custom_call" | custom-call | bytes 70000000 | tf_op jit(solution)/shard_map/pallas_call | solution.py:912
  48.3 5.1 shard_map.233.att.att_h
  53.4 1.7 copy-done
  55.1 70.6 %shard_map.234 = (f32[192,1152]{1,0:T(8,128)}, f32[192,1152]{1,0:T(8,128)}, f32[192,1152]{1,0:T(8,128)}, bf16[192,1152]{1,0:T(8,128)(2,1)}, bf16[768,1152]{1,0:T...) custom-call(bf16[768,512]{1,0:T(8,128)(2,1)} %shard_map.233.att.att_, ...), custom_call_target="tpu_custom_call" | custom-call | bytes 245000000 | tf_op jit(solution)/shard_map/pallas_call | solution.py:912
  125.8 5.1 shard_map.235.att.att_h
  130.9 50.3 %shard_map.236 = (f32[192,1152]{1,0:T(8,128)}, f32[192,1152]{1,0:T(8,128)}, f32[192,1152]{1,0:T(8,128)}, bf16[192,1152]{1,0:T(8,128)(2,1)}, bf16[768,1152]{1,0:T...) custom-call(bf16[768,512]{1,0:T(8,128)(2,1)} %shard_map.235.att.att_h, ...), custom_call_target="tpu_custom_call" | custom-call | bytes 168000000 | tf_op jit(solution)/shard_map/pallas_call | solution.py:912
  181.1 64.0 %shard_map.237 = (bf16[768,1152]{1,0:T(8,128)(2,1)}, bf16[768,512]{1,0:T(8,128)(2,1)}, f32[192,1152]{1,0:T(8,128)}, f32[8,8,576]{2,1,0:T(8,128)}, bf16[4,144,2304]{2,1,0:T(8,128)(2,1)}) custom-call(bf16[2,192,1152]{2,1,0:T(8,128)(2,1)} %dy.1, f32[192,1152]{1,0:T(8,128)} %get-tuple-element.86.br2, f32[192,1152]{1,0:T(8,128)} %get-tuple-element.87.br1, ...), custom_call_target="tpu_custom_call" | custom-call | bytes 182000000 | tf_op jit(solution)/shard_map/pallas_call | solution.py:912
  245.2 9.9 %shard_map.238 = (bf16[768,512]{1,0:T(8,128)(2,1)}, bf16[768,512]{1,0:T(8,128)(2,1)}, bf16[768,512]{1,0:T(8,128)(2,1)}) custom-call(s32[8]{0:T(128)} %get-tuple-element.73.spans, bf16[768,512]{1,0:T(8,128)(2,1)} %get-tuple-element.82.q, bf16[768,512]{1,0:T(8,128)(2,1)} %get-tuple-element.83.k, bf16[768,512]{1,0:T(8,128)(2,1)} %get-tuple-element.84.v, ...), custom_call_target="tpu_custom_call" | custom-call | bytes 35000000 | tf_op jit(solution)/shard_map/pallas_call | solution.py:1021
  255.0 0.7 broadcast_in_dim.23.prev
  255.7 26.3 %shard_map.239 = (f32[192,1152]{1,0:T(8,128)}, bf16[192,1152]{1,0:T(8,128)(2,1)}, f32[2,12,8,576]{3,2,1,0:T(8,128)}, bf16[4,144,1152]{2,1,0:T(8,128)(2,1)}, f32[2,1,512]{2,1,0:T(1,128)}) custom-call(bf16[768,512]{1,0:T(8,128)(2,1)} %get-tuple-element.94.dq, bf16[768,512]{1,0:T(8,128)(2,1)} %get-tuple-element.95.dk, bf16[768,512]{1,0:T(8,128)(2,1)} %get-tuple-element.96.dv, ...), custom_call_target="tpu_custom_call" | custom-call | bytes 77000000 | tf_op jit(solution)/shard_map/pallas_call | solution.py:912
  282.1 57.7 %shard_map.240 = (bf16[768,1152]{1,0:T(8,128)(2,1)}, bf16[768,512]{1,0:T(8,128)(2,1)}, f32[192,1152]{1,0:T(8,128)}, f32[8,8,576]{2,1,0:T(8,128)}, bf16[4,144,2304]{2,1,0:T(8,128)(2,1)}) custom-call(bf16[192,1152]{1,0:T(8,128)(2,1)} %get-tuple-element.102.dy, f32[192,1152]{1,0:T(8,128)} %get-tuple-element.103.br2, f32[192,1152]{1,0:T(8,128)} %get-tuple-element.104.br1, ...), custom_call_target="tpu_custom_call" | custom-call | bytes 182000000 | tf_op jit(solution)/shard_map/pallas_call | solution.py:912
  339.8 9.9 %shard_map.241 = (bf16[768,512]{1,0:T(8,128)(2,1)}, bf16[768,512]{1,0:T(8,128)(2,1)}, bf16[768,512]{1,0:T(8,128)(2,1)}) custom-call(s32[8]{0:T(128)} %get-tuple-element.73.spans, bf16[768,512]{1,0:T(8,128)(2,1)} %get-tuple-element.78.q, bf16[768,512]{1,0:T(8,128)(2,1)} %get-tuple-element.79.k, bf16[768,512]{1,0:T(8,128)(2,1)} %get-tuple-element.80.v, ...), custom_call_target="tpu_custom_call" | custom-call | bytes 35000000 | tf_op jit(solution)/shard_map/pallas_call | solution.py:1021
  349.7 0.7 slice_bitcast_fusion.7.prev
  350.4 27.5 %shard_map.242 = (f32[192,1152]{1,0:T(8,128)}, bf16[192,1152]{1,0:T(8,128)(2,1)}, f32[2,12,8,576]{3,2,1,0:T(8,128)}, bf16[4,144,1152]{2,1,0:T(8,128)(2,1)}, f32[2,1,512]{2,1,0:T(1,128)}) custom-call(bf16[768,512]{1,0:T(8,128)(2,1)} %get-tuple-element.111.dq, bf16[768,512]{1,0:T(8,128)(2,1)} %get-tuple-element.112.dk, ...), custom_call_target="tpu_custom_call" | custom-call | bytes 77000000 | tf_op jit(solution)/shard_map/pallas_call | solution.py:912
  381.3 1.9 select_bitcast_fusion
  383.4 1.6 constant_dynamic-slice_fusion
  385.7 29.5 %shard_map.243 = (f32[288,1728]{1,0:T(8,128)}, f32[1,432]{1,0:T(1,128)}, f32[6,1152]{1,0:T(8,128)}, f32[2,72]{1,0:T(2,128)}) custom-call(f32[2,12,8,576]{3,2,1,0:T(8,128)} %get-tuple-element.123.dmod, f32[2,8,512]{2,1,0:T(8,128)} %pad.4.dgain, f32[8,8,288]{2,1,0:T(8,128)} %bitcast.87, bf16[6,1152]{1,0:T(8,128)(2,1)} %cond.3, bf16[1728,1152]{1,0:T(8,128)(2,1)} %bitcast.76), custom_call_target="tpu_custom_call" | custom-call | bytes 52500000 | tf_op jit(solution)/shard_map/pallas_call | solution.py:912
  415.2 1.1 maximum_select_fusion.2
  416.3 1.3 maximum_select_fusion
  417.6 31.5 %reduce-scatter.11.cloned.1.call-done = bf16[1,144,1152]{2,1,0:T(8,128)(2,1)} async-done(((bf16[4,144,1152]{2,1,0:T(8,128)(2,1)}), bf16[1,144,1152]{2,1,0:T(8,128)(2,1)}) %reduce-scatter.11.cloned.1.call-update) | async-done | bytes 331792 | tf_op jit(solution)/shard_map/reduce_scatter | solution.py:1068
  449.1 1.1 select_bitcast_fusion.2
  450.2 1.1 collective-permute-start.6
  451.3 51.5 %reduce-scatter.5.cloned.1.call-done = bf16[1,144,2304]{2,1,0:T(8,128)(2,1)} async-done(((bf16[4,144,2304]{2,1,0:T(8,128)(2,1)}), bf16[1,144,2304]{2,1,0:T(8,128)(2,1)}) %reduce-scatter.5.cloned.1.call-update) | async-done | bytes 663568 | tf_op jit(solution)/shard_map/reduce_scatter | solution.py:1068
  502.9 54.5 %reduce-scatter.7.cloned.1.call-done = bf16[1,144,2304]{2,1,0:T(8,128)(2,1)} async-done(((bf16[4,144,2304]{2,1,0:T(8,128)(2,1)}), bf16[1,144,2304]{2,1,0:T(8,128)(2,1)}) %reduce-scatter.7.cloned.1.call-update) | async-done | bytes 663568 | tf_op jit(solution)/shard_map/reduce_scatter | solution.py:1068
  557.4 2.2 broadcast_select_fusion.1
  559.6 1.1 collective-permute-start.7
  561.2 1.0 copy.26
  562.2 1.1 maximum_bitcast_fusion.1
  563.6 1.1 slice_bitcast_fusion
  564.7 1.3 maximum_bitcast_fusion
  567.2 1.3 copy.39
  (55 shorter events, 7.8 us)
Async XLA Ops:
  7.2 410.4 %reduce-scatter.9.cloned.1.call-start = ((), (), s32[]{:S(2)}) async-start(), calls=%async_computation.6 | async-start | bytes 1658880 | tf_op jit(solution)/shard_map/reduce_scatter | solution.py:1068
  7.2 46.1 %collective-permute-start.2 = (bf16[2,1152,768]{2,1,0:T(8,128)(2,1)}, bf16[2,1152,768]{2,1,0:T(8,128)(2,1)S(1)}, u32[]{:S(2)}, u32[]{:S(2)}) collective-permute-start(bf16[2,1152,768]{2,1,0:T(8,128)(2,1)} %bitcast.60), channel_id=1, source_target_pairs={{0,16},{16,0},{1,17},{17,1},{2,18},{18,2},{3,19},{19,3},{4,20},{20... | collective-permute-start | bytes 10616840 | tf_op jit(solution)/shard_map/ppermute | solution.py:1033
  7.3 17.1 %collective-permute-start = (bf16[3,288,1152]{2,1,0:T(8,128)(2,1)}, bf16[3,288,1152]{2,1,0:T(8,128)(2,1)}, u32[]{:S(2)}, u32[]{:S(2)}) collective-permute-start(bf16[3,288,1152]{2,1,0:T(8,128)(2,1)} %bitcast.65), channel_id=1, source_target_pairs={{0,16},{16,0},{1,17},{17,1},{2,18},{18,2},{3,19},{19,3},{4,20},{20... | collective-permute-start | bytes 5971976 | tf_op jit(solution)/shard_map/ppermute | solution.py:1033
  7.8 45.6 %collective-permute-start.3 = (bf16[768,1152]{1,0:T(8,128)(2,1)}, bf16[768,1152]{1,0:T(8,128)(2,1)}, u32[]{:S(2)}, u32[]{:S(2)}) collective-permute-start(bf16[768,1152]{1,0:T(8,128)(2,1)} %bitcast.70), channel_id=1, source_target_pairs={{0,16},{16,0},{1,17},{17,1},{2,18},{18,2},{3,19},{19,3},{4,20},{20... | collective-permute-start | bytes 5308424 | tf_op jit(solution)/shard_map/ppermute | solution.py:1033
  7.9 45.5 %collective-permute-start.1 = (bf16[288,1152]{1,0:T(8,128)(2,1)}, bf16[288,1152]{1,0:T(8,128)(2,1)}, u32[]{:S(2)}, u32[]{:S(2)}) collective-permute-start(bf16[288,1152]{1,0:T(8,128)(2,1)} %bitcast.77), channel_id=1, source_target_pairs={{0,16},{16,0},{1,17},{17,1},{2,18},{18,2},{3,19},{19,3},{4,20},{20... | collective-permute-start | bytes 1990664 | tf_op jit(solution)/shard_map/ppermute | solution.py:1033
  53.4 1.7 copy-start
  339.8 9.9 %copy-start.5 = (f32[2,12,8,576]{3,2,1,0:T(8,128)S(1)}, f32[2,12,8,576]{3,2,1,0:T(8,128)}, u32[]{:S(2)}) copy-start(f32[2,12,8,576]{3,2,1,0:T(8,128)} %get-tuple-element.117) | copy-start | bytes 1327108
  377.9 71.1 %reduce-scatter.11.cloned.1.call-start = ((), (), s32[]{:S(2)}) async-start(), calls=%async_computation.7 | async-start | bytes 1658880 | tf_op jit(solution)/shard_map/reduce_scatter | solution.py:1068
  378.7 124.2 %reduce-scatter.5.cloned.1.call-start = ((), (), s32[]{:S(2)}) async-start(), calls=%async_computation.4 | async-start | bytes 3317760 | tf_op jit(solution)/shard_map/reduce_scatter | solution.py:1068
  379.4 1.0 copy-start.3
  379.4 1.3 copy-start.4
  379.4 178.0 %reduce-scatter.7.cloned.1.call-start = ((), (), s32[]{:S(2)}) async-start(), calls=%async_computation.5 | async-start | bytes 3317760 | tf_op jit(solution)/shard_map/reduce_scatter | solution.py:1068
  380.0 1.3 copy-start.1
  380.8 4.2 copy-start.8
  380.8 4.2 copy-start.7
  380.9 35.4 %collective-permute-start.5 = (f32[192,1152]{1,0:T(8,128)S(1)}, f32[192,1152]{1,0:T(8,128)S(1)}, u32[]{:S(2)}, u32[]{:S(2)}) collective-permute-start(f32[192,1152]{1,0:T(8,128)S(1)} %get-tuple-element.156), channel_id=1, source_target_pairs={{0,16},{16,0},{1,17},{17,1},{2,18},{18,2},{3,19},{19,3},{4,20},{20... | collective-permute-start | bytes 2654216 | tf_op jit(solution)/shard_map/ppermute | solution.py:1033
  383.2 32.0 %collective-permute-start.4 = (bf16[192,1152]{1,0:T(8,128)(2,1)}, bf16[192,1152]{1,0:T(8,128)(2,1)S(1)}, u32[]{:S(2)}, u32[]{:S(2)}) collective-permute-start(bf16[192,1152]{1,0:T(8,128)(2,1)} %get-tuple-element.158), channel_id=1, source_target_pairs={{0,16},{16,0},{1,17},{17,1},{2,18},{18,2},{3,19},{19,3},{4,20},{20... | collective-permute-start | bytes 1327112 | tf_op jit(solution)/shard_map/ppermute | solution.py:1033
  450.2 110.5 %collective-permute-start.6 = (bf16[144,1152]{1,0:T(8,128)(2,1)S(1)}, bf16[144,1152]{1,0:T(8,128)(2,1)S(1)}, u32[]{:S(2)}, u32[]{:S(2)}) collective-permute-start(bf16[144,1152]{1,0:T(8,128)(2,1)S(1)} %get-tuple-element.160), channel_id=1, source_target_pairs={{0,16},{16,0},{1,17},{17,1},{2,18},{18,2},{3,19},{19,3},{4,20},{20... | collective-permute-start | bytes 995336 | tf_op jit(solution)/shard_map/ppermute | solution.py:1033
  559.6 3.7 collective-permute-start.7
  564.7 1.3 copy-start.6
  564.7 1.9 copy-start.10
  564.7 2.5 copy-start.2
  567.2 1.3 copy-start.9
Sparse Core Ops, SparseCore 0:
  378.0 37.4 reduce-scatter.8
  417.8 31.2 reduce-scatter.10
  451.4 51.4 reduce-scatter.4
  505.0 52.3 reduce-scatter.6

commit v8 on v7

--- a/solution.py
+++ b/solution.py
@@ -376,11 +376,22 @@
     lax.fori_loop(0, width // 256, body, 0)
 
 
+def half_copy(packs, sems, index, col, width):
+    at = pl.ds(col, width)
+    return pltpu.make_async_remote_copy(
+        src_ref=packs[1].at[:, :, at],
+        dst_ref=packs[2].at[:, :, at],
+        send_sem=sems[0].at[index],
+        recv_sem=sems[1].at[index],
+        device_id={S: 1 - lax.axis_index(S)},
+        device_id_type=pl.DeviceIdType.MESH,
+    )
+
+
 def send_half(packs, sems, index, col, width):
-    at = pl.ds(col, width)
-    return push(
-        packs[1].at[:, :, at], packs[2].at[:, :, at], sems, index, {S: 1 - lax.axis_index(S)}
-    )
+    copy = half_copy(packs, sems, index, col, width)
+    copy.start()
+    return copy
 
 
 def add_halves(packs, copies, total, col, width):
@@ -626,12 +637,13 @@
 
     def late():
         weight_grad(None, dup, flipped, f, packs)
-
+        last.start()
+        add_halves(packs, copies[:1], total, 2 * f, f)
+        add_halves(packs, copies[1:2], total, 0, f)
+
+    last = half_copy(packs, sems, 20, f, f)
     gather(place, h1, whole1, sems, 12, use_out, sums, late)
-    copies.append(send_half(packs, sems, 20, f, f))
-    add_halves(packs, copies[:1], total, 2 * f, f)
-    add_halves(packs, copies[1:2], total, 0, f)
-    add_halves(packs, copies[2:], total, f, f)
+    add_halves(packs, [last], total, f, f)
 
 
 def qkv_back_kernel(layer, square, dq, dk, dv, proj, gain, both, turn, ones, spread, x, dx1, sel,
@@ -670,10 +682,10 @@
                 lanes = slice(pair * 2 * PAD, (pair + 1) * 2 * PAD)
                 turned = src[rows, lanes]
                 back = turned.astype(F32) * cosine - nn(turned, turn[...]) * sine
-                normal, inverse = unit(proj[which, rows, lanes].astype(F32), ones[...], head)
+                normal, inverse = unit(proj[which, rows, lanes].astype(F32), ones[...], head, nn_low)
                 dgain[which, :, lanes] += jnp.sum(back * normal, axis=0, keepdims=True)
                 gained = back * twice(gain[which : which + 1])
-                mean = two(nn, gained * normal, ones[...]) * (1.0 / head)
+                mean = nn_low(gained * normal, ones[...]) * (1.0 / head)
                 parts.append((inverse * (gained - normal * mean)).astype(BF))
             full = jnp.concatenate(parts, axis=1)
             dpack[rows, which * packed : (which + 1) * packed] = nt(full, spread[...]).astype(BF)
@@ -767,11 +779,11 @@
         )
     load.wait()
     half = parts.shape[3]
-    for micro in range(2):
-        for j in range(3):
-            rows = lifted[pl.ds(micro * 8, 8)].astype(BF)
-            here_bias = biases[:, j * half : (j + 1) * half]
-            parts[micro, j] = nt(rows, ada[pl.ds(j * half, half)]) + here_bias
+    for j in range(3):
+        here_bias = biases[:, j * half : (j + 1) * half]
+        made = nt(lifted[...].astype(BF), ada[pl.ds(j * half, half)]) + here_bias
+        parts[0, j] = made[0:8]
+        parts[1, j] = made[8:16]
     for k in range(1, 8):
         peer = (here + k) % 8
         copies.append(push(parts.at[peer // 4], got.at[here], sems, k - 1, cell_id(peer)))
@@ -956,8 +968,16 @@
     each_head(rest)
 
 
-def unit(proj, ones, head):
-    inverse = lax.rsqrt(two(nn, proj * proj, ones) * (1.0 / head) + EPS)
+def nn_low(a, b):
+    return nn(a.astype(BF), b)
+
+
+def nn_two(a, b):
+    return two(nn, a, b)
+
+
+def unit(proj, ones, head, sums=nn_two):
+    inverse = lax.rsqrt(sums(proj * proj, ones) * (1.0 / head) + EPS)
     return proj * inverse, inverse
 
 

time: 579 us -> 576 us (level)
  no operation moved by 1% of the time
where the time goes in v8:
time: 576 us; the launch traced here: 573 us
  Pallas kernels  394 us (68%)
  waiting for transfers between devices  139 us (24%)
  between operations  14.3 us (2%)
  local copies, waits for them, and re-layouts  11.7 us (2%)
  other arithmetic  10.5 us (2%)
    pallas_call x9, Pallas kernels, ring_call(): pl.pallas_call(kernel, out_shape=outs, in_specs=[vmem() if s else anywher...  364 us
    reduce_scatter x4, waiting for transfers between devices, reduced(): return lax.psum_scatter(total, DP, scatter_dimension=0, tiled=True)[0]  137 us
    pallas_call x4, Pallas kernels, local_call(): pl.pallas_call(kernel, out_shape=outs, in_specs=[pl.BlockSpec(memory_spac...  30 us
  transfers between devices with their start and end apart: 12, of which 3 were waited for; matrix products, arithmetic and copies ran while one was open for 2% of the time, Pallas kernels for 13%

profile of v8, /device:TPU:1, one launch (start us, length us, event | category | flops | bytes accessed | tf_op | source)
XLA Modules:
  0.0 573.3 jit_solution(16667208471367234013)
XLA Ops:
  8.3 15.1 %shard_map.231 = (f32[2,6,8,1152]{3,2,1,0:T(8,128)}, f32[4,16,1152]{2,1,0:T(8,128)}, f32[2,8,128]{2,1,0:T(8,128)}, f32[192,8]{1,0:T(8,128)}, f32[768,256]{1,0:T(8,128)}, /*index=5*/s32[8]{0:T(128)}) custom-call(bf16[6,1152]{1,0:T(8,128)(2,1)} %cond.3, bf16[1728,1152]{1,0:T(8,128)(2,1)} %bitcast.75, bf16[1,1728]{1,0:T(2,128)(2,1)} %bias.1, ...), custom_call_target="tpu_custom_call" | custom-call | bytes 42000000 | tf_op jit(solution)/shard_map/pallas_call | solution.py:924
  23.4 23.8 %shard_map.232 = (bf16[768,1152]{1,0:T(8,128)(2,1)}, bf16[2,768,512]{2,1,0:T(8,128)(2,1)}, bf16[768,512]{1,0:T(8,128)(2,1)}, bf16[768,512]{1,0:T(8,128)(2,1)}, bf16[768,512]{1,0:T(8,128)(2,1)}) custom-call(bf16[2,192,1152]{2,1,0:T(8,128)(2,1)} %x.7, f32[192,8]{1,0:T(8,128)} %get-tuple-element.74.sel, f32[2,6,8,1152]{3,2,1,0:T(8,128)} %get-tuple-element.75.mod, ...), custom_call_target="tpu_custom_call" | custom-call | bytes 70000000 | tf_op jit(solution)/shard_map/pallas_call | solution.py:924
  47.3 5.1 shard_map.233.att.att_h
  52.4 1.7 copy-done
  54.1 70.6 %shard_map.234 = (f32[192,1152]{1,0:T(8,128)}, f32[192,1152]{1,0:T(8,128)}, f32[192,1152]{1,0:T(8,128)}, bf16[192,1152]{1,0:T(8,128)(2,1)}, bf16[768,1152]{1,0:T...) custom-call(bf16[768,512]{1,0:T(8,128)(2,1)} %shard_map.233.att.att_, ...), custom_call_target="tpu_custom_call" | custom-call | bytes 245000000 | tf_op jit(solution)/shard_map/pallas_call | solution.py:924
  124.8 5.1 shard_map.235.att.att_h
  129.9 50.3 %shard_map.236 = (f32[192,1152]{1,0:T(8,128)}, f32[192,1152]{1,0:T(8,128)}, f32[192,1152]{1,0:T(8,128)}, bf16[192,1152]{1,0:T(8,128)(2,1)}, bf16[768,1152]{1,0:T...) custom-call(bf16[768,512]{1,0:T(8,128)(2,1)} %shard_map.235.att.att_h, ...), custom_call_target="tpu_custom_call" | custom-call | bytes 168000000 | tf_op jit(solution)/shard_map/pallas_call | solution.py:924
  180.2 63.5 %shard_map.237 = (bf16[768,1152]{1,0:T(8,128)(2,1)}, bf16[768,512]{1,0:T(8,128)(2,1)}, f32[192,1152]{1,0:T(8,128)}, f32[8,8,576]{2,1,0:T(8,128)}, bf16[4,144,2304]{2,1,0:T(8,128)(2,1)}) custom-call(bf16[2,192,1152]{2,1,0:T(8,128)(2,1)} %dy.1, f32[192,1152]{1,0:T(8,128)} %get-tuple-element.86.br2, f32[192,1152]{1,0:T(8,128)} %get-tuple-element.87.br1, ...), custom_call_target="tpu_custom_call" | custom-call | bytes 182000000 | tf_op jit(solution)/shard_map/pallas_call | solution.py:924
  243.6 9.9 %shard_map.238 = (bf16[768,512]{1,0:T(8,128)(2,1)}, bf16[768,512]{1,0:T(8,128)(2,1)}, bf16[768,512]{1,0:T(8,128)(2,1)}) custom-call(s32[8]{0:T(128)} %get-tuple-element.73.spans, bf16[768,512]{1,0:T(8,128)(2,1)} %get-tuple-element.82.q, bf16[768,512]{1,0:T(8,128)(2,1)} %get-tuple-element.83.k, bf16[768,512]{1,0:T(8,128)(2,1)} %get-tuple-element.84.v, ...), custom_call_target="tpu_custom_call" | custom-call | bytes 35000000 | tf_op jit(solution)/shard_map/pallas_call | solution.py:1041
  253.5 0.7 broadcast_in_dim.23.prev
  254.2 25.7 %shard_map.239 = (f32[192,1152]{1,0:T(8,128)}, bf16[192,1152]{1,0:T(8,128)(2,1)}, f32[2,12,8,576]{3,2,1,0:T(8,128)}, bf16[4,144,1152]{2,1,0:T(8,128)(2,1)}, f32[2,1,512]{2,1,0:T(1,128)}) custom-call(bf16[768,512]{1,0:T(8,128)(2,1)} %get-tuple-element.94.dq, bf16[768,512]{1,0:T(8,128)(2,1)} %get-tuple-element.95.dk, bf16[768,512]{1,0:T(8,128)(2,1)} %get-tuple-element.96.dv, ...), custom_call_target="tpu_custom_call" | custom-call | bytes 77000000 | tf_op jit(solution)/shard_map/pallas_call | solution.py:924
  279.9 57.1 %shard_map.240 = (bf16[768,1152]{1,0:T(8,128)(2,1)}, bf16[768,512]{1,0:T(8,128)(2,1)}, f32[192,1152]{1,0:T(8,128)}, f32[8,8,576]{2,1,0:T(8,128)}, bf16[4,144,2304]{2,1,0:T(8,128)(2,1)}) custom-call(bf16[192,1152]{1,0:T(8,128)(2,1)} %get-tuple-element.102.dy, f32[192,1152]{1,0:T(8,128)} %get-tuple-element.103.br2, f32[192,1152]{1,0:T(8,128)} %get-tuple-element.104.br1, ...), custom_call_target="tpu_custom_call" | custom-call | bytes 182000000 | tf_op jit(solution)/shard_map/pallas_call | solution.py:924
  337.0 9.9 %shard_map.241 = (bf16[768,512]{1,0:T(8,128)(2,1)}, bf16[768,512]{1,0:T(8,128)(2,1)}, bf16[768,512]{1,0:T(8,128)(2,1)}) custom-call(s32[8]{0:T(128)} %get-tuple-element.73.spans, bf16[768,512]{1,0:T(8,128)(2,1)} %get-tuple-element.78.q, bf16[768,512]{1,0:T(8,128)(2,1)} %get-tuple-element.79.k, bf16[768,512]{1,0:T(8,128)(2,1)} %get-tuple-element.80.v, ...), custom_call_target="tpu_custom_call" | custom-call | bytes 35000000 | tf_op jit(solution)/shard_map/pallas_call | solution.py:1041
  346.9 0.7 slice_bitcast_fusion.7.prev
  347.7 26.8 %shard_map.242 = (f32[192,1152]{1,0:T(8,128)}, bf16[192,1152]{1,0:T(8,128)(2,1)}, f32[2,12,8,576]{3,2,1,0:T(8,128)}, bf16[4,144,1152]{2,1,0:T(8,128)(2,1)}, f32[2,1,512]{2,1,0:T(1,128)}) custom-call(bf16[768,512]{1,0:T(8,128)(2,1)} %get-tuple-element.111.dq, bf16[768,512]{1,0:T(8,128)(2,1)} %get-tuple-element.112.dk, ...), custom_call_target="tpu_custom_call" | custom-call | bytes 77000000 | tf_op jit(solution)/shard_map/pallas_call | solution.py:924
  377.8 1.9 select_bitcast_fusion
  379.9 1.6 constant_dynamic-slice_fusion
  382.2 31.2 %shard_map.243 = (f32[288,1728]{1,0:T(8,128)}, f32[1,432]{1,0:T(1,128)}, f32[6,1152]{1,0:T(8,128)}, f32[2,72]{1,0:T(2,128)}) custom-call(f32[2,12,8,576]{3,2,1,0:T(8,128)} %get-tuple-element.123.dmod, f32[2,8,512]{2,1,0:T(8,128)} %pad.4.dgain, f32[8,8,288]{2,1,0:T(8,128)} %bitcast.87, bf16[6,1152]{1,0:T(8,128)(2,1)} %cond.3, bf16[1728,1152]{1,0:T(8,128)(2,1)} %bitcast.76), custom_call_target="tpu_custom_call" | custom-call | bytes 52500000 | tf_op jit(solution)/shard_map/pallas_call | solution.py:924
  413.4 1.1 maximum_select_fusion.2
  414.5 1.3 maximum_select_fusion
  415.8 30.8 %reduce-scatter.11.cloned.1.call-done = bf16[1,144,1152]{2,1,0:T(8,128)(2,1)} async-done(((bf16[4,144,1152]{2,1,0:T(8,128)(2,1)}), bf16[1,144,1152]{2,1,0:T(8,128)(2,1)}) %reduce-scatter.11.cloned.1.call-update) | async-done | bytes 331792 | tf_op jit(solution)/shard_map/reduce_scatter | solution.py:1088
  446.6 1.1 select_bitcast_fusion.2
  447.7 1.1 collective-permute-start.6
  448.8 51.5 %reduce-scatter.5.cloned.1.call-done = bf16[1,144,2304]{2,1,0:T(8,128)(2,1)} async-done(((bf16[4,144,2304]{2,1,0:T(8,128)(2,1)}), bf16[1,144,2304]{2,1,0:T(8,128)(2,1)}) %reduce-scatter.5.cloned.1.call-update) | async-done | bytes 663568 | tf_op jit(solution)/shard_map/reduce_scatter | solution.py:1088
  500.4 54.5 %reduce-scatter.7.cloned.1.call-done = bf16[1,144,2304]{2,1,0:T(8,128)(2,1)} async-done(((bf16[4,144,2304]{2,1,0:T(8,128)(2,1)}), bf16[1,144,2304]{2,1,0:T(8,128)(2,1)}) %reduce-scatter.7.cloned.1.call-update) | async-done | bytes 663568 | tf_op jit(solution)/shard_map/reduce_scatter | solution.py:1088
  554.9 2.2 broadcast_select_fusion.1
  557.1 1.1 collective-permute-start.7
  558.7 1.0 copy.26
  559.7 1.1 maximum_bitcast_fusion.1
  561.1 1.1 slice_bitcast_fusion
  562.2 1.3 maximum_bitcast_fusion
  564.7 1.3 copy.39
  (55 shorter events, 7.8 us)
Async XLA Ops:
  7.2 408.6 %reduce-scatter.9.cloned.1.call-start = ((), (), s32[]{:S(2)}) async-start(), calls=%async_computation.6 | async-start | bytes 1658880 | tf_op jit(solution)/shard_map/reduce_scatter | solution.py:1088
  7.2 45.2 %collective-permute-start.2 = (bf16[2,1152,768]{2,1,0:T(8,128)(2,1)}, bf16[2,1152,768]{2,1,0:T(8,128)(2,1)S(1)}, u32[]{:S(2)}, u32[]{:S(2)}) collective-permute-start(bf16[2,1152,768]{2,1,0:T(8,128)(2,1)} %bitcast.60), channel_id=1, source_target_pairs={{0,16},{16,0},{1,17},{17,1},{2,18},{18,2},{3,19},{19,3},{4,20},{20... | collective-permute-start | bytes 10616840 | tf_op jit(solution)/shard_map/ppermute | solution.py:1053
  7.3 16.1 %collective-permute-start = (bf16[3,288,1152]{2,1,0:T(8,128)(2,1)}, bf16[3,288,1152]{2,1,0:T(8,128)(2,1)}, u32[]{:S(2)}, u32[]{:S(2)}) collective-permute-start(bf16[3,288,1152]{2,1,0:T(8,128)(2,1)} %bitcast.65), channel_id=1, source_target_pairs={{0,16},{16,0},{1,17},{17,1},{2,18},{18,2},{3,19},{19,3},{4,20},{20... | collective-permute-start | bytes 5971976 | tf_op jit(solution)/shard_map/ppermute | solution.py:1053
  7.8 44.6 %collective-permute-start.3 = (bf16[768,1152]{1,0:T(8,128)(2,1)}, bf16[768,1152]{1,0:T(8,128)(2,1)}, u32[]{:S(2)}, u32[]{:S(2)}) collective-permute-start(bf16[768,1152]{1,0:T(8,128)(2,1)} %bitcast.70), channel_id=1, source_target_pairs={{0,16},{16,0},{1,17},{17,1},{2,18},{18,2},{3,19},{19,3},{4,20},{20... | collective-permute-start | bytes 5308424 | tf_op jit(solution)/shard_map/ppermute | solution.py:1053
  7.9 44.5 %collective-permute-start.1 = (bf16[288,1152]{1,0:T(8,128)(2,1)}, bf16[288,1152]{1,0:T(8,128)(2,1)}, u32[]{:S(2)}, u32[]{:S(2)}) collective-permute-start(bf16[288,1152]{1,0:T(8,128)(2,1)} %bitcast.77), channel_id=1, source_target_pairs={{0,16},{16,0},{1,17},{17,1},{2,18},{18,2},{3,19},{19,3},{4,20},{20... | collective-permute-start | bytes 1990664 | tf_op jit(solution)/shard_map/ppermute | solution.py:1053
  52.4 1.7 copy-start
  337.0 9.9 %copy-start.5 = (f32[2,12,8,576]{3,2,1,0:T(8,128)S(1)}, f32[2,12,8,576]{3,2,1,0:T(8,128)}, u32[]{:S(2)}) copy-start(f32[2,12,8,576]{3,2,1,0:T(8,128)} %get-tuple-element.117) | copy-start | bytes 1327108
  374.4 72.1 %reduce-scatter.11.cloned.1.call-start = ((), (), s32[]{:S(2)}) async-start(), calls=%async_computation.7 | async-start | bytes 1658880 | tf_op jit(solution)/shard_map/reduce_scatter | solution.py:1088
  375.2 125.2 %reduce-scatter.5.cloned.1.call-start = ((), (), s32[]{:S(2)}) async-start(), calls=%async_computation.4 | async-start | bytes 3317760 | tf_op jit(solution)/shard_map/reduce_scatter | solution.py:1088
  375.9 1.0 copy-start.3
  375.9 1.3 copy-start.4
  375.9 179.0 %reduce-scatter.7.cloned.1.call-start = ((), (), s32[]{:S(2)}) async-start(), calls=%async_computation.5 | async-start | bytes 3317760 | tf_op jit(solution)/shard_map/reduce_scatter | solution.py:1088
  376.5 1.3 copy-start.1
  377.4 4.2 copy-start.8
  377.4 4.2 copy-start.7
  377.4 37.1 %collective-permute-start.5 = (f32[192,1152]{1,0:T(8,128)S(1)}, f32[192,1152]{1,0:T(8,128)S(1)}, u32[]{:S(2)}, u32[]{:S(2)}) collective-permute-start(f32[192,1152]{1,0:T(8,128)S(1)} %get-tuple-element.156), channel_id=1, source_target_pairs={{0,16},{16,0},{1,17},{17,1},{2,18},{18,2},{3,19},{19,3},{4,20},{20... | collective-permute-start | bytes 2654216 | tf_op jit(solution)/shard_map/ppermute | solution.py:1053
  379.7 33.7 %collective-permute-start.4 = (bf16[192,1152]{1,0:T(8,128)(2,1)}, bf16[192,1152]{1,0:T(8,128)(2,1)S(1)}, u32[]{:S(2)}, u32[]{:S(2)}) collective-permute-start(bf16[192,1152]{1,0:T(8,128)(2,1)} %get-tuple-element.158), channel_id=1, source_target_pairs={{0,16},{16,0},{1,17},{17,1},{2,18},{18,2},{3,19},{19,3},{4,20},{20... | collective-permute-start | bytes 1327112 | tf_op jit(solution)/shard_map/ppermute | solution.py:1053
  447.7 110.5 %collective-permute-start.6 = (bf16[144,1152]{1,0:T(8,128)(2,1)S(1)}, bf16[144,1152]{1,0:T(8,128)(2,1)S(1)}, u32[]{:S(2)}, u32[]{:S(2)}) collective-permute-start(bf16[144,1152]{1,0:T(8,128)(2,1)S(1)} %get-tuple-element.160), channel_id=1, source_target_pairs={{0,16},{16,0},{1,17},{17,1},{2,18},{18,2},{3,19},{19,3},{4,20},{20... | collective-permute-start | bytes 995336 | tf_op jit(solution)/shard_map/ppermute | solution.py:1053
  557.1 3.7 collective-permute-start.7
  562.1 1.3 copy-start.6
  562.1 1.9 copy-start.10
  562.1 2.5 copy-start.2
  564.7 1.3 copy-start.9
Sparse Core Ops, SparseCore 0:
  374.6 38.3 reduce-scatter.8
  415.3 31.2 reduce-scatter.10
  448.9 51.4 reduce-scatter.4
  502.5 52.3 reduce-scatter.6
